TPU v7x, 32 devices: a whole 2x2x4 slice. The times are simulated.
32 devices in a mesh: rows: 8 (over z, y), fib: 4 (over x, core).
Axes of the slice: x: 2, y: 2, z: 4, core: 2. Of those that a mesh axis runs over, the one named last changes fastest.
Arguments:
- frames: bfloat16 [20, 1024, 1024], P('fib', 'rows'), may hold values from 0 to 2
- amplitude: float32 [20, 128], P('fib'), may hold values from 0.5 to 2
- line_start: int32 [20, 24], P('fib'), may hold values from 0 to 1016
- bundle_width: float32 [20], replicated, may hold values from 0.8 to 1.6
- fiber_bundle: int32 [128], replicated, may hold values from 0 to 19
- trace_coef: float32 [128, 11], P(('rows', 'fib')), may hold values from -1 to 1
- width_coef: float32 [128, 11], P(('rows', 'fib')), may hold values from -0.15 to 0.15
Outputs:
- trace_fit: float32 [128, 11], P(('rows', 'fib'))
- width_fit: float32 [128, 11], P(('rows', 'fib'))
- residual: bfloat16 [20, 1024, 1024], P('fib', 'rows')
All inputs are finite; a program needn't handle non-finite values.
Results may differ from a plain program's by a relative error of at most 0.001.
Values sent between devices are 32-bit elements; how exact they have to be, the bound alone decides.
No kernel may reach another device: no remote copies, remote signals or barrier semaphores. Data moves between devices by JAX's collectives and lax.ppermute only.
A program may use at most 128 MiB of HBM per device.

v0:
```python
import jax
import jax.numpy as jnp
from jax import lax
from jax.sharding import PartitionSpec as P

K = 11
PIX = 8
WIN = 8
ITERS = 3


HIGH = lax.Precision.HIGHEST


def legendre_upto(first, count, total, degree_count):
    rowpos = (first + jnp.arange(count, dtype=jnp.int32)).astype(jnp.float32)
    tvals = (2.0 * rowpos + 1.0) / total - 1.0
    polys = [jnp.ones_like(tvals), tvals]
    for order in range(1, degree_count - 1):
        polys.append(
            ((2 * order + 1) * tvals * polys[order] - order * polys[order - 1]) / (order + 1)
        )
    return jnp.stack(polys[:degree_count], axis=1)


def legendre_table(first, count, total):
    return legendre_upto(first, count, total, K)


def adams_factor(order):
    value = 1.0
    for index in range(1, order + 1):
        value = value * (2.0 * index - 1.0) / index
    return value


def product_table():
    moment_count = 2 * K - 1
    entries = [[0.0] * (K * K) for index in range(moment_count)]
    for first_deg in range(K):
        for second_deg in range(K):
            for inner_m in range(min(first_deg, second_deg) + 1):
                target = first_deg + second_deg - 2 * inner_m
                weight = (
                    adams_factor(inner_m)
                    * adams_factor(first_deg - inner_m)
                    * adams_factor(second_deg - inner_m)
                )
                weight = weight / adams_factor(first_deg + second_deg - inner_m)
                weight = (
                    weight * (2.0 * target + 1.0) / (2.0 * (first_deg + second_deg - inner_m) + 1.0)
                )
                entries[target][first_deg * K + second_deg] += weight
    return jnp.asarray(entries, dtype=jnp.float32)


def lit_rows(line_start, first, count):
    rowid = first + jnp.arange(count, dtype=jnp.int32)
    low = line_start[:, None, :]
    inside = (rowid[None, :, None] >= low) & (rowid[None, :, None] < low + WIN)
    return jnp.any(inside, axis=2).astype(jnp.float32)


def profile_cols(trace, width, bundle_width, fiber_bundle, ptab):
    onehot = (
        fiber_bundle[:, None] == jnp.arange(bundle_width.shape[0], dtype=jnp.int32)[None, :]
    ).astype(jnp.float32)
    base = jnp.dot(onehot, bundle_width, precision=HIGH)
    centre = jnp.dot(ptab, trace.T, precision=HIGH)
    spread = base[None, :] * jnp.exp(jnp.dot(ptab, width.T, precision=HIGH))
    offsets = jnp.arange(PIX, dtype=jnp.float32) - (PIX - 1) / 2.0
    fibers = trace.shape[0]
    return (
        jnp.repeat(centre, PIX, axis=1),
        jnp.repeat(spread, PIX, axis=1),
        jnp.tile(offsets, fibers),
    )


def lamp_model(lit_row, amp_row, centre, spread, offsets):
    scaled = (offsets[None, :] - centre) / spread
    shape = lit_row[:, None] * amp_row[None, :] * jnp.exp(-0.5 * scaled * scaled)
    return (shape, scaled)


def accumulate(frames, lit, amp_cols, centre, spread, offsets):

    def accumulate_one_lamp(carry, item):
        frame, lit_row, amp_row = item
        shape, scaled = lamp_model(lit_row, amp_row, centre, spread, offsets)
        resid = frame.astype(jnp.float32) - shape
        slope = shape * scaled / spread
        widen = shape * scaled * scaled
        return (
            (
                carry[0] + slope * slope,
                carry[1] + slope * widen,
                carry[2] + widen * widen,
                carry[3] + resid * slope,
                carry[4] + resid * widen,
            ),
            None,
        )

    zeros = jnp.zeros(centre.shape, jnp.float32)
    sums, _ = lax.scan(
        accumulate_one_lamp, (zeros, zeros, zeros, zeros, zeros), (frames, lit, amp_cols)
    )
    rows_here, cols = centre.shape
    return tuple((item.reshape(rows_here, cols // PIX, PIX).sum(axis=2) for item in sums))


def assemble(nxx, nxs, nss):
    fibers = nxx.shape[0]
    upper = jnp.concatenate([nxx, nxs], axis=2)
    lower = jnp.concatenate([jnp.swapaxes(nxs, 1, 2), nss], axis=2)
    return jnp.concatenate([upper, lower], axis=1).reshape(fibers, 4 * K * K)


def gradient_cols(sums, ptab):
    return jnp.concatenate(
        [jnp.dot(sums[3].T, ptab, precision=HIGH), jnp.dot(sums[4].T, ptab, precision=HIGH)], axis=1
    )


def from_moments(moment_xx, moment_xs, moment_ss, link):
    fibers = moment_xx.shape[0]
    nxx = jnp.dot(moment_xx, link, precision=HIGH).reshape(fibers, K, K)
    nxs = jnp.dot(moment_xs, link, precision=HIGH).reshape(fibers, K, K)
    nss = jnp.dot(moment_ss, link, precision=HIGH).reshape(fibers, K, K)
    return assemble(nxx, nxs, nss)


def solve_step(normal, grad, trace, width):
    fibers = normal.shape[0]
    matrix = normal.reshape(fibers, 2 * K, 2 * K)
    diag_vals = jnp.diagonal(matrix, axis1=1, axis2=2)
    eye_mat = jnp.eye(2 * K, dtype=jnp.float32)
    matrix = matrix + (0.5 * diag_vals + 1.0)[:, :, None] * eye_mat[None, :, :]
    factor = jnp.linalg.cholesky(matrix)
    inner = jax.scipy.linalg.solve_triangular(factor, grad[:, :, None], lower=True)
    update = jax.scipy.linalg.solve_triangular(factor, inner, lower=True, trans=1)[:, :, 0]
    return (trace + update[:, :K], width + update[:, K:])


def residual_image(frames, lit, amp_cols, centre, spread, offsets):

    def residual_one_lamp(item):
        frame, lit_row, amp_row = item
        shape, scaled = lamp_model(lit_row, amp_row, centre, spread, offsets)
        return (frame.astype(jnp.float32) - shape).astype(jnp.bfloat16)

    return lax.map(residual_one_lamp, (frames, lit, amp_cols))


def body(frames, amplitude, line_start, bundle_width, fiber_bundle, trace_coef, width_coef):
    rows_here = frames.shape[1]
    nrow = rows_here * lax.axis_size("rows")
    first = lax.axis_index("rows") * rows_here
    ptab = legendre_table(first, rows_here, nrow)
    lit = lit_rows(line_start, first, rows_here)
    amp_cols = jnp.repeat(amplitude, PIX, axis=1)
    trace_all, width_all = (
        lax.all_gather(trace_coef, ("rows", "fib"), axis=0, tiled=True),
        lax.all_gather(width_coef, ("rows", "fib"), axis=0, tiled=True),
    )
    trace_own, width_own = (trace_coef, width_coef)
    wide_tab = legendre_upto(first, rows_here, nrow, 2 * K - 1)
    link = product_table()
    for step in range(ITERS):
        centre, spread, offsets = profile_cols(
            trace_all, width_all, bundle_width, fiber_bundle, ptab
        )
        sums = accumulate(frames, lit, amp_cols, centre, spread, offsets)
        moment_xx = jnp.dot(sums[0].T, wide_tab, precision=HIGH)
        moment_xs = jnp.dot(sums[1].T, wide_tab, precision=HIGH)
        moment_ss = jnp.dot(sums[2].T, wide_tab, precision=HIGH)
        grad = gradient_cols(sums, ptab)
        own_xx, own_xs, own_ss, grad_own = (
            lax.psum_scatter(moment_xx, ("rows", "fib"), scatter_dimension=0, tiled=True),
            lax.psum_scatter(moment_xs, ("rows", "fib"), scatter_dimension=0, tiled=True),
            lax.psum_scatter(moment_ss, ("rows", "fib"), scatter_dimension=0, tiled=True),
            lax.psum_scatter(grad, ("rows", "fib"), scatter_dimension=0, tiled=True),
        )
        normal_own = from_moments(own_xx, own_xs, own_ss, link)
        trace_own, width_own = solve_step(normal_own, grad_own, trace_own, width_own)
        trace_all, width_all = (
            lax.all_gather(trace_own, ("rows", "fib"), axis=0, tiled=True),
            lax.all_gather(width_own, ("rows", "fib"), axis=0, tiled=True),
        )
    centre, spread, offsets = profile_cols(trace_all, width_all, bundle_width, fiber_bundle, ptab)
    return (trace_own, width_own, residual_image(frames, lit, amp_cols, centre, spread, offsets))


def solution(mesh):
    return jax.shard_map(
        body,
        mesh=mesh,
        in_specs=(
            P("fib", "rows", None),
            P("fib", None),
            P("fib", None),
            P(),
            P(),
            P(("rows", "fib"), None),
            P(("rows", "fib"), None),
        ),
        out_specs=(P(("rows", "fib"), None), P(("rows", "fib"), None), P("fib", "rows", None)),
        check_vma=False,
    )
```

profile of v0, /device:TPU:0, one launch (start us, length us, event | category | flops | bytes accessed | tf_op | source)
XLA Modules:
  0.0 621.1 jit_solution(14535736433236922774)
XLA Ops:
  2.3 43.7 %all-gather.1 = f32[32,4,11]{2,1,0:T(4,128)S(1)} all-gather(f32[1,4,11]{2,1,0:T(4,128)} %bitcast.479), channel_id=1, replica_groups=mesh['rows'=8,'fib'=4] {'rows','fib'}, dimensions={0}, use_global_device_ids=true | all-gather | bytes 5808 | tf_op jit(solution)/shard_map/all_gather | solution.py:165
  46.4 37.1 %all-gather = f32[32,4,11]{2,1,0:T(4,128)S(1)} all-gather(f32[1,4,11]{2,1,0:T(4,128)} %bitcast.480), channel_id=1, replica_groups=mesh['rows'=8,'fib'=4] {'rows','fib'}, dimensions={0}, use_global_device_ids=true | all-gather | bytes 5808 | tf_op jit(solution)/shard_map/all_gather | solution.py:164
  89.7 29.6 %while.69 = (s32[]{:T(128)}, f32[128,1024]{0,1:T(8,128)S(1)}, f32[128,1024]{0,1:T(8,128)S(1)}, f32[128,1024]{0,1:T(8,128)S(1)}, f32[128,1024]{0,1:T(8,128)S(1)},...) while((s32[]{:T(128)}, f32[128,1024]{0,1:T(8,128)S(1)}, ...), condition=%wide.region_2.3_spmd.clone, body=%wide.region_1.2_spmd.clone.sunk | while | flops 3407875 | bytes 5666491 | solution.py:106
  98.8 2.6 select_add_fusion.18
  104.8 2.6 select_add_fusion.18
  116.7 2.6 select_add_fusion.18
  122.7 41.0 %all-reduce.14 = (f32[128,22]{0,1:T(8,128)S(1)}, f32[128,21]{1,0:T(8,128)S(1)}, f32[128,21]{1,0:T(8,128)S(1)}, f32[128,21]{1,0:T(8,128)S(1)}) all-reduce(f32[128,22]{0,1:T(8,128)S(1)} %pad_maximum_fusion, f32[128,21]{1,0:T(8,128)S(1)} %fusion.80, f32[128,21]{1,0:T(8,128)S(1)} %fusion.79, ...), channel_id=5, replica_groups=mesh['rows'=8,'fib'=4] {'rows','fib'}, use_global_device_ids=true, to_apply=%region_13.15.clone | all-reduce | flops 10880 | bytes 87040
  166.1 8.1 %custom-call.36 = f32[4,22,22]{2,1,0:T(8,128)S(1)} custom-call(f32[4,22,22]{2,1,0:T(8,128)S(1)} %fusion.59), custom_call_target="Cholesky" | custom-call | tf_op jit(solution)/shard_map/jit(cholesky)/cholesky | solution.py:140
  175.0 6.8 %custom-call.38 = f32[4,1,22,22]{2,3,1,0:T(8,128)S(1)} custom-call(f32[4,1,22,22]{3,2,1,0:T(8,128)S(1)} %select_bitcast_fusion.2), custom_call_target="InvertDiagBlocksLowerTriangular" | custom-call | tf_op jit(solution)/shard_map/jit(_solve_triangular)/vmap()/triangular_solve | solution.py:142
  182.9 39.6 %all-gather.3 = f32[32,4,11]{2,1,0:T(4,128)S(1)} all-gather(f32[1,4,11]{2,1,0:T(4,128)S(1)} %get-tuple-element.689), channel_id=1, replica_groups=mesh['rows'=8,'fib'=4] {'rows','fib'}, dimensions={0}, use_global_device_ids=true | all-gather | bytes 5808 | tf_op jit(solution)/shard_map/all_gather | solution.py:189
  222.9 36.8 %all-gather.2 = f32[32,4,11]{2,1,0:T(4,128)S(1)} all-gather(f32[1,4,11]{2,1,0:T(4,128)S(1)} %get-tuple-element.690), channel_id=1, replica_groups=mesh['rows'=8,'fib'=4] {'rows','fib'}, dimensions={0}, use_global_device_ids=true | all-gather | bytes 5808 | tf_op jit(solution)/shard_map/all_gather | solution.py:188
  260.6 32.4 %while.70 = (s32[]{:T(128)}, f32[128,1024]{0,1:T(8,128)S(1)}, f32[128,1024]{0,1:T(8,128)S(1)}, f32[128,1024]{0,1:T(8,128)S(1)}, f32[128,1024]{0,1:T(8,128)S(1)},...) while((s32[]{:T(128)}, f32[128,1024]{0,1:T(8,128)S(1)}, ...), condition=%wide.region_15.19_spmd.clone, body=%wide.region_14.18_spmd.clone.sunk | while | flops 3407875 | bytes 5666491 | solution.py:106
  295.6 41.2 %all-reduce.13 = (f32[128,22]{0,1:T(8,128)S(1)}, f32[128,21]{1,0:T(8,128)S(1)}, f32[128,21]{1,0:T(8,128)S(1)}, f32[128,21]{1,0:T(8,128)S(1)}) all-reduce(f32[128,22]{0,1:T(8,128)S(1)} %pad_maximum_fusion.1, f32[128,21]{1,0:T(8,128)S(1)} %fusion.86, ...), channel_id=9, replica_groups=mesh['rows'=8,'fib'=4] {'rows','fib'}, use_global_device_ids=true, to_apply=%region_24.28.clone | all-reduce | flops 10880 | bytes 87040
  339.2 8.1 %custom-call.39 = f32[4,22,22]{2,1,0:T(8,128)S(1)} custom-call(f32[4,22,22]{2,1,0:T(8,128)S(1)} %fusion.55), custom_call_target="Cholesky" | custom-call | tf_op jit(solution)/shard_map/jit(cholesky)/cholesky | solution.py:140
  347.5 6.8 %custom-call.41 = f32[4,1,22,22]{2,3,1,0:T(8,128)S(1)} custom-call(f32[4,1,22,22]{3,2,1,0:T(8,128)S(1)} %select_bitcast_fusion.1), custom_call_target="InvertDiagBlocksLowerTriangular" | custom-call | tf_op jit(solution)/shard_map/jit(_solve_triangular)/vmap()/triangular_solve | solution.py:142
  354.9 39.6 %all-gather.5 = f32[32,4,11]{2,1,0:T(4,128)S(1)} all-gather(f32[1,4,11]{2,1,0:T(4,128)S(1)} %get-tuple-element.687), channel_id=1, replica_groups=mesh['rows'=8,'fib'=4] {'rows','fib'}, dimensions={0}, use_global_device_ids=true | all-gather | bytes 5808 | tf_op jit(solution)/shard_map/all_gather | solution.py:189
  395.0 36.8 %all-gather.4 = f32[32,4,11]{2,1,0:T(4,128)S(1)} all-gather(f32[1,4,11]{2,1,0:T(4,128)S(1)} %get-tuple-element.688), channel_id=1, replica_groups=mesh['rows'=8,'fib'=4] {'rows','fib'}, dimensions={0}, use_global_device_ids=true | all-gather | bytes 5808 | tf_op jit(solution)/shard_map/all_gather | solution.py:188
  432.6 32.4 %while.71 = (s32[]{:T(128)}, f32[128,1024]{0,1:T(8,128)S(1)}, f32[128,1024]{0,1:T(8,128)S(1)}, f32[128,1024]{0,1:T(8,128)S(1)}, f32[128,1024]{0,1:T(8,128)S(1)},...) while((s32[]{:T(128)}, f32[128,1024]{0,1:T(8,128)S(1)}, ...), condition=%wide.region_26.30_spmd.clone, body=%wide.region_25.29_spmd.clone.sunk | while | flops 3407875 | bytes 5666491 | solution.py:106
  467.6 41.0 %all-reduce.12 = (f32[128,22]{0,1:T(8,128)S(1)}, f32[128,21]{1,0:T(8,128)S(1)}, f32[128,21]{1,0:T(8,128)S(1)}, f32[128,21]{1,0:T(8,128)S(1)}) all-reduce(f32[128,22]{0,1:T(8,128)S(1)} %pad_maximum_fusion.2, f32[128,21]{1,0:T(8,128)S(1)} %fusion.92, ...), channel_id=13, replica_groups=mesh['rows'=8,'fib'=4] {'rows','fib'}, use_global_device_ids=true, to_apply=%region_35.39.clone | all-reduce | flops 10880 | bytes 87040
  511.0 8.1 %custom-call.42 = f32[4,22,22]{2,1,0:T(8,128)S(1)} custom-call(f32[4,22,22]{2,1,0:T(8,128)S(1)} %fusion.51), custom_call_target="Cholesky" | custom-call | tf_op jit(solution)/shard_map/jit(cholesky)/cholesky | solution.py:140
  519.3 6.8 %custom-call.44 = f32[4,1,22,22]{2,3,1,0:T(8,128)S(1)} custom-call(f32[4,1,22,22]{3,2,1,0:T(8,128)S(1)} %select_bitcast_fusion), custom_call_target="InvertDiagBlocksLowerTriangular" | custom-call | tf_op jit(solution)/shard_map/jit(_solve_triangular)/vmap()/triangular_solve | solution.py:142
  526.8 39.6 %all-gather.7 = f32[32,4,11]{2,1,0:T(4,128)S(1)} all-gather(f32[1,4,11]{2,1,0:T(4,128)S(1)} %bitcast.482), channel_id=1, replica_groups=mesh['rows'=8,'fib'=4] {'rows','fib'}, dimensions={0}, use_global_device_ids=true | all-gather | bytes 5808 | tf_op jit(solution)/shard_map/all_gather | solution.py:189
  566.8 36.8 %all-gather.6 = f32[32,4,11]{2,1,0:T(4,128)S(1)} all-gather(f32[1,4,11]{2,1,0:T(4,128)S(1)} %bitcast.483), channel_id=1, replica_groups=mesh['rows'=8,'fib'=4] {'rows','fib'}, dimensions={0}, use_global_device_ids=true | all-gather | bytes 5808 | tf_op jit(solution)/shard_map/all_gather | solution.py:188
  603.8 17.3 %while.68 = (s32[]{:T(128)}, bf16[5,128,1024]{2,1,0:T(8,128)(2,1)}, bf16[5,128,1024]{1,2,0:T(8,128)(2,1)S(1)}, f32[5,128]{1,0:T(8,128)}, f32[5,1024]{1,0:T(8,128...) while((s32[]{:T(128)}, bf16[5,128,1024]{2,1,0:T(8,128)(2,1)}, ...), condition=%wide.region_37.41_spmd.clone, body=%wide.region_36.40_spmd.clone.sunk | while | flops 1179650 | bytes 1734793 | solution.py:153
  (385 shorter events, 133.7 us)
Async XLA Ops:
  2.3 84.1 %copy-start.29 = (f32[128]{0:T(128)}, f32[128]{0:T(128)S(1)}, u32[]{:S(2)}) copy-start(f32[128]{0:T(128)S(1)} %convolution_bitcast_fusion.3) | copy-start | bytes 1540
  120.9 42.7 %copy-start.6 = (f32[21,121]{1,0:T(8,128)S(1)}, f32[21,121]{1,0:T(8,128)}, u32[]{:S(2)}) copy-start(f32[21,121]{1,0:T(8,128)} %constant.247.clone) | copy-start | bytes 30496
  121.8 43.3 %copy-start.3 = (f32[128,21]{0,1:T(8,128)}, f32[128,21]{0,1:T(8,128)S(1)}, u32[]{:S(2)}) copy-start(f32[128,21]{0,1:T(8,128)S(1)} %stack.5) | copy-start | bytes 32260
  122.3 60.0 %copy-start.23 = (f32[4,11]{1,0:T(4,128)S(1)}, f32[4,11]{1,0:T(4,128)}, u32[]{:S(2)}) copy-start(f32[4,11]{1,0:T(4,128)} %param.27) | copy-start | bytes 532
  122.3 60.0 %copy-start.26 = (f32[4,11]{1,0:T(4,128)S(1)}, f32[4,11]{1,0:T(4,128)}, u32[]{:S(2)}) copy-start(f32[4,11]{1,0:T(4,128)} %param.26) | copy-start | bytes 532
  122.4 100.2 %copy-start.30 = (f32[128]{0:T(128)S(1)}, f32[128]{0:T(128)}, u32[]{:S(2)}) copy-start(f32[128]{0:T(128)} %copy-done.29) | copy-start | bytes 1540
  165.9 94.6 %copy-start.9 = (f32[22,22]{0,1:T(8,128)}, f32[22,22]{0,1:T(8,128)S(1)}, u32[]{:S(2)}) copy-start(f32[22,22]{0,1:T(8,128)S(1)} %fusion.61) | copy-start | bytes 5812
  294.6 44.5 %copy-start.10 = (f32[22,22]{0,1:T(8,128)S(1)}, f32[22,22]{0,1:T(8,128)}, u32[]{:S(2)}) copy-start(f32[22,22]{0,1:T(8,128)} %copy-done.9) | copy-start | bytes 5812
  294.8 52.5 %copy-start.21 = (pred[22,22]{1,0:T(8,128)(4,1)S(1)}, pred[22,22]{1,0:T(8,128)(4,1)}, u32[]{:S(2)}) copy-start(pred[22,22]{1,0:T(8,128)(4,1)} %copy-done.20) | copy-start | bytes 1456
  294.9 52.5 %copy-start.18 = (pred[22,22]{1,0:T(8,128)(4,1)S(1)}, pred[22,22]{1,0:T(8,128)(4,1)}, u32[]{:S(2)}) copy-start(pred[22,22]{1,0:T(8,128)(4,1)} %copy-done.17) | copy-start | bytes 1456
  294.9 59.9 %copy-start.13 = (f32[4,1,22]{2,1,0:T(1,128)S(1)}, f32[4,1,22]{2,1,0:T(1,128)}, u32[]{:S(2)}) copy-start(f32[4,1,22]{2,1,0:T(1,128)} %copy-done.12) | copy-start | bytes 1060
  295.0 59.9 %copy-start.24 = (f32[4,11]{1,0:T(4,128)S(1)}, f32[4,11]{1,0:T(4,128)}, u32[]{:S(2)}) copy-start(f32[4,11]{1,0:T(4,128)} %param.27) | copy-start | bytes 532
  295.0 59.9 %copy-start.27 = (f32[4,11]{1,0:T(4,128)S(1)}, f32[4,11]{1,0:T(4,128)}, u32[]{:S(2)}) copy-start(f32[4,11]{1,0:T(4,128)} %param.26) | copy-start | bytes 532
  295.2 99.4 %copy-start.31 = (f32[128]{0:T(128)S(1)}, f32[128]{0:T(128)}, u32[]{:S(2)}) copy-start(f32[128]{0:T(128)} %copy-done.29) | copy-start | bytes 1540
  466.6 44.3 %copy-start.11 = (f32[22,22]{0,1:T(8,128)S(1)}, f32[22,22]{0,1:T(8,128)}, u32[]{:S(2)}) copy-start(f32[22,22]{0,1:T(8,128)} %copy-done.9) | copy-start | bytes 5812
  466.8 52.3 %copy-start.22 = (pred[22,22]{1,0:T(8,128)(4,1)S(1)}, pred[22,22]{1,0:T(8,128)(4,1)}, u32[]{:S(2)}) copy-start(pred[22,22]{1,0:T(8,128)(4,1)} %copy-done.20) | copy-start | bytes 1456
  466.9 52.3 %copy-start.19 = (pred[22,22]{1,0:T(8,128)(4,1)S(1)}, pred[22,22]{1,0:T(8,128)(4,1)}, u32[]{:S(2)}) copy-start(pred[22,22]{1,0:T(8,128)(4,1)} %copy-done.17) | copy-start | bytes 1456
  466.9 59.7 %copy-start.14 = (f32[4,1,22]{2,1,0:T(1,128)S(1)}, f32[4,1,22]{2,1,0:T(1,128)}, u32[]{:S(2)}) copy-start(f32[4,1,22]{2,1,0:T(1,128)} %copy-done.12) | copy-start | bytes 1060
  467.0 59.7 %copy-start.16 = (f32[4,1,22]{2,1,0:T(1,128)S(1)}, f32[4,1,22]{2,1,0:T(1,128)}, u32[]{:S(2)}) copy-start(f32[4,1,22]{2,1,0:T(1,128)} %copy-done.15) | copy-start | bytes 1060
  467.0 59.7 %copy-start.25 = (f32[4,11]{1,0:T(4,128)S(1)}, f32[4,11]{1,0:T(4,128)}, u32[]{:S(2)}) copy-start(f32[4,11]{1,0:T(4,128)} %param.27) | copy-start | bytes 532
  467.0 59.7 %copy-start.28 = (f32[4,11]{1,0:T(4,128)S(1)}, f32[4,11]{1,0:T(4,128)}, u32[]{:S(2)}) copy-start(f32[4,11]{1,0:T(4,128)} %param.26) | copy-start | bytes 532
  467.2 99.2 %copy-start.32 = (f32[128]{0:T(128)S(1)}, f32[128]{0:T(128)}, u32[]{:S(2)}) copy-start(f32[128]{0:T(128)} %copy-done.29) | copy-start | bytes 1540
  526.8 77.1 %copy-start.33 = (f32[4,11]{1,0:T(4,128)}, f32[4,11]{1,0:T(4,128)S(1)}, u32[]{:S(2)}) copy-start(f32[4,11]{1,0:T(4,128)S(1)} %get-tuple-element.685) | copy-start | bytes 532
  526.8 77.1 %copy-start.34 = (f32[4,11]{1,0:T(4,128)}, f32[4,11]{1,0:T(4,128)S(1)}, u32[]{:S(2)}) copy-start(f32[4,11]{1,0:T(4,128)S(1)} %get-tuple-element.686) | copy-start | bytes 532
  (34 other events, 183.6 us)
where the time goes:
time: 624 us; the launch traced here: 621 us
  blocking collectives  433 us (69%)
  other arithmetic  91.9 us (15%)
  local copies, waits for them, and re-layouts  82.8 us (13%)
  matrix products  11.3 us (2%)
    unnamed x3, blocking collectives  123 us
    all_gather x3, blocking collectives, body(): lax.all_gather(width_own, ('rows', 'fib'), axis=0, tiled=True)  119 us
    all_gather x3, blocking collectives, body(): lax.all_gather(trace_own, ('rows', 'fib'), axis=0, tiled=True)  110 us
    all_gather x1, blocking collectives, body(): lax.all_gather(width_coef, ('rows', 'fib'), axis=0, tiled=True)  43.7 us
    add x15, other arithmetic, accumulate_one_lamp(): carry[4] + resid * widen  38 us
    all_gather x1, blocking collectives, body(): lax.all_gather(trace_coef, ('rows', 'fib'), axis=0, tiled=True)  37.1 us
    dynamic_slice x25, local copies, waits for them, and re-layouts, accumulate(): lax.scan(accumulate_one_lamp, (zeros, zeros, zeros, zeros, zeros), (frame...  27.6 us
    another operation x10, other arithmetic, solve_step(): factor = jnp.linalg.cholesky(matrix)  24.7 us

commit v1 on v0

v1 whole, which is shorter than its diff:
```python
import functools

import jax
import jax.numpy as jnp
from jax import lax
from jax.experimental import pallas as pl
from jax.experimental.pallas import tpu as pltpu
from jax.sharding import PartitionSpec as P

K = 11
PIX = 8
WIN = 8
ITERS = 3
SUB = 8
LANE = 128
KROWS = 24
RHS = 2 * K

HIGH = lax.Precision.HIGHEST
BOTH = ("rows", "fib")


def legendre_list(rowpos, total):
    tvals = (2.0 * rowpos + 1.0) / total - 1.0
    polys = [jnp.ones_like(tvals), tvals]
    for order in range(1, K - 1):
        polys.append(
            ((2 * order + 1) * tvals * polys[order] - order * polys[order - 1]) / (order + 1)
        )
    return polys


def stacked_legendre(rowpos, total):
    polys = legendre_list(rowpos, total)
    row = lax.broadcasted_iota(jnp.int32, (KROWS, rowpos.shape[1]), 0)
    table = jnp.zeros((KROWS, rowpos.shape[1]), jnp.float32)
    for order in range(K):
        table = jnp.where((row == order) | (row == K + order), polys[order], table)
    return jnp.where(row == RHS, 1.0, table)


def lit_by_lamp(start, first, rows):
    lamps, lines = start.shape
    rowid = first + lax.broadcasted_iota(jnp.int32, (lamps, rows), 1)
    lit = jnp.zeros((lamps, rows), jnp.float32)
    for line in range(lines):
        away = rowid - start[:, line : line + 1]
        lit = jnp.where((away >= 0) & (away < WIN), 1.0, lit)
    return lit


def lit_columns(lit):
    lamps, rows = lit.shape
    which = lax.broadcasted_iota(jnp.int32, (lamps, lamps * LANE), 1) // LANE
    own = lax.broadcasted_iota(jnp.int32, (lamps, lamps * LANE), 0)
    spread = jnp.where(which == own, 1.0, 0.0)
    return lax.dot_general(
        lit, spread, (((0,), (0,)), ((), ())), preferred_element_type=jnp.float32
    )


def per_column(values, tile):
    each = LANE // PIX
    part = (tile * each) // LANE
    lane = lax.broadcasted_iota(jnp.int32, (values.shape[0], LANE), 1)
    index = (tile * each) % LANE + lane // PIX
    block = values[:, part * LANE : (part + 1) * LANE]
    return jnp.take_along_axis(block, index, axis=1, mode="promise_in_bounds")


def collapse_kernel(owned, frames_ref, amp_ref, start_ref, out_ref, lit_ref):
    lamps, rows, cols = frames_ref.shape
    first = lax.axis_index("rows") * rows
    amp = amp_ref[...]
    lit = lit_by_lamp(start_ref[...], first, rows)
    lit_ref[...] = lit_columns(lit)
    square = lax.dot_general(
        amp * amp, lit, (((0,), (0,)), ((), ())), precision=HIGH, preferred_element_type=jnp.float32
    )
    wide = owned * PIX
    for dest in range(cols // wide):
        out_ref[dest, wide : wide + owned, :] = square[dest * owned : (dest + 1) * owned]
    for tile in range(cols // LANE):
        amp_cols = per_column(amp, tile)
        total = jnp.zeros((rows, LANE), jnp.float32)
        for lamp in range(lamps):
            frame = frames_ref[lamp, :, tile * LANE : (tile + 1) * LANE].astype(jnp.float32)
            weight = lit_ref[:, lamp * LANE : (lamp + 1) * LANE] * amp_cols[lamp : lamp + 1]
            total = total + weight * frame
        flipped = total.T
        for part in range(LANE // wide):
            out_ref[tile * (LANE // wide) + part, 0:wide, :] = flipped[
                part * wide : (part + 1) * wide
            ]


def collapse(frames, amplitude, line_start, owned, height, devices):
    lamps, rows, cols = frames.shape
    return pl.pallas_call(
        functools.partial(collapse_kernel, owned),
        out_shape=jax.ShapeDtypeStruct((devices, height, rows), jnp.float32),
        in_specs=[pl.BlockSpec(memory_space=pltpu.VMEM)] * 3,
        out_specs=pl.BlockSpec(memory_space=pltpu.VMEM),
        scratch_shapes=[pltpu.VMEM((rows, lamps * LANE), jnp.float32)],
        name="collapse",
    )(frames, amplitude, line_start)


def fit_kernel(
    height,
    sources,
    bundle_ref,
    which_ref,
    got_ref,
    trace_ref,
    width_ref,
    trace_out,
    width_out,
    send_ref,
    sum_ref,
    poly_ref,
    high_ref,
    low_ref,
    weight_ref,
    coef_ref,
    splat_ref,
    square_ref,
):
    owned = trace_ref.shape[0]
    wide = owned * PIX
    steps = got_ref.shape[0] // (height * sources)
    rows = got_ref.shape[1]
    total_rows = steps * rows
    used = wide + owned
    me = lax.axis_index("rows") * sources + lax.axis_index("fib")

    for group in range(steps // SUB):
        for item in range(used):
            value = None
            for source in range(sources):
                start = (group * SUB * sources + source) * height + item
                part = got_ref[pl.ds(start, SUB, stride=sources * height), :]
                value = part if value is None else value + part
            sum_ref[item, group * SUB : (group + 1) * SUB, :] = value

    rowpos = (
        lax.broadcasted_iota(jnp.int32, (steps, rows), 0) * rows
        + lax.broadcasted_iota(jnp.int32, (steps, rows), 1)
    ).astype(jnp.float32)
    polys = legendre_list(rowpos, total_rows)
    for order in range(K):
        poly_ref[order * steps : (order + 1) * steps, :] = polys[order]
        poly_ref[(K + order) * steps : (K + order + 1) * steps, :] = polys[order]
    poly_ref[RHS * steps : (RHS + 1) * steps, :] = jnp.ones((steps, rows), jnp.float32)
    poly_ref[(RHS + 1) * steps :, :] = jnp.zeros((steps, rows), jnp.float32)
    for step in range(steps):
        stack = poly_ref[pl.ds(step, KROWS, stride=steps), :]
        pairs = jnp.concatenate([stack * stack[i : i + 1] for i in range(K)], axis=0)
        high = pairs.astype(jnp.bfloat16)
        high_ref[:, step * rows : (step + 1) * rows] = high
        low_ref[:, step * rows : (step + 1) * rows] = (pairs - high.astype(jnp.float32)).astype(
            jnp.bfloat16
        )

    square_ref[...] = jnp.zeros_like(square_ref)
    square_ref[0:owned, 0:K] = trace_ref[...]
    square_ref[0:owned, K : 2 * K] = width_ref[...]
    coef_ref[...] = square_ref[...].T[0:KROWS]
    weight_ref[...] = jnp.zeros_like(weight_ref)

    inverse_base = []
    for fiber in range(owned):
        base = bundle_ref[which_ref[me * owned + fiber]]
        inverse_base.append(1.0 / jnp.full((1, rows), base, jnp.float32))

    def newton_step(index, carry):
        for fiber in range(owned):
            splat_ref[fiber] = jnp.broadcast_to(
                coef_ref[:, fiber : fiber + 1], (KROWS, rows)
            )
        for group in range(steps // SUB):
            here = slice(group * SUB, (group + 1) * SUB)
            for fiber in range(owned):
                centre = jnp.zeros((SUB, rows), jnp.float32)
                spread = jnp.zeros((SUB, rows), jnp.float32)
                for order in range(K):
                    poly = poly_ref[order * steps + group * SUB : order * steps + (group + 1) * SUB, :]
                    centre = centre + splat_ref[fiber, order : order + 1, :] * poly
                    spread = spread + splat_ref[fiber, K + order : K + order + 1, :] * poly
                inverse = jnp.exp(-spread) * inverse_base[fiber]
                power = sum_ref[wide + fiber, here, :]
                sums = [jnp.zeros((SUB, rows), jnp.float32) for _ in range(5)]
                for pixel in range(PIX):
                    scaled = ((pixel - (PIX - 1) / 2.0) - centre) * inverse
                    shape = jnp.exp(-0.5 * scaled * scaled)
                    bend = shape * scaled
                    slope = bend * inverse
                    widen = bend * scaled
                    resid = sum_ref[fiber * PIX + pixel, here, :] - power * shape
                    sums[0] = sums[0] + slope * slope
                    sums[1] = sums[1] + slope * widen
                    sums[2] = sums[2] + widen * widen
                    sums[3] = sums[3] + resid * slope
                    sums[4] = sums[4] + resid * widen
                for kind in range(5):
                    value = sums[kind] * power if kind < 3 else sums[kind]
                    at = (kind * owned + fiber) * steps + group * SUB
                    weight_ref[at : at + SUB, :] = value
        count = weight_ref.shape[0] // steps
        weights = jnp.concatenate(
            [weight_ref[pl.ds(step, count, stride=steps), :] for step in range(steps)], axis=1
        )
        upper = weights.astype(jnp.bfloat16).astype(jnp.float32)
        both = jnp.concatenate([upper, weights - upper], axis=0).astype(jnp.bfloat16)
        dims = (((1,), (1,)), ((), ()))
        moments = lax.dot_general(
            high_ref[...], both, dims, preferred_element_type=jnp.float32
        ) + lax.dot_general(low_ref[...], both, dims, preferred_element_type=jnp.float32)
        lanes = moments.shape[1]
        moments = jnp.concatenate(
            [moments, jnp.zeros((moments.shape[0], LANE - lanes), jnp.float32)], axis=1
        )
        moments = moments + pltpu.roll(moments, LANE - count, 1)
        aligned = [moments] + [
            pltpu.roll(moments, LANE - kind * owned, 1) for kind in range(1, 5)
        ]
        row = lax.broadcasted_iota(jnp.int32, (KROWS, LANE), 0)

        def matrix_row(i, second):
            block = [item[i * KROWS : (i + 1) * KROWS] for item in aligned]
            left, right, side = (block[1], block[2], block[4]) if second else (
                block[0],
                block[1],
                block[3],
            )
            value = jnp.where(row < K, left, jnp.where(row < 2 * K, right, side))
            at = i + K if second else i
            return jnp.where(row == at, 1.5 * value + 1.0, value)

        matrix = [matrix_row(i, False) for i in range(K)] + [matrix_row(i, True) for i in range(K)]
        for pivot in range(2 * K):
            cut = KROWS - matrix[pivot].shape[0]
            inverse = 1.0 / matrix[pivot][pivot - cut : pivot - cut + 1]
            chosen = matrix[pivot] * inverse
            for i in range(2 * K):
                if i != pivot:
                    scale = matrix[i][pivot - cut : pivot - cut + 1]
                    matrix[i] = matrix[i] - scale * chosen
            matrix[pivot] = chosen
            if (pivot + 1) % SUB == 0:
                matrix = [item[SUB:] for item in matrix]
        for i in range(2 * K):
            cut = KROWS - matrix[i].shape[0]
            coef_ref[i : i + 1, :] = coef_ref[i : i + 1, :] + matrix[i][RHS - cut : RHS - cut + 1]
        return carry

    lax.fori_loop(0, ITERS, newton_step, 0)

    square_ref[...] = jnp.zeros_like(square_ref)
    lane = lax.broadcasted_iota(jnp.int32, (KROWS, LANE), 1)
    square_ref[0:KROWS, :] = jnp.where(lane < owned, coef_ref[...], 0.0)
    result = square_ref[...].T[0:owned]
    trace_out[...] = result[:, 0:K]
    width_out[...] = result[:, K : 2 * K]
    for device in range(send_ref.shape[0]):
        send_ref[device] = result


def fit(got, bundle_width, fiber_bundle, trace_coef, width_coef, devices, height, sources):
    owned = trace_coef.shape[0]
    rows = got.shape[1]
    steps = devices // sources
    count = -(-5 * owned // SUB) * SUB
    vmem = pl.BlockSpec(memory_space=pltpu.VMEM)
    smem = pl.BlockSpec(memory_space=pltpu.SMEM)
    return pl.pallas_call(
        functools.partial(fit_kernel, height, sources),
        out_shape=(
            jax.ShapeDtypeStruct((owned, K), jnp.float32),
            jax.ShapeDtypeStruct((owned, K), jnp.float32),
            jax.ShapeDtypeStruct((devices, owned, LANE), jnp.float32),
        ),
        in_specs=[smem, smem, vmem, vmem, vmem],
        out_specs=(vmem, vmem, vmem),
        scratch_shapes=[
            pltpu.VMEM((owned * PIX + owned, steps, rows), jnp.float32),
            pltpu.VMEM((KROWS * steps, rows), jnp.float32),
            pltpu.VMEM((K * KROWS, steps * rows), jnp.bfloat16),
            pltpu.VMEM((K * KROWS, steps * rows), jnp.bfloat16),
            pltpu.VMEM((count * steps, rows), jnp.float32),
            pltpu.VMEM((KROWS, LANE), jnp.float32),
            pltpu.VMEM((owned, KROWS, rows), jnp.float32),
            pltpu.VMEM((LANE, LANE), jnp.float32),
        ],
        name="fit",
    )(bundle_width, fiber_bundle, got, trace_coef, width_coef)


def residual_kernel(
    bundle_ref, which_ref, coef_ref, frames_ref, amp_ref, start_ref, out_ref, lit_ref
):
    lamps, rows, cols = frames_ref.shape
    total_rows = rows * lax.axis_size("rows")
    fibers = coef_ref.shape[0]
    first = lax.axis_index("rows") * rows
    lit_ref[...] = lit_columns(lit_by_lamp(start_ref[...], first, rows))
    which = which_ref[...]
    base = jnp.zeros((1, fibers), jnp.float32)
    for bundle in range(bundle_ref.shape[0]):
        base = jnp.where(which == bundle, bundle_ref[bundle], base)

    rowpos = (first + lax.broadcasted_iota(jnp.int32, (1, rows), 1)).astype(jnp.float32)
    stack = stacked_legendre(rowpos, total_rows)
    row = lax.broadcasted_iota(jnp.int32, (KROWS, rows), 0)
    tables = jnp.concatenate(
        [jnp.where(row < K, stack, 0.0), jnp.where((row >= K) & (row < 2 * K), stack, 0.0)], axis=1
    )
    coef = coef_ref[...].T[0:KROWS]
    curves = lax.dot_general(
        tables, coef, (((0,), (0,)), ((), ())), precision=HIGH, preferred_element_type=jnp.float32
    )
    centre = curves[0:rows]
    inverse = jnp.exp(-curves[rows : 2 * rows]) * (1.0 / base)
    amp = amp_ref[...]
    pixel = (lax.broadcasted_iota(jnp.int32, (rows, LANE), 1) % PIX).astype(jnp.float32)
    offset = pixel - (PIX - 1) / 2.0
    for tile in range(cols // LANE):
        here = slice(tile * LANE, (tile + 1) * LANE)
        scaled = (offset - per_column(centre, tile)) * per_column(inverse, tile)
        shape = jnp.exp(-0.5 * scaled * scaled)
        amp_cols = per_column(amp, tile)
        for lamp in range(lamps):
            weight = lit_ref[:, lamp * LANE : (lamp + 1) * LANE] * amp_cols[lamp : lamp + 1]
            frame = frames_ref[lamp, :, here].astype(jnp.float32)
            out_ref[lamp, :, here] = (frame - weight * shape).astype(jnp.bfloat16)


def residual(bundle_width, fiber_bundle, coef, frames, amplitude, line_start):
    lamps, rows, cols = frames.shape
    vmem = pl.BlockSpec(memory_space=pltpu.VMEM)
    smem = pl.BlockSpec(memory_space=pltpu.SMEM)
    return pl.pallas_call(
        residual_kernel,
        out_shape=jax.ShapeDtypeStruct(frames.shape, jnp.bfloat16),
        in_specs=[smem, vmem, vmem, vmem, vmem, vmem],
        out_specs=vmem,
        scratch_shapes=[pltpu.VMEM((rows, lamps * LANE), jnp.float32)],
        name="residual",
    )(bundle_width, fiber_bundle.reshape(1, -1), coef, frames, amplitude, line_start)


def body(frames, amplitude, line_start, bundle_width, fiber_bundle, trace_coef, width_coef):
    sources = lax.axis_size("fib")
    devices = lax.axis_size("rows") * sources
    rows = frames.shape[1]
    owned = trace_coef.shape[0]
    height = -(-(owned * PIX + owned) // SUB) * SUB
    partial = collapse(frames, amplitude, line_start, owned, height, devices)
    got = lax.all_to_all(partial, BOTH, 0, 0, tiled=True).reshape(devices * height, rows)
    trace_fit, width_fit, send = fit(
        got, bundle_width, fiber_bundle, trace_coef, width_coef, devices, height, sources
    )
    coef = lax.all_to_all(send, BOTH, 0, 0, tiled=True).reshape(devices * owned, LANE)
    image = residual(bundle_width, fiber_bundle, coef, frames, amplitude, line_start)
    return (trace_fit, width_fit, image)


def solution(mesh):
    return jax.shard_map(
        body,
        mesh=mesh,
        in_specs=(
            P("fib", "rows", None),
            P("fib", None),
            P("fib", None),
            P(),
            P(),
            P(BOTH, None),
            P(BOTH, None),
        ),
        out_specs=(P(BOTH, None), P(BOTH, None), P("fib", "rows", None)),
        check_vma=False,
    )
```

time: 624 us -> 50 us (0.08)
  blocking collectives: 433 us -> 36.4 us
  other arithmetic: 91.9 us -> 0 us
  local copies, waits for them, and re-layouts: 82.8 us -> 0 us
  Pallas kernels: 0 us -> 12.7 us
  matrix products: 11.3 us -> 0 us
    all_gather x8 -> x0, blocking collectives: 310 us -> none  [the longest x3 119 us: body(): lax.all_gather(width_own, ('rows', 'fib'), axis=0, tiled=True)]
    unnamed x3 -> x0, blocking collectives: 123 us -> none
    another operation x17 -> x0, other arithmetic: 45.2 us -> none  [the longest x10 24.7 us: solve_step(): factor = jnp.linalg.cholesky(matrix)]
    add x24 -> x0, other arithmetic: 38.8 us -> none  [the longest x15 38 us: accumulate_one_lamp(): carry[4] + resid * widen]
    all_to_all x0 -> x2, blocking collectives: none -> 36.4 us  [the longest x1 25.4 us: body(): lax.all_to_all(partial, BOTH, 0, 0, tiled=True)]
    dynamic_slice x25 -> x0, local copies, waits for them, and re-layouts: 27.6 us -> none  [accumulate(): lax.scan(accumulate_one_lamp, (zeros, zeros, zeros, zeros, zeros), (frame...]
    mul x15 -> x0, local copies, waits for them, and re-layouts: 18.6 us -> none  [lamp_model(): lit_row[:, None] * amp_row[None, :] * jnp.exp(-0.5 * scaled * scaled)]
    another operation x29 -> x0, local copies, waits for them, and re-layouts: 14.2 us -> none  [the longest x20 13.6 us: profile_cols(): jnp.tile(offsets, fibers)]
where the time goes in v1:
time: 50 us; the launch traced here: 49.7 us
  blocking collectives  36.4 us (73%)
  Pallas kernels  12.7 us (25%)
  between operations  0.63 us (1%)
    all_to_all x1, blocking collectives, body(): lax.all_to_all(partial, BOTH, 0, 0, tiled=True)  25.4 us
    all_to_all x1, blocking collectives, body(): lax.all_to_all(send, BOTH, 0, 0, tiled=True).reshape(devices * owned, LANE)  10.9 us
    pallas_call x1, Pallas kernels, fit(): pl.pallas_call(functools.partial(fit_kernel, height, sources), out_shape=...  5.98 us
    pallas_call x1, Pallas kernels, residual(): pl.pallas_call(residual_kernel, out_shape=jax.ShapeDtypeStruct(frames.sha...  3.83 us
    pallas_call x1, Pallas kernels, collapse(): pl.pallas_call(functools.partial(collapse_kernel, owned), out_shape=jax.S...  2.88 us

profile of v1, /device:TPU:0, one launch (start us, length us, event | category | flops | bytes accessed | tf_op | source)
XLA Modules:
  0.0 49.7 jit_solution(2272351263143761574)
XLA Ops:
  0.6 2.9 %collapse.1 = f32[32,40,128]{2,1,0:T(8,128)} custom-call(bf16[5,128,1024]{2,1,0:T(8,128)(2,1)} %frames_ref.3, f32[5,128]{1,0:T(8,128)} %amp_ref.3, s32[5,24]{1,0:T(8,128)} %start_ref.3), custom_call_target="tpu_custom_call" | custom-call | tf_op jit(solution)/shard_map/collapse/pallas_call | solution.py:99
  3.5 25.4 %all_to_all.10 = f32[32,40,128]{2,1,0:T(8,128)} all-to-all(f32[32,40,128]{2,1,0:T(8,128)} %collapse.1), channel_id=1, replica_groups=mesh['rows'=8,'fib'=4] {'rows','fib'}, dimensions={0} | all-to-all | bytes 1310720 | tf_op jit(solution)/shard_map/all_to_all | solution.py:359
  28.9 6.0 %fit.1 = (f32[4,11]{1,0:T(4,128)}, f32[4,11]{1,0:T(4,128)}, f32[32,4,128]{2,1,0:T(4,128)}) custom-call(f32[20]{0:T(128)} %bundle_ref.3, s32[128]{0:T(128)} %which_ref.1, f32[1280,128]{1,0:T(8,128)} %bitcast.3, f32[4,11]{1,0:T(4,128)} %trace_ref.1, f32[4,11]{1,0:T(4,128)} %width_ref.1), custom_call_target="tpu_custom_call" | custom-call | tf_op jit(solution)/shard_map/fit/pallas_call | solution.py:276
  34.9 10.9 %all_to_all.11 = f32[32,4,128]{2,1,0:T(4,128)} all-to-all(f32[32,4,128]{2,1,0:T(4,128)} %get-tuple-element.8), channel_id=1, replica_groups=mesh['rows'=8,'fib'=4] {'rows','fib'}, dimensions={0} | all-to-all | bytes 131072 | tf_op jit(solution)/shard_map/all_to_all | solution.py:363
  45.9 3.8 %residual.1 = bf16[5,128,1024]{2,1,0:T(8,128)(2,1)} custom-call(f32[20]{0:T(128)} %bundle_ref.3, s32[1,128]{1,0:T(1,128)} %bitcast.5, f32[128,128]{1,0:T(8,128)} %bitcast.4, bf16[5,128,1024]{2,1,0:T(8,128)(2,1)} %frames_ref.3, f32[5,128]{1,0:T(8,128)} %amp_ref.3, s32[5,24]{1,0:T(8,128)} %start_ref.3), custom_call_target="tpu_custom_call" | custom-call | tf_op jit(solution)/shard_map/residual/pallas_call | solution.py:342

commit v2 on v1

--- a/solution.py
+++ b/solution.py
@@ -15,6 +15,7 @@
 LANE = 128
 KROWS = 24
 RHS = 2 * K
+VMEM_BYTES = 20 << 20
 
 HIGH = lax.Precision.HIGHEST
 BOTH = ("rows", "fib")
@@ -102,6 +103,7 @@
         in_specs=[pl.BlockSpec(memory_space=pltpu.VMEM)] * 3,
         out_specs=pl.BlockSpec(memory_space=pltpu.VMEM),
         scratch_shapes=[pltpu.VMEM((rows, lamps * LANE), jnp.float32)],
+        compiler_params=pltpu.CompilerParams(vmem_limit_bytes=VMEM_BYTES),
         name="collapse",
     )(frames, amplitude, line_start)
 
@@ -292,6 +294,7 @@
             pltpu.VMEM((owned, KROWS, rows), jnp.float32),
             pltpu.VMEM((LANE, LANE), jnp.float32),
         ],
+        compiler_params=pltpu.CompilerParams(vmem_limit_bytes=VMEM_BYTES),
         name="fit",
     )(bundle_width, fiber_bundle, got, trace_coef, width_coef)
 
@@ -345,6 +348,7 @@
         in_specs=[smem, vmem, vmem, vmem, vmem, vmem],
         out_specs=vmem,
         scratch_shapes=[pltpu.VMEM((rows, lamps * LANE), jnp.float32)],
+        compiler_params=pltpu.CompilerParams(vmem_limit_bytes=VMEM_BYTES),
         name="residual",
     )(bundle_width, fiber_bundle.reshape(1, -1), coef, frames, amplitude, line_start)
 

time: 50 us -> 48.4 us (0.968)
  Pallas kernels: 12.7 us -> 9.05 us
  local copies, waits for them, and re-layouts: 0 us -> 2.71 us
  blocking collectives: 36.4 us -> 35.7 us
    unnamed x0 -> x16, local copies, waits for them, and re-layouts: none -> 2.71 us
    pallas_call x1, Pallas kernels: 2.88 us -> 0.7 us  [collapse(): pl.pallas_call(functools.partial(collapse_kernel, owned), out_shape=jax.S...]
    pallas_call x1, Pallas kernels: 3.83 us -> 2.98 us  [residual(): pl.pallas_call(residual_kernel, out_shape=jax.ShapeDtypeStruct(frames.sha...]
    pallas_call x1, Pallas kernels: 5.98 us -> 5.36 us  [fit(): pl.pallas_call(functools.partial(fit_kernel, height, sources), out_shape=...]
where the time goes in v2:
time: 48.4 us; the launch traced here: 48.2 us
  blocking collectives  35.7 us (74%)
  Pallas kernels  9.05 us (19%)
  local copies, waits for them, and re-layouts  2.71 us (6%)
  between operations  0.68 us (1%)
    all_to_all x1, blocking collectives, body(): lax.all_to_all(partial, BOTH, 0, 0, tiled=True)  25.1 us
    all_to_all x1, blocking collectives, body(): lax.all_to_all(send, BOTH, 0, 0, tiled=True).reshape(devices * owned, LANE)  10.6 us
    pallas_call x1, Pallas kernels, fit(): pl.pallas_call(functools.partial(fit_kernel, height, sources), out_shape=...  5.36 us
    pallas_call x1, Pallas kernels, residual(): pl.pallas_call(residual_kernel, out_shape=jax.ShapeDtypeStruct(frames.sha...  2.98 us
    unnamed x16, local copies, waits for them, and re-layouts  2.71 us

profile of v2, /device:TPU:0, one launch (start us, length us, event | category | flops | bytes accessed | tf_op | source)
XLA Modules:
  0.0 48.2 jit_solution(10020268372739306029)
XLA Ops:
  0.6 0.0 copy-start
  0.6 1.3 %copy-done = bf16[5,128,1024]{2,1,0:T(8,128)(2,1)S(1)} copy-done((bf16[5,128,1024]{2,1,0:T(8,128)(2,1)S(1)}, bf16[5,128,1024]{2,1,0:T(8,128)(2,1)}, u32[]{:S(2)}) %copy-start) | copy-done | bytes 1310744
  2.0 0.0 copy-start.2
  2.0 0.7 %copy-done.2 = f32[5,128]{1,0:T(8,128)S(1)} copy-done((f32[5,128]{1,0:T(8,128)S(1)}, f32[5,128]{1,0:T(8,128)}, u32[]{:S(2)}) %copy-start.2) | copy-done | bytes 2584
  2.6 0.0 copy-start.3
  2.6 0.7 %copy-done.3 = s32[5,24]{1,0:T(8,128)S(1)} copy-done((s32[5,24]{1,0:T(8,128)S(1)}, s32[5,24]{1,0:T(8,128)}, u32[]{:S(2)}) %copy-start.3) | copy-done | bytes 504
  3.3 0.0 copy-start.4
  3.3 0.0 copy-start.5
  3.3 0.0 copy-start.6
  3.3 0.0 copy-start.7
  3.3 0.7 %collapse.1 = f32[32,40,128]{2,1,0:T(8,128)S(1)} custom-call(bf16[5,128,1024]{2,1,0:T(8,128)(2,1)S(1)} %copy-done, f32[5,128]{1,0:T(8,128)S(1)} %copy-done.2, s32[5,24]{1,0:T(8,128)S(1)} %copy-done.3), custom_call_target="tpu_custom_call" | custom-call | tf_op jit(solution)/shard_map/collapse/pallas_call | solution.py:100
  4.0 0.0 copy-start.1
  4.1 25.1 %all_to_all.10 = f32[32,40,128]{2,1,0:T(8,128)S(1)} all-to-all(f32[32,40,128]{2,1,0:T(8,128)S(1)} %collapse.1), channel_id=1, replica_groups=mesh['rows'=8,'fib'=4] {'rows','fib'}, dimensions={0} | all-to-all | bytes 1310720 | tf_op jit(solution)/shard_map/all_to_all | solution.py:363
  29.2 0.0 copy-done.4
  29.2 0.0 copy-done.5
  29.2 0.0 copy-done.6
  29.2 0.0 copy-done.7
  29.2 5.4 %fit.1 = (f32[4,11]{1,0:T(4,128)}, f32[4,11]{1,0:T(4,128)}, f32[32,4,128]{2,1,0:T(4,128)S(1)}) custom-call(f32[20]{0:T(128)S(1)} %copy-done.6, s32[128]{0:T(128)S(1)} %copy-done.7, f32[1280,128]{1,0:T(8,128)S(1)} %bitcast.3, f32[4,11]{1,0:T(4,128)S(1)} %copy-done.4, f32[4,11]{1,0:T(4,128)S(1)} %copy-done.5), custom_call_target="tpu_custom_call" | custom-call | tf_op jit(solution)/shard_map/fit/pallas_call | solution.py:278
  34.6 10.6 %all_to_all.11 = f32[32,4,128]{2,1,0:T(4,128)S(1)} all-to-all(f32[32,4,128]{2,1,0:T(4,128)S(1)} %get-tuple-element.8), channel_id=1, replica_groups=mesh['rows'=8,'fib'=4] {'rows','fib'}, dimensions={0} | all-to-all | bytes 131072 | tf_op jit(solution)/shard_map/all_to_all | solution.py:367
  45.2 0.0 copy-done.1
  45.2 3.0 %residual.1 = bf16[5,128,1024]{2,1,0:T(8,128)(2,1)} custom-call(f32[20]{0:T(128)S(1)} %copy-done.6, s32[1,128]{1,0:T(1,128)S(1)} %bitcast.5, f32[128,128]{1,0:T(8,128)S(1)} %bitcast.4, bf16[5,128,1024]{2,1,0:T(8,128)(2,1)S(1)} %copy-done.1, f32[5,128]{1,0:T(8,128)S(1)} %copy-done.2, s32[5,24]{1,0:T(8,128)S(1)} %copy-done.3), custom_call_target="tpu_custom_call" | custom-call | tf_op jit(solution)/shard_map/residual/pallas_call | solution.py:345
Async XLA Ops:
  0.6 1.3 %copy-start = (bf16[5,128,1024]{2,1,0:T(8,128)(2,1)S(1)}, bf16[5,128,1024]{2,1,0:T(8,128)(2,1)}, u32[]{:S(2)}) copy-start(bf16[5,128,1024]{2,1,0:T(8,128)(2,1)} %frames_ref.3) | copy-start | bytes 3932164
  2.0 0.7 %copy-start.2 = (f32[5,128]{1,0:T(8,128)S(1)}, f32[5,128]{1,0:T(8,128)}, u32[]{:S(2)}) copy-start(f32[5,128]{1,0:T(8,128)} %amp_ref.3) | copy-start | bytes 7684
  2.6 0.7 %copy-start.3 = (s32[5,24]{1,0:T(8,128)S(1)}, s32[5,24]{1,0:T(8,128)}, u32[]{:S(2)}) copy-start(s32[5,24]{1,0:T(8,128)} %start_ref.3) | copy-start | bytes 1444
  3.3 25.9 %copy-start.4 = (f32[4,11]{1,0:T(4,128)S(1)}, f32[4,11]{1,0:T(4,128)}, u32[]{:S(2)}) copy-start(f32[4,11]{1,0:T(4,128)} %trace_ref.1) | copy-start | bytes 532
  3.3 25.9 %copy-start.5 = (f32[4,11]{1,0:T(4,128)S(1)}, f32[4,11]{1,0:T(4,128)}, u32[]{:S(2)}) copy-start(f32[4,11]{1,0:T(4,128)} %width_ref.1) | copy-start | bytes 532
  3.3 25.9 %copy-start.6 = (f32[20]{0:T(128)S(1)}, f32[20]{0:T(128)}, u32[]{:S(2)}) copy-start(f32[20]{0:T(128)} %bundle_ref.3) | copy-start | bytes 244
  3.3 25.9 %copy-start.7 = (s32[128]{0:T(128)S(1)}, s32[128]{0:T(128)}, u32[]{:S(2)}) copy-start(s32[128]{0:T(128)} %which_ref.1) | copy-start | bytes 1540
  4.0 41.1 %copy-start.1 = (bf16[5,128,1024]{2,1,0:T(8,128)(2,1)S(1)}, bf16[5,128,1024]{2,1,0:T(8,128)(2,1)}, u32[]{:S(2)}) copy-start(bf16[5,128,1024]{2,1,0:T(8,128)(2,1)} %frames_ref.3) | copy-start | bytes 3932164

commit v3 on v2

--- a/solution.py
+++ b/solution.py
@@ -16,6 +16,7 @@
 KROWS = 24
 RHS = 2 * K
 VMEM_BYTES = 20 << 20
+CHUNK = 256
 
 HIGH = lax.Precision.HIGHEST
 BOTH = ("rows", "fib")
@@ -69,81 +70,66 @@
     return jnp.take_along_axis(block, index, axis=1, mode="promise_in_bounds")
 
 
-def collapse_kernel(owned, frames_ref, amp_ref, start_ref, out_ref, lit_ref):
-    lamps, rows, cols = frames_ref.shape
-    first = lax.axis_index("rows") * rows
-    amp = amp_ref[...]
-    lit = lit_by_lamp(start_ref[...], first, rows)
-    lit_ref[...] = lit_columns(lit)
-    square = lax.dot_general(
-        amp * amp, lit, (((0,), (0,)), ((), ())), precision=HIGH, preferred_element_type=jnp.float32
-    )
-    wide = owned * PIX
-    for dest in range(cols // wide):
-        out_ref[dest, wide : wide + owned, :] = square[dest * owned : (dest + 1) * owned]
-    for tile in range(cols // LANE):
-        amp_cols = per_column(amp, tile)
-        total = jnp.zeros((rows, LANE), jnp.float32)
-        for lamp in range(lamps):
-            frame = frames_ref[lamp, :, tile * LANE : (tile + 1) * LANE].astype(jnp.float32)
-            weight = lit_ref[:, lamp * LANE : (lamp + 1) * LANE] * amp_cols[lamp : lamp + 1]
-            total = total + weight * frame
-        flipped = total.T
-        for part in range(LANE // wide):
-            out_ref[tile * (LANE // wide) + part, 0:wide, :] = flipped[
-                part * wide : (part + 1) * wide
-            ]
-
-
-def collapse(frames, amplitude, line_start, owned, height, devices):
-    lamps, rows, cols = frames.shape
-    return pl.pallas_call(
-        functools.partial(collapse_kernel, owned),
-        out_shape=jax.ShapeDtypeStruct((devices, height, rows), jnp.float32),
-        in_specs=[pl.BlockSpec(memory_space=pltpu.VMEM)] * 3,
-        out_specs=pl.BlockSpec(memory_space=pltpu.VMEM),
-        scratch_shapes=[pltpu.VMEM((rows, lamps * LANE), jnp.float32)],
-        compiler_params=pltpu.CompilerParams(vmem_limit_bytes=VMEM_BYTES),
-        name="collapse",
-    )(frames, amplitude, line_start)
-
-
-def fit_kernel(
-    height,
-    sources,
-    bundle_ref,
-    which_ref,
-    got_ref,
-    trace_ref,
-    width_ref,
-    trace_out,
-    width_out,
+def start_copies(sources, targets, sems):
+    copies = [
+        pltpu.make_async_copy(source, target, sems.at[index])
+        for index, (source, target) in enumerate(zip(sources, targets))
+    ]
+    for copy in copies:
+        copy.start()
+    return copies
+
+
+def collapse_kernel(
+    frames_hbm,
+    amp_hbm,
+    start_hbm,
+    bundle_hbm,
+    which_hbm,
+    trace_hbm,
+    width_hbm,
+    keep_ref,
     send_ref,
-    sum_ref,
+    lit_ref,
+    table_ref,
+    base_ref,
+    own_base_ref,
+    coef_ref,
     poly_ref,
     high_ref,
     low_ref,
-    weight_ref,
-    coef_ref,
-    splat_ref,
+    frames_ref,
+    amp_ref,
+    start_ref,
+    bundle_ref,
+    which_ref,
+    trace_ref,
+    width_ref,
     square_ref,
+    small_sems,
+    frame_sems,
 ):
+    lamps, rows, cols = frames_ref.shape
     owned = trace_ref.shape[0]
-    wide = owned * PIX
-    steps = got_ref.shape[0] // (height * sources)
-    rows = got_ref.shape[1]
+    fibers = which_ref.shape[1]
+    steps = lax.axis_size("rows")
     total_rows = steps * rows
-    used = wide + owned
-    me = lax.axis_index("rows") * sources + lax.axis_index("fib")
-
-    for group in range(steps // SUB):
-        for item in range(used):
-            value = None
-            for source in range(sources):
-                start = (group * SUB * sources + source) * height + item
-                part = got_ref[pl.ds(start, SUB, stride=sources * height), :]
-                value = part if value is None else value + part
-            sum_ref[item, group * SUB : (group + 1) * SUB, :] = value
+    me = lax.axis_index("rows") * lax.axis_size("fib") + lax.axis_index("fib")
+    first = lax.axis_index("rows") * rows
+    odd = lax.axis_index("fib") % 2 == 1
+
+    small = start_copies(
+        [amp_hbm, start_hbm, bundle_hbm, which_hbm, trace_hbm, width_hbm],
+        [amp_ref, start_ref, bundle_ref, which_ref, trace_ref, width_ref],
+        small_sems,
+    )
+    chunk = min(CHUNK, cols)
+    spans = [slice(at, at + chunk) for at in range(0, cols, chunk)]
+    arriving = start_copies(
+        [frames_hbm.at[:, :, span] for span in spans],
+        [frames_ref.at[:, :, span] for span in spans],
+        frame_sems,
+    )
 
     rowpos = (
         lax.broadcasted_iota(jnp.int32, (steps, rows), 0) * rows
@@ -163,17 +149,150 @@
         low_ref[:, step * rows : (step + 1) * rows] = (pairs - high.astype(jnp.float32)).astype(
             jnp.bfloat16
         )
+    here = (first + lax.broadcasted_iota(jnp.int32, (1, rows), 1)).astype(jnp.float32)
+    stack = stacked_legendre(here, total_rows)
+    row = lax.broadcasted_iota(jnp.int32, (KROWS, rows), 0)
+    table_ref[:, 0:rows] = jnp.where(row < K, stack, 0.0)
+    table_ref[:, rows : 2 * rows] = jnp.where((row >= K) & (row < 2 * K), stack, 0.0)
+
+    for copy in small:
+        copy.wait()
+    amp = amp_ref[...]
+    lit = lit_by_lamp(start_ref[...], first, rows)
+    lit_ref[...] = lit_columns(lit)
+    which = which_ref[...]
+    bundles = bundle_ref[...]
+    base = jnp.zeros((1, fibers), jnp.float32)
+    for bundle in range(bundles.shape[1]):
+        base = jnp.where(which == bundle, bundles[:, bundle : bundle + 1], base)
+    inverse = 1.0 / base
+    base_ref[...] = inverse
+    lane = lax.broadcasted_iota(jnp.int32, (1, fibers), 1)
+    for fiber in range(owned):
+        own = jnp.sum(jnp.where(lane == me * owned + fiber, inverse, 0.0), axis=1, keepdims=True)
+        own_base_ref[fiber : fiber + 1, :] = jnp.broadcast_to(own, (1, rows))
 
     square_ref[...] = jnp.zeros_like(square_ref)
     square_ref[0:owned, 0:K] = trace_ref[...]
     square_ref[0:owned, K : 2 * K] = width_ref[...]
     coef_ref[...] = square_ref[...].T[0:KROWS]
+
+    square = lax.dot_general(
+        amp * amp, lit, (((0,), (0,)), ((), ())), precision=HIGH, preferred_element_type=jnp.float32
+    )
+    wide = owned * PIX
+
+    def place(block, at, even_value, odd_value):
+        keep_ref[block, at, :] = jnp.where(odd, odd_value, even_value)
+        send_ref[block, at, :] = jnp.where(odd, even_value, odd_value)
+
+    for block in range(fibers // (2 * owned)):
+        low = 2 * block * owned
+        place(
+            block,
+            slice(wide, wide + owned),
+            square[low : low + owned],
+            square[low + owned : low + 2 * owned],
+        )
+    for tile in range(cols // LANE):
+        if (tile * LANE) % chunk == 0:
+            arriving[tile * LANE // chunk].wait()
+        amp_cols = per_column(amp, tile)
+        total = jnp.zeros((rows, LANE), jnp.float32)
+        for lamp in range(lamps):
+            frame = frames_ref[lamp, :, tile * LANE : (tile + 1) * LANE].astype(jnp.float32)
+            weight = lit_ref[:, lamp * LANE : (lamp + 1) * LANE] * amp_cols[lamp : lamp + 1]
+            total = total + weight * frame
+        flipped = total.T
+        for pair in range(LANE // (2 * wide)):
+            low = 2 * pair * wide
+            place(
+                tile * (LANE // (2 * wide)) + pair,
+                slice(0, wide),
+                flipped[low : low + wide],
+                flipped[low + wide : low + 2 * wide],
+            )
+
+
+def collapse(
+    frames, amplitude, line_start, bundle_width, fiber_bundle, trace_coef, width_coef, height
+):
+    lamps, rows, cols = frames.shape
+    owned = trace_coef.shape[0]
+    steps = lax.axis_size("rows")
+    blocks = steps * lax.axis_size("fib") // 2
+    args = (
+        frames,
+        amplitude,
+        line_start,
+        bundle_width.reshape(1, -1),
+        fiber_bundle.reshape(1, -1),
+        trace_coef,
+        width_coef,
+    )
+    shape = jax.ShapeDtypeStruct
+    outs = (
+        shape((blocks, height, rows), jnp.float32),
+        shape((blocks, height, rows), jnp.float32),
+        shape((rows, lamps * LANE), jnp.float32),
+        shape((KROWS, 2 * rows), jnp.float32),
+        shape((1, fiber_bundle.shape[0]), jnp.float32),
+        shape((owned, rows), jnp.float32),
+        shape((KROWS, LANE), jnp.float32),
+        shape((KROWS * steps, rows), jnp.float32),
+        shape((K * KROWS, steps * rows), jnp.bfloat16),
+        shape((K * KROWS, steps * rows), jnp.bfloat16),
+    )
+    return pl.pallas_call(
+        collapse_kernel,
+        out_shape=outs,
+        in_specs=[pl.BlockSpec(memory_space=pltpu.HBM)] * len(args),
+        out_specs=[pl.BlockSpec(memory_space=pltpu.VMEM)] * len(outs),
+        scratch_shapes=[pltpu.VMEM(arg.shape, arg.dtype) for arg in args]
+        + [
+            pltpu.VMEM((LANE, LANE), jnp.float32),
+            pltpu.SemaphoreType.DMA((len(args) - 1,)),
+            pltpu.SemaphoreType.DMA((cols // min(CHUNK, cols),)),
+        ],
+        compiler_params=pltpu.CompilerParams(vmem_limit_bytes=VMEM_BYTES),
+        name="collapse",
+    )(*args)
+
+
+def fit_kernel(
+    height,
+    sources,
+    owned,
+    got_ref,
+    start_ref,
+    base_ref,
+    poly_ref,
+    high_ref,
+    low_ref,
+    send_ref,
+    sum_ref,
+    weight_ref,
+    coef_ref,
+    splat_ref,
+    square_ref,
+):
+    wide = owned * PIX
+    steps = got_ref.shape[0] // (height * sources)
+    rows = got_ref.shape[1]
+    used = wide + owned
+
+    for group in range(steps // SUB):
+        for item in range(used):
+            value = None
+            for source in range(sources):
+                start = (group * SUB * sources + source) * height + item
+                part = got_ref[pl.ds(start, SUB, stride=sources * height), :]
+                value = part if value is None else value + part
+            sum_ref[item, group * SUB : (group + 1) * SUB, :] = value
+
+    coef_ref[...] = start_ref[...]
+    inverse_base = [base_ref[fiber : fiber + 1, :] for fiber in range(owned)]
     weight_ref[...] = jnp.zeros_like(weight_ref)
-
-    inverse_base = []
-    for fiber in range(owned):
-        base = bundle_ref[which_ref[me * owned + fiber]]
-        inverse_base.append(1.0 / jnp.full((1, rows), base, jnp.float32))
 
     def newton_step(index, carry):
         for fiber in range(owned):
@@ -262,33 +381,22 @@
     lane = lax.broadcasted_iota(jnp.int32, (KROWS, LANE), 1)
     square_ref[0:KROWS, :] = jnp.where(lane < owned, coef_ref[...], 0.0)
     result = square_ref[...].T[0:owned]
-    trace_out[...] = result[:, 0:K]
-    width_out[...] = result[:, K : 2 * K]
     for device in range(send_ref.shape[0]):
         send_ref[device] = result
 
 
-def fit(got, bundle_width, fiber_bundle, trace_coef, width_coef, devices, height, sources):
-    owned = trace_coef.shape[0]
-    rows = got.shape[1]
-    steps = devices // sources
+def fit(got, start, base, poly, high, low, devices, height, sources):
+    owned, rows = base.shape
+    steps = got.shape[0] // (height * sources)
     count = -(-5 * owned // SUB) * SUB
     vmem = pl.BlockSpec(memory_space=pltpu.VMEM)
-    smem = pl.BlockSpec(memory_space=pltpu.SMEM)
     return pl.pallas_call(
-        functools.partial(fit_kernel, height, sources),
-        out_shape=(
-            jax.ShapeDtypeStruct((owned, K), jnp.float32),
-            jax.ShapeDtypeStruct((owned, K), jnp.float32),
-            jax.ShapeDtypeStruct((devices, owned, LANE), jnp.float32),
-        ),
-        in_specs=[smem, smem, vmem, vmem, vmem],
-        out_specs=(vmem, vmem, vmem),
+        functools.partial(fit_kernel, height, sources, owned),
+        out_shape=jax.ShapeDtypeStruct((devices, owned, LANE), jnp.float32),
+        in_specs=[vmem] * 6,
+        out_specs=vmem,
         scratch_shapes=[
             pltpu.VMEM((owned * PIX + owned, steps, rows), jnp.float32),
-            pltpu.VMEM((KROWS * steps, rows), jnp.float32),
-            pltpu.VMEM((K * KROWS, steps * rows), jnp.bfloat16),
-            pltpu.VMEM((K * KROWS, steps * rows), jnp.bfloat16),
             pltpu.VMEM((count * steps, rows), jnp.float32),
             pltpu.VMEM((KROWS, LANE), jnp.float32),
             pltpu.VMEM((owned, KROWS, rows), jnp.float32),
@@ -296,37 +404,47 @@
         ],
         compiler_params=pltpu.CompilerParams(vmem_limit_bytes=VMEM_BYTES),
         name="fit",
-    )(bundle_width, fiber_bundle, got, trace_coef, width_coef)
+    )(got, start, base, poly, high, low)
 
 
 def residual_kernel(
-    bundle_ref, which_ref, coef_ref, frames_ref, amp_ref, start_ref, out_ref, lit_ref
+    owned,
+    coef_ref,
+    table_ref,
+    base_ref,
+    lit_ref,
+    amp_ref,
+    frames_ref,
+    trace_hbm,
+    width_hbm,
+    image_hbm,
+    trace_ref,
+    width_ref,
+    image_ref,
+    small_sems,
+    image_sems,
 ):
     lamps, rows, cols = frames_ref.shape
-    total_rows = rows * lax.axis_size("rows")
-    fibers = coef_ref.shape[0]
-    first = lax.axis_index("rows") * rows
-    lit_ref[...] = lit_columns(lit_by_lamp(start_ref[...], first, rows))
-    which = which_ref[...]
-    base = jnp.zeros((1, fibers), jnp.float32)
-    for bundle in range(bundle_ref.shape[0]):
-        base = jnp.where(which == bundle, bundle_ref[bundle], base)
-
-    rowpos = (first + lax.broadcasted_iota(jnp.int32, (1, rows), 1)).astype(jnp.float32)
-    stack = stacked_legendre(rowpos, total_rows)
-    row = lax.broadcasted_iota(jnp.int32, (KROWS, rows), 0)
-    tables = jnp.concatenate(
-        [jnp.where(row < K, stack, 0.0), jnp.where((row >= K) & (row < 2 * K), stack, 0.0)], axis=1
-    )
+    me = lax.axis_index("rows") * lax.axis_size("fib") + lax.axis_index("fib")
+    own = coef_ref[pl.ds(me * owned, owned), :]
+    trace_ref[...] = own[:, 0:K]
+    width_ref[...] = own[:, K : 2 * K]
+    leaving = start_copies([trace_ref, width_ref], [trace_hbm, width_hbm], small_sems)
+
     coef = coef_ref[...].T[0:KROWS]
     curves = lax.dot_general(
-        tables, coef, (((0,), (0,)), ((), ())), precision=HIGH, preferred_element_type=jnp.float32
+        table_ref[...],
+        coef,
+        (((0,), (0,)), ((), ())),
+        precision=HIGH,
+        preferred_element_type=jnp.float32,
     )
     centre = curves[0:rows]
-    inverse = jnp.exp(-curves[rows : 2 * rows]) * (1.0 / base)
+    inverse = jnp.exp(-curves[rows : 2 * rows]) * base_ref[...]
     amp = amp_ref[...]
     pixel = (lax.broadcasted_iota(jnp.int32, (rows, LANE), 1) % PIX).astype(jnp.float32)
     offset = pixel - (PIX - 1) / 2.0
+    chunk = min(CHUNK, cols)
     for tile in range(cols // LANE):
         here = slice(tile * LANE, (tile + 1) * LANE)
         scaled = (offset - per_column(centre, tile)) * per_column(inverse, tile)
@@ -335,22 +453,40 @@
         for lamp in range(lamps):
             weight = lit_ref[:, lamp * LANE : (lamp + 1) * LANE] * amp_cols[lamp : lamp + 1]
             frame = frames_ref[lamp, :, here].astype(jnp.float32)
-            out_ref[lamp, :, here] = (frame - weight * shape).astype(jnp.bfloat16)
-
-
-def residual(bundle_width, fiber_bundle, coef, frames, amplitude, line_start):
-    lamps, rows, cols = frames.shape
+            image_ref[lamp, :, here] = (frame - weight * shape).astype(jnp.bfloat16)
+        if ((tile + 1) * LANE) % chunk == 0:
+            span = slice((tile + 1) * LANE - chunk, (tile + 1) * LANE)
+            copy = pltpu.make_async_copy(
+                image_ref.at[:, :, span],
+                image_hbm.at[:, :, span],
+                image_sems.at[tile * LANE // chunk],
+            )
+            copy.start()
+            leaving.append(copy)
+    for copy in leaving:
+        copy.wait()
+
+
+def residual(owned, coef, table, base, lit, amplitude, frames):
+    cols = frames.shape[2]
     vmem = pl.BlockSpec(memory_space=pltpu.VMEM)
-    smem = pl.BlockSpec(memory_space=pltpu.SMEM)
+    hbm = pl.BlockSpec(memory_space=pltpu.HBM)
+    fitted = jax.ShapeDtypeStruct((owned, K), jnp.float32)
     return pl.pallas_call(
-        residual_kernel,
-        out_shape=jax.ShapeDtypeStruct(frames.shape, jnp.bfloat16),
-        in_specs=[smem, vmem, vmem, vmem, vmem, vmem],
-        out_specs=vmem,
-        scratch_shapes=[pltpu.VMEM((rows, lamps * LANE), jnp.float32)],
+        functools.partial(residual_kernel, owned),
+        out_shape=(fitted, fitted, jax.ShapeDtypeStruct(frames.shape, jnp.bfloat16)),
+        in_specs=[vmem] * 6,
+        out_specs=[hbm] * 3,
+        scratch_shapes=[
+            pltpu.VMEM((owned, K), jnp.float32),
+            pltpu.VMEM((owned, K), jnp.float32),
+            pltpu.VMEM(frames.shape, jnp.bfloat16),
+            pltpu.SemaphoreType.DMA((2,)),
+            pltpu.SemaphoreType.DMA((cols // min(CHUNK, cols),)),
+        ],
         compiler_params=pltpu.CompilerParams(vmem_limit_bytes=VMEM_BYTES),
         name="residual",
-    )(bundle_width, fiber_bundle.reshape(1, -1), coef, frames, amplitude, line_start)
+    )(coef, table, base, lit, amplitude, frames)
 
 
 def body(frames, amplitude, line_start, bundle_width, fiber_bundle, trace_coef, width_coef):
@@ -359,14 +495,16 @@
     rows = frames.shape[1]
     owned = trace_coef.shape[0]
     height = -(-(owned * PIX + owned) // SUB) * SUB
-    partial = collapse(frames, amplitude, line_start, owned, height, devices)
-    got = lax.all_to_all(partial, BOTH, 0, 0, tiled=True).reshape(devices * height, rows)
-    trace_fit, width_fit, send = fit(
-        got, bundle_width, fiber_bundle, trace_coef, width_coef, devices, height, sources
-    )
-    coef = lax.all_to_all(send, BOTH, 0, 0, tiled=True).reshape(devices * owned, LANE)
-    image = residual(bundle_width, fiber_bundle, coef, frames, amplitude, line_start)
-    return (trace_fit, width_fit, image)
+    keep, send, lit, table, base, own_base, start, poly, high, low = collapse(
+        frames, amplitude, line_start, bundle_width, fiber_bundle, trace_coef, width_coef, height
+    )
+    came = lax.ppermute(send, "fib", [(index, index ^ 1) for index in range(sources)])
+    alike = [[index for index in range(devices) if index % 2 == odd] for odd in range(2)]
+    got = lax.all_to_all(keep + came, BOTH, 0, 0, axis_index_groups=alike, tiled=True)
+    got = got.reshape(devices // 2 * height, rows)
+    reply = fit(got, start, own_base, poly, high, low, devices, height, sources // 2)
+    coef = lax.all_to_all(reply, BOTH, 0, 0, tiled=True).reshape(devices * owned, LANE)
+    return residual(owned, coef, table, base, lit, amplitude, frames)
 
 
 def solution(mesh):

time: 48.4 us -> 45.3 us (0.936)
  blocking collectives: 35.7 us -> 29.5 us
  local copies, waits for them, and re-layouts: 2.71 us -> 5.37 us
  Pallas kernels: 9.05 us -> 7.63 us
  waiting for transfers between devices: 0 us -> 1.26 us
  starting transfers between devices: 0 us -> 0.56 us
    all_to_all x2, blocking collectives: 35.7 us -> 29.5 us  [the longest x1 19.8 us: body(): lax.all_to_all(keep + came, BOTH, 0, 0, axis_index_groups=alike, tiled=True)]
    unnamed x16 -> x18, local copies, waits for them, and re-layouts: 2.71 us -> 5.37 us
    pallas_call x3, Pallas kernels: 9.05 us -> 7.63 us  [the longest x1 3.53 us: fit(): pl.pallas_call(functools.partial(fit_kernel, height, sources, owned), out...]
    ppermute x0 -> x1, waiting for transfers between devices: none -> 1.26 us  [body(): lax.ppermute(send, 'fib', [(index, index ^ 1) for index in range(sources)])]
    ppermute x0 -> x1, starting transfers between devices: none -> 0.56 us  [body(): lax.ppermute(send, 'fib', [(index, index ^ 1) for index in range(sources)])]
  transfers between devices with their start and end apart: 0 -> 1, of which waited for: 0 -> 1; matrix products, arithmetic and copies ran while one was open for 0% -> 0% of each run, Pallas kernels for 0% -> 0%
where the time goes in v3:
time: 45.3 us; the launch traced here: 45 us
  blocking collectives  29.5 us (65%)
  Pallas kernels  7.63 us (17%)
  local copies, waits for them, and re-layouts  5.37 us (12%)
  waiting for transfers between devices  1.26 us (3%)
  between operations  0.68 us (2%)
  starting transfers between devices  0.56 us (1%)
    all_to_all x1, blocking collectives, body(): lax.all_to_all(keep + came, BOTH, 0, 0, axis_index_groups=alike, tiled=True)  19.8 us
    all_to_all x1, blocking collectives, body(): lax.all_to_all(reply, BOTH, 0, 0, tiled=True).reshape(devices * owned, LANE)  9.69 us
    unnamed x18, local copies, waits for them, and re-layouts  5.37 us
    pallas_call x1, Pallas kernels, fit(): pl.pallas_call(functools.partial(fit_kernel, height, sources, owned), out...  3.53 us
    pallas_call x1, Pallas kernels, residual(): pl.pallas_call(functools.partial(residual_kernel, owned), out_shape=(fitt...  2.13 us
    pallas_call x1, Pallas kernels, collapse(): pl.pallas_call(collapse_kernel, out_shape=outs, in_specs=[pl.BlockSpec(me...  1.97 us
    ppermute x1, waiting for transfers between devices, body(): lax.ppermute(send, 'fib', [(index, index ^ 1) for index in range(sources)])  1.26 us
  transfers between devices with their start and end apart: 1, of which 1 were waited for; matrix products, arithmetic and copies ran while one was open for 0% of the time, Pallas kernels for 0%

profile of v3, /device:TPU:0, one launch (start us, length us, event | category | flops | bytes accessed | tf_op | source)
XLA Modules:
  0.0 45.0 jit_solution(2754568306158158501)
XLA Ops:
  0.6 0.0 copy-start
  0.6 1.3 %copy-done = bf16[5,128,1024]{2,1,0:T(8,128)(2,1)S(1)} copy-done((bf16[5,128,1024]{2,1,0:T(8,128)(2,1)S(1)}, bf16[5,128,1024]{2,1,0:T(8,128)(2,1)}, u32[]{:S(2)}) %copy-start) | copy-done | bytes 1310744
  2.0 0.0 copy-start.2
  2.0 0.7 %copy-done.2 = f32[5,128]{1,0:T(8,128)S(1)} copy-done((f32[5,128]{1,0:T(8,128)S(1)}, f32[5,128]{1,0:T(8,128)}, u32[]{:S(2)}) %copy-start.2) | copy-done | bytes 2584
  2.6 0.0 copy-start.4
  2.6 0.7 %copy-done.4 = s32[5,24]{1,0:T(8,128)S(1)} copy-done((s32[5,24]{1,0:T(8,128)S(1)}, s32[5,24]{1,0:T(8,128)}, u32[]{:S(2)}) %copy-start.4) | copy-done | bytes 504
  3.3 0.0 copy-start.5
  3.3 0.7 %copy-done.5 = f32[4,11]{1,0:T(4,128)S(1)} copy-done((f32[4,11]{1,0:T(4,128)S(1)}, f32[4,11]{1,0:T(4,128)}, u32[]{:S(2)}) %copy-start.5) | copy-done | bytes 200
  4.0 0.0 copy-start.6
  4.0 0.7 %copy-done.6 = f32[4,11]{1,0:T(4,128)S(1)} copy-done((f32[4,11]{1,0:T(4,128)S(1)}, f32[4,11]{1,0:T(4,128)}, u32[]{:S(2)}) %copy-start.6) | copy-done | bytes 200
  4.7 0.0 copy-start.7
  4.7 0.7 %copy-done.7 = f32[20]{0:T(128)S(1)} copy-done((f32[20]{0:T(128)S(1)}, f32[20]{0:T(128)}, u32[]{:S(2)}) %copy-start.7) | copy-done | bytes 104
  5.3 0.7 %copy-done.8 = s32[128]{0:T(128)S(1)} copy-done((s32[128]{0:T(128)S(1)}, s32[128]{0:T(128)}, u32[]{:S(2)}) %copy-start.8) | copy-done | bytes 536
  6.0 2.0 %collapse.1 = (f32[16,40,128]{2,1,0:T(8,128)S(1)}, f32[16,40,128]{2,1,0:T(8,128)S(1)}, f32[128,640]{1,0:T(8,128)S(1)}, f32[24,256]{1,0:T(8,128)S(1)}, f32[1,128]...) custom-call(bf16[5,128,1024]{2,1,0:T(8,128)(2,1)S(1)} %copy-done, ...), custom_call_target="tpu_custom_call" | custom-call | tf_op jit(solution)/shard_map/collapse/pallas_call | solution.py:246
  8.0 0.6 %collective-permute-start = (f32[16,40,128]{2,1,0:T(8,128)S(1)}, f32[16,40,128]{2,1,0:T(8,128)S(1)}, u32[]{:S(2)}, u32[]{:S(2)}) collective-permute-start(f32[16,40,128]{2,1,0:T(8,128)S(1)} %get-tuple-element.14), channel_id=1, source_target_pairs={{0,1},{1,0},{2,3},{3,2},{4,5},{5,4},{6,7},{7,6},{8,9},{9,8},{10,11... | collective-permute-start | bytes 983048 | tf_op jit(solution)/shard_map/ppermute | solution.py:501
  8.5 1.3 %collective-permute-done = f32[16,40,128]{2,1,0:T(8,128)S(1)} collective-permute-done((f32[16,40,128]{2,1,0:T(8,128)S(1)}, f32[16,40,128]{2,1,0:T(8,128)S(1)}, u32[]{:S(2)}, u32[]{:S(2)}) %collective-permute-start) | collective-permute-done | bytes 327712 | tf_op jit(solution)/shard_map/ppermute | solution.py:501
  9.8 0.0 copy-start.1
  9.8 0.0 copy-start.3
  9.9 19.8 %all_to_all.10 = f32[16,40,128]{2,1,0:T(8,128)S(1)} all-to-all(f32[16,40,128]{2,1,0:T(8,128)S(1)} %add.3), channel_id=1, replica_groups={{0,2,4,6,8,10,12,14,16,18,20,22,24,26,28,30},{1,3,5,7,9,11,13,15,17,19,..., dimensions={0} | all-to-all | bytes 655360 | tf_op jit(solution)/shard_map/all_to_all | solution.py:503
  29.6 3.5 %fit.1 = f32[32,4,128]{2,1,0:T(4,128)S(1)} custom-call(f32[640,128]{1,0:T(8,128)S(1)} %bitcast.4, f32[24,128]{1,0:T(8,128)S(1)} %get-tuple-element.15.start_ref, f32[4,128]{1,0:T(4,128)S(1)} %get-tuple-element.16.base_ref, f32[192,128]{1,0:T(8,128)S(1)} %get-tuple-element.17.poly_ref, bf16[264,1024]{1,0:T(8,128)(2,1)S(1)} %get-tuple-element.18.high_ref, ...), custom_call_target="tpu_custom_call" | custom-call | tf_op jit(solution)/shard_map/fit/pallas_call | solution.py:393
  33.2 9.7 %all_to_all.11 = f32[32,4,128]{2,1,0:T(4,128)S(1)} all-to-all(f32[32,4,128]{2,1,0:T(4,128)S(1)} %fit.1), channel_id=1, replica_groups=mesh['rows'=8,'fib'=4] {'rows','fib'}, dimensions={0} | all-to-all | bytes 131072 | tf_op jit(solution)/shard_map/all_to_all | solution.py:506
  42.9 0.0 copy-done.1
  42.9 0.0 copy-done.3
  42.9 2.1 %residual.1 = (f32[4,11]{1,0:T(4,128)}, f32[4,11]{1,0:T(4,128)}, bf16[5,128,1024]{2,1,0:T(8,128)(2,1)}) custom-call(f32[128,128]{1,0:T(8,128)S(1)} %bitcast.5, f32[24,256]{1,0:T(8,128)S(1)} %get-tuple-element.20.table_ref, f32[1,128]{1,0:T(1,128)S(1)} %get-tuple-element.21.base_ref, f32[128,640]{1,0:T(8,128)S(1)} %get-tuple-element.22.lit_ref, ...), custom_call_target="tpu_custom_call" | custom-call | tf_op jit(solution)/shard_map/residual/pallas_call | solution.py:475
  (2 shorter events, 0.0 us)
Async XLA Ops:
  0.6 1.3 %copy-start = (bf16[5,128,1024]{2,1,0:T(8,128)(2,1)S(1)}, bf16[5,128,1024]{2,1,0:T(8,128)(2,1)}, u32[]{:S(2)}) copy-start(bf16[5,128,1024]{2,1,0:T(8,128)(2,1)} %frames_ref.1) | copy-start | bytes 3932164
  2.0 0.7 %copy-start.2 = (f32[5,128]{1,0:T(8,128)S(1)}, f32[5,128]{1,0:T(8,128)}, u32[]{:S(2)}) copy-start(f32[5,128]{1,0:T(8,128)} %amp_ref.1) | copy-start | bytes 7684
  2.6 0.7 %copy-start.4 = (s32[5,24]{1,0:T(8,128)S(1)}, s32[5,24]{1,0:T(8,128)}, u32[]{:S(2)}) copy-start(s32[5,24]{1,0:T(8,128)} %start_hbm.1) | copy-start | bytes 1444
  3.3 0.7 %copy-start.5 = (f32[4,11]{1,0:T(4,128)S(1)}, f32[4,11]{1,0:T(4,128)}, u32[]{:S(2)}) copy-start(f32[4,11]{1,0:T(4,128)} %trace_hbm.1) | copy-start | bytes 532
  4.0 0.7 %copy-start.6 = (f32[4,11]{1,0:T(4,128)S(1)}, f32[4,11]{1,0:T(4,128)}, u32[]{:S(2)}) copy-start(f32[4,11]{1,0:T(4,128)} %width_hbm.1) | copy-start | bytes 532
  4.7 0.7 %copy-start.7 = (f32[20]{0:T(128)S(1)}, f32[20]{0:T(128)}, u32[]{:S(2)}) copy-start(f32[20]{0:T(128)} %param.10) | copy-start | bytes 244
  5.3 0.7 %copy-start.8 = (s32[128]{0:T(128)S(1)}, s32[128]{0:T(128)}, u32[]{:S(2)}) copy-start(s32[128]{0:T(128)} %param.11) | copy-start | bytes 1540
  8.0 1.8 %collective-permute-start = (f32[16,40,128]{2,1,0:T(8,128)S(1)}, f32[16,40,128]{2,1,0:T(8,128)S(1)}, u32[]{:S(2)}, u32[]{:S(2)}) collective-permute-start(f32[16,40,128]{2,1,0:T(8,128)S(1)} %get-tuple-element.14), channel_id=1, source_target_pairs={{0,1},{1,0},{2,3},{3,2},{4,5},{5,4},{6,7},{7,6},{8,9},{9,8},{10,11... | collective-permute-start | bytes 983048 | tf_op jit(solution)/shard_map/ppermute | solution.py:501
  9.8 33.0 %copy-start.1 = (bf16[5,128,1024]{2,1,0:T(8,128)(2,1)S(1)}, bf16[5,128,1024]{2,1,0:T(8,128)(2,1)}, u32[]{:S(2)}) copy-start(bf16[5,128,1024]{2,1,0:T(8,128)(2,1)} %frames_ref.1) | copy-start | bytes 3932164
  9.8 33.0 %copy-start.3 = (f32[5,128]{1,0:T(8,128)S(1)}, f32[5,128]{1,0:T(8,128)}, u32[]{:S(2)}) copy-start(f32[5,128]{1,0:T(8,128)} %amp_ref.1) | copy-start | bytes 7684

commit v4 on v3

--- a/solution.py
+++ b/solution.py
@@ -256,7 +256,7 @@
         ],
         compiler_params=pltpu.CompilerParams(vmem_limit_bytes=VMEM_BYTES),
         name="collapse",
-    )(*args)
+    )(*[pltpu.with_memory_space_constraint(arg, pltpu.HBM) for arg in args])
 
 
 def fit_kernel(

time: 45.3 us -> 40.3 us (0.89)
  local copies, waits for them, and re-layouts: 5.37 us -> 0.01 us
  Pallas kernels: 7.63 us -> 8.09 us
    unnamed x18 -> x4, local copies, waits for them, and re-layouts: 5.37 us -> 0.01 us
    pallas_call x1, Pallas kernels: 1.97 us -> 2.44 us  [collapse(): pl.pallas_call(collapse_kernel, out_shape=outs, in_specs=[pl.BlockSpec(me...]
where the time goes in v4:
time: 40.3 us; the launch traced here: 40.1 us
  blocking collectives  29.5 us (73%)
  Pallas kernels  8.09 us (20%)
  waiting for transfers between devices  1.26 us (3%)
  between operations  0.66 us (2%)
  starting transfers between devices  0.56 us (1%)
    all_to_all x1, blocking collectives, body(): lax.all_to_all(keep + came, BOTH, 0, 0, axis_index_groups=alike, tiled=True)  19.8 us
    all_to_all x1, blocking collectives, body(): lax.all_to_all(reply, BOTH, 0, 0, tiled=True).reshape(devices * owned, LANE)  9.69 us
    pallas_call x1, Pallas kernels, fit(): pl.pallas_call(functools.partial(fit_kernel, height, sources, owned), out...  3.52 us
    pallas_call x1, Pallas kernels, collapse(): pl.pallas_call(collapse_kernel, out_shape=outs, in_specs=[pl.BlockSpec(me...  2.44 us
    pallas_call x1, Pallas kernels, residual(): pl.pallas_call(functools.partial(residual_kernel, owned), out_shape=(fitt...  2.13 us
    ppermute x1, waiting for transfers between devices, body(): lax.ppermute(send, 'fib', [(index, index ^ 1) for index in range(sources)])  1.26 us
  transfers between devices with their start and end apart: 1, of which 1 were waited for; matrix products, arithmetic and copies ran while one was open for 0% of the time, Pallas kernels for 0%

profile of v4, /device:TPU:0, one launch (start us, length us, event | category | flops | bytes accessed | tf_op | source)
XLA Modules:
  0.0 40.1 jit_solution(10006240560563244898)
XLA Ops:
  0.6 2.4 %collapse.1 = (f32[16,40,128]{2,1,0:T(8,128)S(1)}, f32[16,40,128]{2,1,0:T(8,128)S(1)}, f32[128,640]{1,0:T(8,128)S(1)}, f32[24,256]{1,0:T(8,128)S(1)}, f32[1,128]...) custom-call(bf16[5,128,1024]{2,1,0:T(8,128)(2,1)} %frames_ref.1, ...), custom_call_target="tpu_custom_call" | custom-call | tf_op jit(solution)/shard_map/collapse/pallas_call | solution.py:246
  3.1 0.6 %collective-permute-start = (f32[16,40,128]{2,1,0:T(8,128)S(1)}, f32[16,40,128]{2,1,0:T(8,128)S(1)}, u32[]{:S(2)}, u32[]{:S(2)}) collective-permute-start(f32[16,40,128]{2,1,0:T(8,128)S(1)} %get-tuple-element.14), channel_id=1, source_target_pairs={{0,1},{1,0},{2,3},{3,2},{4,5},{5,4},{6,7},{7,6},{8,9},{9,8},{10,11... | collective-permute-start | bytes 983048 | tf_op jit(solution)/shard_map/ppermute | solution.py:501
  3.6 1.3 %collective-permute-done = f32[16,40,128]{2,1,0:T(8,128)S(1)} collective-permute-done((f32[16,40,128]{2,1,0:T(8,128)S(1)}, f32[16,40,128]{2,1,0:T(8,128)S(1)}, u32[]{:S(2)}, u32[]{:S(2)}) %collective-permute-start) | collective-permute-done | bytes 327712 | tf_op jit(solution)/shard_map/ppermute | solution.py:501
  4.9 0.0 copy-start
  4.9 0.0 copy-start.1
  5.0 19.8 %all_to_all.10 = f32[16,40,128]{2,1,0:T(8,128)S(1)} all-to-all(f32[16,40,128]{2,1,0:T(8,128)S(1)} %add.3), channel_id=1, replica_groups={{0,2,4,6,8,10,12,14,16,18,20,22,24,26,28,30},{1,3,5,7,9,11,13,15,17,19,..., dimensions={0} | all-to-all | bytes 655360 | tf_op jit(solution)/shard_map/all_to_all | solution.py:503
  24.7 3.5 %fit.1 = f32[32,4,128]{2,1,0:T(4,128)S(1)} custom-call(f32[640,128]{1,0:T(8,128)S(1)} %bitcast.4, f32[24,128]{1,0:T(8,128)S(1)} %get-tuple-element.15.start_ref, f32[4,128]{1,0:T(4,128)S(1)} %get-tuple-element.16.base_ref, f32[192,128]{1,0:T(8,128)S(1)} %get-tuple-element.17.poly_ref, bf16[264,1024]{1,0:T(8,128)(2,1)S(1)} %get-tuple-element.18.high_ref, ...), custom_call_target="tpu_custom_call" | custom-call | tf_op jit(solution)/shard_map/fit/pallas_call | solution.py:393
  28.2 9.7 %all_to_all.11 = f32[32,4,128]{2,1,0:T(4,128)S(1)} all-to-all(f32[32,4,128]{2,1,0:T(4,128)S(1)} %fit.1), channel_id=1, replica_groups=mesh['rows'=8,'fib'=4] {'rows','fib'}, dimensions={0} | all-to-all | bytes 131072 | tf_op jit(solution)/shard_map/all_to_all | solution.py:506
  37.9 0.0 copy-done
  37.9 0.0 copy-done.1
  37.9 2.1 %residual.1 = (f32[4,11]{1,0:T(4,128)}, f32[4,11]{1,0:T(4,128)}, bf16[5,128,1024]{2,1,0:T(8,128)(2,1)}) custom-call(f32[128,128]{1,0:T(8,128)S(1)} %bitcast.5, f32[24,256]{1,0:T(8,128)S(1)} %get-tuple-element.20.table_ref, f32[1,128]{1,0:T(1,128)S(1)} %get-tuple-element.21.base_ref, f32[128,640]{1,0:T(8,128)S(1)} %get-tuple-element.22.lit_ref, ...), custom_call_target="tpu_custom_call" | custom-call | tf_op jit(solution)/shard_map/residual/pallas_call | solution.py:475
  (1 shorter events, 0.0 us)
Async XLA Ops:
  3.1 1.8 %collective-permute-start = (f32[16,40,128]{2,1,0:T(8,128)S(1)}, f32[16,40,128]{2,1,0:T(8,128)S(1)}, u32[]{:S(2)}, u32[]{:S(2)}) collective-permute-start(f32[16,40,128]{2,1,0:T(8,128)S(1)} %get-tuple-element.14), channel_id=1, source_target_pairs={{0,1},{1,0},{2,3},{3,2},{4,5},{5,4},{6,7},{7,6},{8,9},{9,8},{10,11... | collective-permute-start | bytes 983048 | tf_op jit(solution)/shard_map/ppermute | solution.py:501
  4.9 33.0 %copy-start = (bf16[5,128,1024]{2,1,0:T(8,128)(2,1)S(1)}, bf16[5,128,1024]{2,1,0:T(8,128)(2,1)}, u32[]{:S(2)}) copy-start(bf16[5,128,1024]{2,1,0:T(8,128)(2,1)} %frames_ref.1) | copy-start | bytes 3932164
  4.9 33.0 %copy-start.1 = (f32[5,128]{1,0:T(8,128)S(1)}, f32[5,128]{1,0:T(8,128)}, u32[]{:S(2)}) copy-start(f32[5,128]{1,0:T(8,128)} %amp_ref.1) | copy-start | bytes 7684

commit v5 on v4

v5 whole, which is shorter than its diff:
```python
import functools

import jax
import jax.numpy as jnp
import numpy as np
from jax import lax
from jax.experimental import pallas as pl
from jax.experimental.pallas import tpu as pltpu
from jax.sharding import PartitionSpec as P

K = 11
PIX = 8
WIN = 8
ITERS = 3
SUB = 8
LANE = 128
KROWS = 24
RHS = 2 * K
PARTS = 9 * KROWS + 8
VMEM_BYTES = 20 << 20

HIGH = lax.Precision.HIGHEST
BOTH = ("rows", "fib")


def adams_factor(order):
    value = 1.0
    for index in range(1, order + 1):
        value = value * (2.0 * index - 1.0) / index
    return value


def system_map():
    table = np.zeros((K * KROWS, 3 * KROWS))
    for i in range(K):
        table[i * KROWS + RHS, 2 * KROWS + i] = 1.0
        for j in range(K):
            for inner in range(min(i, j) + 1):
                target = i + j - 2 * inner
                value = adams_factor(inner) * adams_factor(i - inner) * adams_factor(j - inner)
                value = value / adams_factor(i + j - inner)
                value = value * (2.0 * target + 1.0) / (2.0 * (i + j - inner) + 1.0)
                table[i * KROWS + j, target] += value
                table[i * KROWS + K + j, KROWS + target] += value
    high = table.astype(jnp.bfloat16)
    low = (table - high.astype(np.float64)).astype(jnp.bfloat16)
    spare = np.zeros((K * KROWS, PARTS - 9 * KROWS), jnp.bfloat16)
    return np.concatenate([high, high, low, spare], axis=1)


def legendre_list(rowpos, total, count):
    tvals = (2.0 * rowpos + 1.0) / total - 1.0
    polys = [jnp.ones_like(tvals), tvals]
    for order in range(1, count - 1):
        polys.append(
            ((2 * order + 1) * tvals * polys[order] - order * polys[order - 1]) / (order + 1)
        )
    return polys


def stacked_legendre(rowpos, total):
    polys = legendre_list(rowpos, total, K)
    row = lax.broadcasted_iota(jnp.int32, (KROWS, rowpos.shape[1]), 0)
    table = jnp.zeros((KROWS, rowpos.shape[1]), jnp.float32)
    for order in range(K):
        table = jnp.where((row == order) | (row == K + order), polys[order], table)
    return jnp.where(row == RHS, 1.0, table)


def lit_by_lamp(start, first, rows):
    lamps, lines = start.shape
    rowid = first + lax.broadcasted_iota(jnp.int32, (lamps, rows), 1)
    lit = jnp.zeros((lamps, rows), jnp.float32)
    for line in range(lines):
        away = rowid - start[:, line : line + 1]
        lit = jnp.where((away >= 0) & (away < WIN), 1.0, lit)
    return lit


def lit_columns(lit):
    lamps, rows = lit.shape
    which = lax.broadcasted_iota(jnp.int32, (lamps, lamps * LANE), 1) // LANE
    own = lax.broadcasted_iota(jnp.int32, (lamps, lamps * LANE), 0)
    spread = jnp.where(which == own, 1.0, 0.0)
    return lax.dot_general(
        lit, spread, (((0,), (0,)), ((), ())), preferred_element_type=jnp.float32
    )


def take_lanes(values, index):
    parts = values.shape[1] // LANE
    result = None
    for part in range(parts):
        block = values[:, part * LANE : (part + 1) * LANE]
        taken = jnp.take_along_axis(block, index % LANE, axis=1, mode="promise_in_bounds")
        result = taken if result is None else jnp.where(index // LANE == part, taken, result)
    return result


def per_column(values, tile, owned, grouped):
    fiber = tile * (LANE // PIX) + (
        lax.broadcasted_iota(jnp.int32, (values.shape[0], LANE), 1) // PIX
    )
    if grouped:
        fiber = (fiber % owned) * (values.shape[1] // owned) + fiber // owned
    else:
        part = tile * (LANE // PIX) // LANE
        values = values[:, part * LANE : (part + 1) * LANE]
        fiber = fiber % LANE
    return take_lanes(values, fiber)


def start_copies(sources, targets, sems):
    copies = [
        pltpu.make_async_copy(source, target, sems.at[index])
        for index, (source, target) in enumerate(zip(sources, targets))
    ]
    for copy in copies:
        copy.start()
    return copies


def collapse_kernel(
    frames_hbm,
    amp_hbm,
    start_hbm,
    bundle_hbm,
    which_hbm,
    trace_hbm,
    width_hbm,
    keep_ref,
    send_ref,
    lit_ref,
    table_ref,
    coef_ref,
    poly_ref,
    split_ref,
    frames_ref,
    amp_ref,
    start_ref,
    bundle_ref,
    which_ref,
    trace_ref,
    width_ref,
    square_ref,
    small_sems,
    frame_sems,
):
    lamps, rows, cols = frames_ref.shape
    owned = trace_ref.shape[0]
    fibers = which_ref.shape[1]
    steps = lax.axis_size("rows")
    total_rows = steps * rows
    me = lax.axis_index("rows") * lax.axis_size("fib") + lax.axis_index("fib")
    first = lax.axis_index("rows") * rows
    odd = lax.axis_index("fib") % 2 == 1

    small = start_copies(
        [amp_hbm, start_hbm, bundle_hbm, which_hbm, trace_hbm, width_hbm],
        [amp_ref, start_ref, bundle_ref, which_ref, trace_ref, width_ref],
        small_sems,
    )
    arriving = start_copies([frames_hbm], [frames_ref], frame_sems)

    rowpos = (
        lax.broadcasted_iota(jnp.int32, (steps, rows), 0) * rows
        + lax.broadcasted_iota(jnp.int32, (steps, rows), 1)
    ).astype(jnp.float32)
    polys = legendre_list(rowpos, total_rows, 2 * K - 1)
    for order in range(KROWS):
        poly_ref[order * steps : (order + 1) * steps, :] = (
            polys[order] if order < 2 * K - 1 else jnp.zeros((steps, rows), jnp.float32)
        )
    for step in range(steps):
        stack = poly_ref[pl.ds(step, KROWS, stride=steps), :]
        high = stack.astype(jnp.bfloat16).astype(jnp.float32)
        split_ref[:, step * rows : (step + 1) * rows] = jnp.concatenate(
            [high, stack - high], axis=0
        ).astype(jnp.bfloat16)

    here = (first + lax.broadcasted_iota(jnp.int32, (1, rows), 1)).astype(jnp.float32)
    stack = stacked_legendre(here, total_rows)
    row = lax.broadcasted_iota(jnp.int32, (KROWS, rows), 0)
    table_ref[:, 0:rows] = jnp.where(row < K, stack, 0.0)
    table_ref[:, rows : 2 * rows] = jnp.where((row >= K) & (row < 2 * K), stack, 0.0)

    for copy in small:
        copy.wait()
    amp = amp_ref[...]
    lit = lit_by_lamp(start_ref[...], first, rows)
    lit_ref[...] = lit_columns(lit)
    which = which_ref[...]
    bundles = bundle_ref[...]
    base = jnp.zeros((1, fibers), jnp.float32)
    for bundle in range(bundles.shape[1]):
        base = jnp.where(which == bundle, bundles[:, bundle : bundle + 1], base)
    inverse = 1.0 / base
    lane = lax.broadcasted_iota(jnp.int32, (1, fibers), 1)

    square_ref[...] = jnp.zeros_like(square_ref)
    square_ref[0:owned, 0:K] = trace_ref[...]
    square_ref[0:owned, K : 2 * K] = width_ref[...]
    for fiber in range(owned):
        square_ref[fiber : fiber + 1, RHS : RHS + 1] = jnp.sum(
            jnp.where(lane == me * owned + fiber, inverse, 0.0), axis=1, keepdims=True
        )
    coef_ref[...] = square_ref[...].T[0:KROWS]

    square = lax.dot_general(
        amp * amp, lit, (((0,), (0,)), ((), ())), precision=HIGH, preferred_element_type=jnp.float32
    )
    wide = owned * PIX

    height = wide + owned

    def place(block, offset, even_value, odd_value):
        at = slice(block * height + offset, block * height + offset + even_value.shape[0])
        keep_ref[at, :] = jnp.where(odd, odd_value, even_value)
        send_ref[at, :] = jnp.where(odd, even_value, odd_value)

    for block in range(fibers // (2 * owned)):
        low = 2 * block * owned
        place(
            block,
            wide,
            square[low : low + owned],
            square[low + owned : low + 2 * owned],
        )
    for copy in arriving:
        copy.wait()
    for tile in range(cols // LANE):
        amp_cols = per_column(amp, tile, owned, False)
        total = jnp.zeros((rows, LANE), jnp.float32)
        for lamp in range(lamps):
            frame = frames_ref[lamp, :, tile * LANE : (tile + 1) * LANE].astype(jnp.float32)
            weight = lit_ref[:, lamp * LANE : (lamp + 1) * LANE] * amp_cols[lamp : lamp + 1]
            total = total + weight * frame
        flipped = total.T
        for pair in range(LANE // (2 * wide)):
            low = 2 * pair * wide
            place(
                tile * (LANE // (2 * wide)) + pair,
                0,
                flipped[low : low + wide],
                flipped[low + wide : low + 2 * wide],
            )


def collapse(
    frames, amplitude, line_start, bundle_width, fiber_bundle, trace_coef, width_coef, height
):
    lamps, rows, cols = frames.shape
    steps = lax.axis_size("rows")
    blocks = steps * lax.axis_size("fib") // 2
    args = (
        frames,
        amplitude,
        line_start,
        bundle_width.reshape(1, -1),
        fiber_bundle.reshape(1, -1),
        trace_coef,
        width_coef,
    )
    shape = jax.ShapeDtypeStruct
    outs = (
        shape((blocks * height, rows), jnp.float32),
        shape((blocks * height, rows), jnp.float32),
        shape((rows, lamps * LANE), jnp.float32),
        shape((KROWS, 2 * rows), jnp.float32),
        shape((KROWS, LANE), jnp.float32),
        shape((KROWS * steps, rows), jnp.float32),
        shape((2 * KROWS, steps * rows), jnp.bfloat16),
    )
    return pl.pallas_call(
        collapse_kernel,
        out_shape=outs,
        in_specs=[pl.BlockSpec(memory_space=pltpu.HBM)] * len(args),
        out_specs=[pl.BlockSpec(memory_space=pltpu.VMEM)] * len(outs),
        scratch_shapes=[pltpu.VMEM(arg.shape, arg.dtype) for arg in args]
        + [
            pltpu.VMEM((LANE, LANE), jnp.float32),
            pltpu.SemaphoreType.DMA((len(args) - 1,)),
            pltpu.SemaphoreType.DMA((1,)),
        ],
        compiler_params=pltpu.CompilerParams(vmem_limit_bytes=VMEM_BYTES),
        name="collapse",
    )(*[pltpu.with_memory_space_constraint(arg, pltpu.HBM) for arg in args])


def fit_kernel(
    height,
    sources,
    owned,
    got_ref,
    start_ref,
    poly_ref,
    split_ref,
    map_ref,
    send_ref,
    sum_ref,
    weight_ref,
    coef_ref,
    splat_ref,
    square_ref,
):
    wide = owned * PIX
    steps = got_ref.shape[0] // (height * sources)
    rows = got_ref.shape[1]
    used = wide + owned

    for group in range(steps // SUB):
        for item in range(used):
            value = None
            for source in range(sources):
                start = (group * SUB * sources + source) * height + item
                part = got_ref[pl.ds(start, SUB, stride=sources * height), :]
                value = part if value is None else value + part
            sum_ref[item, group * SUB : (group + 1) * SUB, :] = value

    coef_ref[...] = start_ref[...]
    weight_ref[...] = jnp.zeros_like(weight_ref)

    def newton_step(index, carry):
        for fiber in range(owned):
            splat_ref[fiber] = jnp.broadcast_to(
                coef_ref[:, fiber : fiber + 1], (KROWS, rows)
            )
        for group in range(steps // SUB):
            here = slice(group * SUB, (group + 1) * SUB)
            for fiber in range(owned):
                centre = jnp.zeros((SUB, rows), jnp.float32)
                spread = jnp.zeros((SUB, rows), jnp.float32)
                for order in range(K):
                    poly = poly_ref[order * steps + group * SUB : order * steps + (group + 1) * SUB, :]
                    centre = centre + splat_ref[fiber, order : order + 1, :] * poly
                    spread = spread + splat_ref[fiber, K + order : K + order + 1, :] * poly
                inverse = jnp.exp(-spread) * splat_ref[fiber, RHS : RHS + 1, :]
                power = sum_ref[wide + fiber, here, :]
                sums = [jnp.zeros((SUB, rows), jnp.float32) for _ in range(5)]
                for pixel in range(PIX):
                    scaled = ((pixel - (PIX - 1) / 2.0) - centre) * inverse
                    shape = jnp.exp(-0.5 * scaled * scaled)
                    bend = shape * scaled
                    slope = bend * inverse
                    widen = bend * scaled
                    resid = sum_ref[fiber * PIX + pixel, here, :] - power * shape
                    sums[0] = sums[0] + slope * slope
                    sums[1] = sums[1] + slope * widen
                    sums[2] = sums[2] + widen * widen
                    sums[3] = sums[3] + resid * slope
                    sums[4] = sums[4] + resid * widen
                for kind in range(5):
                    value = sums[kind] * power if kind < 3 else sums[kind]
                    at = (kind * owned + fiber) * steps + group * SUB
                    weight_ref[at : at + SUB, :] = value
        count = weight_ref.shape[0] // steps
        weights = jnp.concatenate(
            [weight_ref[pl.ds(step, count, stride=steps), :] for step in range(steps)], axis=1
        )
        upper = weights.astype(jnp.bfloat16).astype(jnp.float32)
        both = jnp.concatenate([upper, weights - upper], axis=0).astype(jnp.bfloat16)
        moments = lax.dot_general(
            split_ref[...], both, (((1,), (1,)), ((), ())), preferred_element_type=jnp.float32
        )
        moments = moments[0:KROWS] + moments[KROWS:]
        moments = jnp.concatenate(
            [moments, jnp.zeros((KROWS, LANE - 2 * count), jnp.float32)], axis=1
        )
        moments = moments + pltpu.roll(moments, LANE - count, 1)
        kinds = [moments] + [
            pltpu.roll(moments, LANE - kind * owned, 1) for kind in range(1, 5)
        ]
        stacked = jnp.concatenate(
            [
                jnp.concatenate([kinds[0], kinds[1], kinds[3]], axis=0),
                jnp.concatenate([kinds[1], kinds[2], kinds[4]], axis=0),
            ],
            axis=1,
        )
        high = stacked.astype(jnp.bfloat16).astype(jnp.float32)
        spare = jnp.zeros((PARTS - 9 * KROWS, 2 * LANE), jnp.float32)
        system = jnp.dot(
            map_ref[...],
            jnp.concatenate([high, stacked - high, high, spare], axis=0).astype(jnp.bfloat16),
            preferred_element_type=jnp.float32,
        )
        row = lax.broadcasted_iota(jnp.int32, (KROWS, LANE), 0)
        matrix = []
        for i in range(2 * K):
            second, at = divmod(i, K)
            value = system[at * KROWS : (at + 1) * KROWS, second * LANE : (second + 1) * LANE]
            matrix.append(jnp.where(row == i, 1.5 * value + 1.0, value))
        for pivot in range(2 * K):
            cut = KROWS - matrix[pivot].shape[0]
            inverse = 1.0 / matrix[pivot][pivot - cut : pivot - cut + 1]
            chosen = matrix[pivot] * inverse
            for i in range(2 * K):
                if i != pivot:
                    scale = matrix[i][pivot - cut : pivot - cut + 1]
                    matrix[i] = matrix[i] - scale * chosen
            matrix[pivot] = chosen
            if (pivot + 1) % SUB == 0:
                matrix = [item[SUB:] for item in matrix]
        for i in range(2 * K):
            cut = KROWS - matrix[i].shape[0]
            coef_ref[i : i + 1, :] = coef_ref[i : i + 1, :] + matrix[i][RHS - cut : RHS - cut + 1]
        return carry

    lax.fori_loop(0, ITERS, newton_step, 0)

    square_ref[...] = jnp.zeros_like(square_ref)
    lane = lax.broadcasted_iota(jnp.int32, (KROWS, LANE), 1)
    square_ref[0:KROWS, :] = jnp.where(lane < owned, coef_ref[...], 0.0)
    result = square_ref[...].T[0:owned]
    packed = result[0:1]
    for fiber in range(1, owned):
        packed = packed + pltpu.roll(result[fiber : fiber + 1], fiber * (LANE // owned), 1)
    send_ref[...] = jnp.broadcast_to(packed, send_ref.shape)


def fit(got, start, poly, split, owned, devices, height, sources):
    rows = got.shape[1]
    steps = got.shape[0] // (height * sources)
    count = -(-5 * owned // SUB) * SUB
    vmem = pl.BlockSpec(memory_space=pltpu.VMEM)
    return pl.pallas_call(
        functools.partial(fit_kernel, height, sources, owned),
        out_shape=jax.ShapeDtypeStruct((devices, LANE), jnp.float32),
        in_specs=[vmem] * 5,
        out_specs=vmem,
        scratch_shapes=[
            pltpu.VMEM((owned * PIX + owned, steps, rows), jnp.float32),
            pltpu.VMEM((count * steps, rows), jnp.float32),
            pltpu.VMEM((KROWS, LANE), jnp.float32),
            pltpu.VMEM((owned, KROWS, rows), jnp.float32),
            pltpu.VMEM((LANE, LANE), jnp.float32),
        ],
        compiler_params=pltpu.CompilerParams(vmem_limit_bytes=VMEM_BYTES),
        name="fit",
    )(got, start, poly, split, jnp.asarray(system_map()))


def residual_kernel(
    owned,
    coef_ref,
    table_ref,
    lit_ref,
    amp_ref,
    frames_ref,
    trace_hbm,
    width_hbm,
    image_hbm,
    trace_ref,
    width_ref,
    image_ref,
    shape_ref,
    bright_ref,
    small_sems,
    image_sems,
):
    lamps, rows, cols = frames_ref.shape
    me = lax.axis_index("rows") * lax.axis_size("fib") + lax.axis_index("fib")
    own = coef_ref[pl.ds(me, 1), :]
    each = LANE // owned
    for fiber in range(owned):
        at = fiber * each
        trace_ref[fiber : fiber + 1, :] = own[:, at : at + K]
        width_ref[fiber : fiber + 1, :] = own[:, at + K : at + 2 * K]
    leaving = start_copies([trace_ref, width_ref], [trace_hbm, width_hbm], small_sems)

    flipped = coef_ref[...].T
    coef = jnp.concatenate(
        [flipped[fiber * each : fiber * each + KROWS] for fiber in range(owned)], axis=1
    )
    curves = lax.dot_general(
        table_ref[...],
        coef,
        (((0,), (0,)), ((), ())),
        precision=HIGH,
        preferred_element_type=jnp.float32,
    )
    centre = curves[0:rows]
    inverse = jnp.exp(-curves[rows : 2 * rows]) * coef[RHS : RHS + 1]
    amp = amp_ref[...]
    pixel = (lax.broadcasted_iota(jnp.int32, (rows, LANE), 1) % PIX).astype(jnp.float32)
    offset = pixel - (PIX - 1) / 2.0
    for tile in range(cols // LANE):
        here = slice(tile * LANE, (tile + 1) * LANE)
        scaled = (offset - per_column(centre, tile, owned, True)) * per_column(
            inverse, tile, owned, True
        )
        shape_ref[:, here] = jnp.exp(-0.5 * scaled * scaled)
        bright = per_column(amp, tile, owned, False)
        for lamp in range(lamps):
            bright_ref[lamp, :, here] = bright[lamp : lamp + 1]

    def leave(lamp):
        return pltpu.make_async_copy(
            image_ref.at[lamp], image_hbm.at[lamp], image_sems.at[lamp]
        )

    def one_lamp(lamp, carry):
        lit = lit_ref[:, pl.ds(pl.multiple_of(lamp * LANE, LANE), LANE)]
        for tile in range(cols // LANE):
            here = slice(tile * LANE, (tile + 1) * LANE)
            weight = lit * bright_ref[lamp, :, here]
            frame = frames_ref[lamp, :, here].astype(jnp.float32)
            image_ref[lamp, :, here] = (frame - weight * shape_ref[:, here]).astype(jnp.bfloat16)
        leave(lamp).start()
        return carry

    lax.fori_loop(0, lamps, one_lamp, 0)
    for lamp in range(lamps):
        leave(lamp).wait()
    for copy in leaving:
        copy.wait()


def residual(owned, coef, table, lit, amplitude, frames):
    lamps, rows, cols = frames.shape
    vmem = pl.BlockSpec(memory_space=pltpu.VMEM)
    hbm = pl.BlockSpec(memory_space=pltpu.HBM)
    fitted = jax.ShapeDtypeStruct((owned, K), jnp.float32)
    return pl.pallas_call(
        functools.partial(residual_kernel, owned),
        out_shape=(fitted, fitted, jax.ShapeDtypeStruct(frames.shape, jnp.bfloat16)),
        in_specs=[vmem] * 5,
        out_specs=[hbm] * 3,
        scratch_shapes=[
            pltpu.VMEM((owned, K), jnp.float32),
            pltpu.VMEM((owned, K), jnp.float32),
            pltpu.VMEM(frames.shape, jnp.bfloat16),
            pltpu.VMEM((rows, cols), jnp.float32),
            pltpu.VMEM((lamps, 1, cols), jnp.float32),
            pltpu.SemaphoreType.DMA((2,)),
            pltpu.SemaphoreType.DMA((lamps,)),
        ],
        compiler_params=pltpu.CompilerParams(vmem_limit_bytes=VMEM_BYTES),
        name="residual",
    )(coef, table, lit, amplitude, frames)


def body(frames, amplitude, line_start, bundle_width, fiber_bundle, trace_coef, width_coef):
    sources = lax.axis_size("fib")
    devices = lax.axis_size("rows") * sources
    rows = frames.shape[1]
    owned = trace_coef.shape[0]
    height = owned * PIX + owned
    keep, send, lit, table, start, poly, split = collapse(
        frames, amplitude, line_start, bundle_width, fiber_bundle, trace_coef, width_coef, height
    )
    came = lax.ppermute(send, "fib", [(index, index ^ 1) for index in range(sources)])
    alike = [[index for index in range(devices) if index % 2 == odd] for odd in range(2)]
    unit = 4 if height % 4 == 0 else 1
    got = lax.all_to_all(
        (keep + came).reshape(devices // 2, height // unit, unit, rows),
        BOTH,
        0,
        0,
        axis_index_groups=alike,
        tiled=True,
    ).reshape(devices // 2 * height, rows)
    reply = fit(got, start, poly, split, owned, devices, height, sources // 2)
    coef = lax.all_to_all(reply, BOTH, 0, 0, tiled=True)
    return residual(owned, coef, table, lit, amplitude, frames)


def solution(mesh):
    return jax.shard_map(
        body,
        mesh=mesh,
        in_specs=(
            P("fib", "rows", None),
            P("fib", None),
            P("fib", None),
            P(),
            P(),
            P(BOTH, None),
            P(BOTH, None),
        ),
        out_specs=(P(BOTH, None), P(BOTH, None), P("fib", "rows", None)),
        check_vma=False,
    )
```

time: 40.3 us -> 38.8 us (0.963)
  blocking collectives: 29.5 us -> 28.4 us
  Pallas kernels: 8.09 us -> 7.65 us
    all_to_all x2, blocking collectives: 29.5 us -> 28.4 us  [the longest x1 19 us: body(): lax.all_to_all((keep + came).reshape(devices // 2, height // unit, unit,...]
    pallas_call x1, Pallas kernels: 2.44 us -> 2.02 us  [collapse(): pl.pallas_call(collapse_kernel, out_shape=outs, in_specs=[pl.BlockSpec(me...]
where the time goes in v5:
time: 38.8 us; the launch traced here: 38.6 us
  blocking collectives  28.4 us (73%)
  Pallas kernels  7.65 us (20%)
  waiting for transfers between devices  1.21 us (3%)
  between operations  0.67 us (2%)
  starting transfers between devices  0.56 us (1%)
    all_to_all x1, blocking collectives, body(): lax.all_to_all((keep + came).reshape(devices // 2, height // unit, unit,...  19 us
    all_to_all x1, blocking collectives, body(): coef = lax.all_to_all(reply, BOTH, 0, 0, tiled=True)  9.4 us
    pallas_call x1, Pallas kernels, fit(): pl.pallas_call(functools.partial(fit_kernel, height, sources, owned), out...  3.35 us
    pallas_call x1, Pallas kernels, residual(): pl.pallas_call(functools.partial(residual_kernel, owned), out_shape=(fitt...  2.29 us
    pallas_call x1, Pallas kernels, collapse(): pl.pallas_call(collapse_kernel, out_shape=outs, in_specs=[pl.BlockSpec(me...  2.02 us
    ppermute x1, waiting for transfers between devices, body(): lax.ppermute(send, 'fib', [(index, index ^ 1) for index in range(sources)])  1.21 us
  transfers between devices with their start and end apart: 1, of which 1 were waited for; matrix products, arithmetic and copies ran while one was open for 0% of the time, Pallas kernels for 0%

profile of v5, /device:TPU:0, one launch (start us, length us, event | category | flops | bytes accessed | tf_op | source)
XLA Modules:
  0.0 38.6 jit_solution(15278180069681474409)
XLA Ops:
  0.6 0.0 copy-start.1
  0.6 2.0 %collapse.1 = (f32[576,128]{1,0:T(8,128)S(1)}, f32[576,128]{1,0:T(8,128)S(1)}, f32[128,640]{1,0:T(8,128)S(1)}, f32[24,256]{1,0:T(8,128)S(1)}, f32[24,128]{1,0:T(...) custom-call(bf16[5,128,1024]{2,1,0:T(8,128)(2,1)} %frames_ref.1, f32[5,128]{1,0:T(8,128)} %amp_ref.1, ...), custom_call_target="tpu_custom_call" | custom-call | tf_op jit(solution)/shard_map/collapse/pallas_call | solution.py:274
  2.7 0.0 copy-start
  2.7 0.0 copy-start.2
  2.7 0.6 %collective-permute-start = (f32[576,128]{1,0:T(8,128)S(1)}, f32[576,128]{1,0:T(8,128)S(1)}, u32[]{:S(2)}, u32[]{:S(2)}) collective-permute-start(f32[576,128]{1,0:T(8,128)S(1)} %get-tuple-element.11), channel_id=1, source_target_pairs={{0,1},{1,0},{2,3},{3,2},{4,5},{5,4},{6,7},{7,6},{8,9},{9,8},{10,11... | collective-permute-start | bytes 884744 | tf_op jit(solution)/shard_map/ppermute | solution.py:552
  3.3 1.2 %collective-permute-done = f32[576,128]{1,0:T(8,128)S(1)} collective-permute-done((f32[576,128]{1,0:T(8,128)S(1)}, f32[576,128]{1,0:T(8,128)S(1)}, u32[]{:S(2)}, u32[]{:S(2)}) %collective-permute-start) | collective-permute-done | bytes 294944 | tf_op jit(solution)/shard_map/ppermute | solution.py:552
  4.5 19.0 %all_to_all.16 = f32[16,9,4,128]{3,2,1,0:T(4,128)S(1)} all-to-all(f32[16,9,4,128]{3,2,1,0:T(4,128)S(1)} %bitcast.11), channel_id=1, replica_groups={{0,2,4,6,8,10,12,14,16,18,20,22,24,26,28,30},{1,3,5,7,9,11,13,15,17,19,..., dimensions={0} | all-to-all | bytes 589824 | tf_op jit(solution)/shard_map/all_to_all | solution.py:555
  23.5 0.0 copy-done.1
  23.5 3.3 %fit.1 = f32[32,128]{1,0:T(8,128)S(1)} custom-call(f32[576,128]{1,0:T(8,128)S(1)} %bitcast.8, f32[24,128]{1,0:T(8,128)S(1)} %get-tuple-element.12.start_ref, f32[192,128]{1,0:T(8,128)S(1)} %get-tuple-element.13.poly_ref, bf16[48,1024]{1,0:T(8,128)(2,1)S(1)} %get-tuple-element.14.split_ref, bf16[264,224]{1,0:T(8,128)(2,1)S(1)} %copy-done.1), custom_call_target="tpu_custom_call" | custom-call | tf_op jit(solution)/shard_map/fit/pallas_call | solution.py:426
  26.9 9.4 %all_to_all.17 = f32[32,1,128]{2,1,0:T(1,128)S(1)} all-to-all(f32[32,1,128]{2,1,0:T(1,128)S(1)} %bitcast.10), channel_id=1, replica_groups=mesh['rows'=8,'fib'=4] {'rows','fib'}, dimensions={0} | all-to-all | bytes 32768 | tf_op jit(solution)/shard_map/all_to_all | solution.py:564
  36.3 0.0 copy-done
  36.3 0.0 copy-done.2
  36.3 2.3 %residual.1 = (f32[4,11]{1,0:T(4,128)}, f32[4,11]{1,0:T(4,128)}, bf16[5,128,1024]{2,1,0:T(8,128)(2,1)}) custom-call(f32[32,128]{1,0:T(8,128)S(1)} %bitcast.9, f32[24,256]{1,0:T(8,128)S(1)} %get-tuple-element.15.table_ref, f32[128,640]{1,0:T(8,128)S(1)} %get-tuple-element.16.lit_ref, f32[5,128]{1,0:T(8,128)S(1)} %copy-done.2, bf16[5,128,1024]{2,1,0:T(8,128)(2,1)S(1)} %copy-done), custom_call_target="tpu_custom_call" | custom-call | tf_op jit(solution)/shard_map/residual/pallas_call | solution.py:524
  (1 shorter events, 0.0 us)
Async XLA Ops:
  0.6 22.9 %copy-start.1 = (bf16[264,224]{1,0:T(8,128)(2,1)S(1)}, bf16[264,224]{1,0:T(8,128)(2,1)}, u32[]{:S(2)}) copy-start(bf16[264,224]{1,0:T(8,128)(2,1)} %constant.2.clone.map_ref) | copy-start | bytes 354820
  2.7 33.6 %copy-start = (bf16[5,128,1024]{2,1,0:T(8,128)(2,1)S(1)}, bf16[5,128,1024]{2,1,0:T(8,128)(2,1)}, u32[]{:S(2)}) copy-start(bf16[5,128,1024]{2,1,0:T(8,128)(2,1)} %frames_ref.1) | copy-start | bytes 3932164
  2.7 33.6 %copy-start.2 = (f32[5,128]{1,0:T(8,128)S(1)}, f32[5,128]{1,0:T(8,128)}, u32[]{:S(2)}) copy-start(f32[5,128]{1,0:T(8,128)} %amp_ref.1) | copy-start | bytes 7684
  2.7 1.8 %collective-permute-start = (f32[576,128]{1,0:T(8,128)S(1)}, f32[576,128]{1,0:T(8,128)S(1)}, u32[]{:S(2)}, u32[]{:S(2)}) collective-permute-start(f32[576,128]{1,0:T(8,128)S(1)} %get-tuple-element.11), channel_id=1, source_target_pairs={{0,1},{1,0},{2,3},{3,2},{4,5},{5,4},{6,7},{7,6},{8,9},{9,8},{10,11... | collective-permute-start | bytes 884744 | tf_op jit(solution)/shard_map/ppermute | solution.py:552

commit v6 on v5

--- a/solution.py
+++ b/solution.py
@@ -16,7 +16,7 @@
 LANE = 128
 KROWS = 24
 RHS = 2 * K
-PARTS = 9 * KROWS + 8
+WIDTH = RHS + 1
 VMEM_BYTES = 20 << 20
 
 HIGH = lax.Precision.HIGHEST
@@ -31,21 +31,20 @@
 
 
 def system_map():
-    table = np.zeros((K * KROWS, 3 * KROWS))
+    table = np.zeros((LANE, 2 * LANE))
     for i in range(K):
-        table[i * KROWS + RHS, 2 * KROWS + i] = 1.0
+        table[2 * KROWS + i, i * WIDTH + RHS] = 1.0
         for j in range(K):
             for inner in range(min(i, j) + 1):
                 target = i + j - 2 * inner
                 value = adams_factor(inner) * adams_factor(i - inner) * adams_factor(j - inner)
                 value = value / adams_factor(i + j - inner)
                 value = value * (2.0 * target + 1.0) / (2.0 * (i + j - inner) + 1.0)
-                table[i * KROWS + j, target] += value
-                table[i * KROWS + K + j, KROWS + target] += value
+                table[target, i * WIDTH + j] += value
+                table[KROWS + target, i * WIDTH + K + j] += value
     high = table.astype(jnp.bfloat16)
     low = (table - high.astype(np.float64)).astype(jnp.bfloat16)
-    spare = np.zeros((K * KROWS, PARTS - 9 * KROWS), jnp.bfloat16)
-    return np.concatenate([high, high, low, spare], axis=1)
+    return np.concatenate([high, low], axis=0)
 
 
 def legendre_list(rowpos, total, count):
@@ -56,15 +55,6 @@
             ((2 * order + 1) * tvals * polys[order] - order * polys[order - 1]) / (order + 1)
         )
     return polys
-
-
-def stacked_legendre(rowpos, total):
-    polys = legendre_list(rowpos, total, K)
-    row = lax.broadcasted_iota(jnp.int32, (KROWS, rowpos.shape[1]), 0)
-    table = jnp.zeros((KROWS, rowpos.shape[1]), jnp.float32)
-    for order in range(K):
-        table = jnp.where((row == order) | (row == K + order), polys[order], table)
-    return jnp.where(row == RHS, 1.0, table)
 
 
 def lit_by_lamp(start, first, rows):
@@ -118,6 +108,55 @@
     for copy in copies:
         copy.start()
     return copies
+
+
+def tables_kernel(after_ref, poly_ref, split_ref, local_ref):
+    rows = poly_ref.shape[1]
+    steps = poly_ref.shape[0] // KROWS
+
+    rowpos = (
+        lax.broadcasted_iota(jnp.int32, (steps, rows), 0) * rows
+        + lax.broadcasted_iota(jnp.int32, (steps, rows), 1)
+    ).astype(jnp.float32)
+    polys = legendre_list(rowpos, steps * rows, 2 * K - 1)
+    for order in range(KROWS):
+        poly_ref[order * steps : (order + 1) * steps, :] = (
+            polys[order] if order < 2 * K - 1 else jnp.zeros((steps, rows), jnp.float32)
+        )
+
+    spare = jnp.zeros((LANE - 3 * KROWS, rows), jnp.float32)
+    for step in range(steps):
+        stack = poly_ref[pl.ds(step, KROWS, stride=steps), :]
+        high = stack.astype(jnp.bfloat16).astype(jnp.float32)
+        for half, part in enumerate([high, stack - high]):
+            split_ref[step * rows : (step + 1) * rows, half * LANE : (half + 1) * LANE] = (
+                jnp.concatenate([part, part, part, spare], axis=0).T.astype(jnp.bfloat16)
+            )
+
+    first = lax.axis_index("rows") * rows
+    here = (first + lax.broadcasted_iota(jnp.int32, (rows, LANE), 0)).astype(jnp.float32)
+    for order, poly in enumerate(legendre_list(here, steps * rows, K)):
+        local_ref[order] = poly
+
+
+def tables(after, rows):
+    steps = lax.axis_size("rows")
+    shape = jax.ShapeDtypeStruct
+    vmem = pl.BlockSpec(memory_space=pltpu.VMEM)
+    size = 2 * LANE * steps * rows
+    return pl.pallas_call(
+        tables_kernel,
+        out_shape=(
+            shape((KROWS * steps, rows), jnp.float32),
+            shape((steps * rows, 2 * LANE), jnp.bfloat16),
+            shape((K, rows, LANE), jnp.float32),
+        ),
+        in_specs=[vmem],
+        out_specs=[vmem] * 3,
+        compiler_params=pltpu.CompilerParams(vmem_limit_bytes=VMEM_BYTES),
+        cost_estimate=pl.CostEstimate(flops=8 * size, bytes_accessed=4 * size, transcendentals=0),
+        name="tables",
+    )(after)
 
 
 def collapse_kernel(
@@ -131,10 +170,7 @@
     keep_ref,
     send_ref,
     lit_ref,
-    table_ref,
     coef_ref,
-    poly_ref,
-    split_ref,
     frames_ref,
     amp_ref,
     start_ref,
@@ -149,8 +185,6 @@
     lamps, rows, cols = frames_ref.shape
     owned = trace_ref.shape[0]
     fibers = which_ref.shape[1]
-    steps = lax.axis_size("rows")
-    total_rows = steps * rows
     me = lax.axis_index("rows") * lax.axis_size("fib") + lax.axis_index("fib")
     first = lax.axis_index("rows") * rows
     odd = lax.axis_index("fib") % 2 == 1
@@ -161,28 +195,6 @@
         small_sems,
     )
     arriving = start_copies([frames_hbm], [frames_ref], frame_sems)
-
-    rowpos = (
-        lax.broadcasted_iota(jnp.int32, (steps, rows), 0) * rows
-        + lax.broadcasted_iota(jnp.int32, (steps, rows), 1)
-    ).astype(jnp.float32)
-    polys = legendre_list(rowpos, total_rows, 2 * K - 1)
-    for order in range(KROWS):
-        poly_ref[order * steps : (order + 1) * steps, :] = (
-            polys[order] if order < 2 * K - 1 else jnp.zeros((steps, rows), jnp.float32)
-        )
-    for step in range(steps):
-        stack = poly_ref[pl.ds(step, KROWS, stride=steps), :]
-        high = stack.astype(jnp.bfloat16).astype(jnp.float32)
-        split_ref[:, step * rows : (step + 1) * rows] = jnp.concatenate(
-            [high, stack - high], axis=0
-        ).astype(jnp.bfloat16)
-
-    here = (first + lax.broadcasted_iota(jnp.int32, (1, rows), 1)).astype(jnp.float32)
-    stack = stacked_legendre(here, total_rows)
-    row = lax.broadcasted_iota(jnp.int32, (KROWS, rows), 0)
-    table_ref[:, 0:rows] = jnp.where(row < K, stack, 0.0)
-    table_ref[:, rows : 2 * rows] = jnp.where((row >= K) & (row < 2 * K), stack, 0.0)
 
     for copy in small:
         copy.wait()
@@ -266,10 +278,7 @@
         shape((blocks * height, rows), jnp.float32),
         shape((blocks * height, rows), jnp.float32),
         shape((rows, lamps * LANE), jnp.float32),
-        shape((KROWS, 2 * rows), jnp.float32),
         shape((KROWS, LANE), jnp.float32),
-        shape((KROWS * steps, rows), jnp.float32),
-        shape((2 * KROWS, steps * rows), jnp.bfloat16),
     )
     return pl.pallas_call(
         collapse_kernel,
@@ -302,6 +311,8 @@
     coef_ref,
     splat_ref,
     square_ref,
+    moment_ref,
+    system_ref,
 ):
     wide = owned * PIX
     steps = got_ref.shape[0] // (height * sources)
@@ -319,6 +330,8 @@
 
     coef_ref[...] = start_ref[...]
     weight_ref[...] = jnp.zeros_like(weight_ref)
+    moment_ref[...] = jnp.zeros_like(moment_ref)
+    system_ref[...] = jnp.zeros_like(system_ref)
 
     def newton_step(index, carry):
         for fiber in range(owned):
@@ -359,36 +372,36 @@
         )
         upper = weights.astype(jnp.bfloat16).astype(jnp.float32)
         both = jnp.concatenate([upper, weights - upper], axis=0).astype(jnp.bfloat16)
-        moments = lax.dot_general(
-            split_ref[...], both, (((1,), (1,)), ((), ())), preferred_element_type=jnp.float32
-        )
-        moments = moments[0:KROWS] + moments[KROWS:]
-        moments = jnp.concatenate(
-            [moments, jnp.zeros((KROWS, LANE - 2 * count), jnp.float32)], axis=1
-        )
-        moments = moments + pltpu.roll(moments, LANE - count, 1)
-        kinds = [moments] + [
-            pltpu.roll(moments, LANE - kind * owned, 1) for kind in range(1, 5)
-        ]
-        stacked = jnp.concatenate(
-            [
-                jnp.concatenate([kinds[0], kinds[1], kinds[3]], axis=0),
-                jnp.concatenate([kinds[1], kinds[2], kinds[4]], axis=0),
-            ],
-            axis=1,
-        )
-        high = stacked.astype(jnp.bfloat16).astype(jnp.float32)
-        spare = jnp.zeros((PARTS - 9 * KROWS, 2 * LANE), jnp.float32)
+        moments = jnp.dot(both, split_ref[...], preferred_element_type=jnp.float32)
+        moments = moments[:, 0:LANE] + moments[:, LANE:]
+        moment_ref[0:count, :] = moments[0:count] + moments[count:]
+        kinds = [moment_ref[kind * owned : kind * owned + SUB, :] for kind in range(5)]
+        lane = lax.broadcasted_iota(jnp.int32, (SUB, LANE), 1)
+
+        def three_kinds(one, two, three):
+            return jnp.where(lane < KROWS, one, jnp.where(lane < 2 * KROWS, two, three))
+
+        values = jnp.concatenate(
+            [three_kinds(kinds[0], kinds[1], kinds[3]), three_kinds(kinds[1], kinds[2], kinds[4])],
+            axis=0,
+        )
+        high = values.astype(jnp.bfloat16).astype(jnp.float32)
+        values = jnp.concatenate([high, values - high], axis=0)
         system = jnp.dot(
+            jnp.concatenate([values, values], axis=1).astype(jnp.bfloat16),
             map_ref[...],
-            jnp.concatenate([high, stacked - high, high, spare], axis=0).astype(jnp.bfloat16),
             preferred_element_type=jnp.float32,
         )
+        system = system[0 : 2 * SUB] + system[2 * SUB :]
+        for second in range(2):
+            for part in range(2):
+                turned = system[second * SUB : (second + 1) * SUB, part * LANE : (part + 1) * LANE].T
+                system_ref[second, part * LANE : (part + 1) * LANE, 0:SUB] = turned
         row = lax.broadcasted_iota(jnp.int32, (KROWS, LANE), 0)
         matrix = []
         for i in range(2 * K):
             second, at = divmod(i, K)
-            value = system[at * KROWS : (at + 1) * KROWS, second * LANE : (second + 1) * LANE]
+            value = system_ref[second, at * WIDTH : at * WIDTH + KROWS, :]
             matrix.append(jnp.where(row == i, 1.5 * value + 1.0, value))
         for pivot in range(2 * K):
             cut = KROWS - matrix[pivot].shape[0]
@@ -434,6 +447,8 @@
             pltpu.VMEM((KROWS, LANE), jnp.float32),
             pltpu.VMEM((owned, KROWS, rows), jnp.float32),
             pltpu.VMEM((LANE, LANE), jnp.float32),
+            pltpu.VMEM((count + SUB, LANE), jnp.float32),
+            pltpu.VMEM((2, 2 * LANE, LANE), jnp.float32),
         ],
         compiler_params=pltpu.CompilerParams(vmem_limit_bytes=VMEM_BYTES),
         name="fit",
@@ -443,7 +458,7 @@
 def residual_kernel(
     owned,
     coef_ref,
-    table_ref,
+    local_ref,
     lit_ref,
     amp_ref,
     frames_ref,
@@ -472,15 +487,13 @@
     coef = jnp.concatenate(
         [flipped[fiber * each : fiber * each + KROWS] for fiber in range(owned)], axis=1
     )
-    curves = lax.dot_general(
-        table_ref[...],
-        coef,
-        (((0,), (0,)), ((), ())),
-        precision=HIGH,
-        preferred_element_type=jnp.float32,
-    )
-    centre = curves[0:rows]
-    inverse = jnp.exp(-curves[rows : 2 * rows]) * coef[RHS : RHS + 1]
+    centre = jnp.zeros((rows, coef.shape[1]), jnp.float32)
+    spread = jnp.zeros((rows, coef.shape[1]), jnp.float32)
+    for order in range(K):
+        poly = jnp.concatenate([local_ref[order]] * (coef.shape[1] // LANE), axis=1)
+        centre = centre + poly * coef[order : order + 1]
+        spread = spread + poly * coef[K + order : K + order + 1]
+    inverse = jnp.exp(-spread) * coef[RHS : RHS + 1]
     amp = amp_ref[...]
     pixel = (lax.broadcasted_iota(jnp.int32, (rows, LANE), 1) % PIX).astype(jnp.float32)
     offset = pixel - (PIX - 1) / 2.0
@@ -516,7 +529,7 @@
         copy.wait()
 
 
-def residual(owned, coef, table, lit, amplitude, frames):
+def residual(owned, coef, local, lit, amplitude, frames):
     lamps, rows, cols = frames.shape
     vmem = pl.BlockSpec(memory_space=pltpu.VMEM)
     hbm = pl.BlockSpec(memory_space=pltpu.HBM)
@@ -537,7 +550,7 @@
         ],
         compiler_params=pltpu.CompilerParams(vmem_limit_bytes=VMEM_BYTES),
         name="residual",
-    )(coef, table, lit, amplitude, frames)
+    )(coef, local, lit, amplitude, frames)
 
 
 def body(frames, amplitude, line_start, bundle_width, fiber_bundle, trace_coef, width_coef):
@@ -546,10 +559,12 @@
     rows = frames.shape[1]
     owned = trace_coef.shape[0]
     height = owned * PIX + owned
-    keep, send, lit, table, start, poly, split = collapse(
+    keep, send, lit, start = collapse(
         frames, amplitude, line_start, bundle_width, fiber_bundle, trace_coef, width_coef, height
     )
     came = lax.ppermute(send, "fib", [(index, index ^ 1) for index in range(sources)])
+    poly, split, local = tables(start, rows)
+    came, poly, split, local = lax.optimization_barrier((came, poly, split, local))
     alike = [[index for index in range(devices) if index % 2 == odd] for odd in range(2)]
     unit = 4 if height % 4 == 0 else 1
     got = lax.all_to_all(
@@ -562,7 +577,7 @@
     ).reshape(devices // 2 * height, rows)
     reply = fit(got, start, poly, split, owned, devices, height, sources // 2)
     coef = lax.all_to_all(reply, BOTH, 0, 0, tiled=True)
-    return residual(owned, coef, table, lit, amplitude, frames)
+    return residual(owned, coef, local, lit, amplitude, frames)
 
 
 def solution(mesh):

time: 38.8 us -> 38.2 us (0.985)
  waiting for transfers between devices: 1.21 us -> 0.82 us
    ppermute x1, waiting for transfers between devices: 1.21 us -> 0.82 us  [body(): lax.ppermute(send, 'fib', [(index, index ^ 1) for index in range(sources)])]
  transfers between devices with their start and end apart: 1 -> 1, of which waited for: 1 -> 1; matrix products, arithmetic and copies ran while one was open for 0% -> 0% of each run, Pallas kernels for 0% -> 1%
where the time goes in v6:
time: 38.2 us; the launch traced here: 38 us
  blocking collectives  28.4 us (74%)
  Pallas kernels  7.53 us (20%)
  waiting for transfers between devices  0.82 us (2%)
  between operations  0.68 us (2%)
  starting transfers between devices  0.56 us (1%)
    all_to_all x1, blocking collectives, body(): lax.all_to_all((keep + came).reshape(devices // 2, height // unit, unit,...  19 us
    all_to_all x1, blocking collectives, body(): coef = lax.all_to_all(reply, BOTH, 0, 0, tiled=True)  9.4 us
    pallas_call x1, Pallas kernels, fit(): pl.pallas_call(functools.partial(fit_kernel, height, sources, owned), out...  3.22 us
    pallas_call x1, Pallas kernels, collapse(): pl.pallas_call(collapse_kernel, out_shape=outs, in_specs=[pl.BlockSpec(me...  2.02 us
    pallas_call x1, Pallas kernels, residual(): pl.pallas_call(functools.partial(residual_kernel, owned), out_shape=(fitt...  1.91 us
    ppermute x1, waiting for transfers between devices, body(): lax.ppermute(send, 'fib', [(index, index ^ 1) for index in range(sources)])  0.82 us
  transfers between devices with their start and end apart: 1, of which 1 were waited for; matrix products, arithmetic and copies ran while one was open for 0% of the time, Pallas kernels for 1%

profile of v6, /device:TPU:0, one launch (start us, length us, event | category | flops | bytes accessed | tf_op | source)
XLA Modules:
  0.0 38.0 jit_solution(8386123613793497820)
XLA Ops:
  0.6 0.0 copy-start.1
  0.6 2.0 %collapse.1 = (f32[576,128]{1,0:T(8,128)S(1)}, f32[576,128]{1,0:T(8,128)S(1)}, f32[128,640]{1,0:T(8,128)S(1)}, f32[24,128]{1,0:T(8,128)S(1)}) custom-call(bf16[5,128,1024]{2,1,0:T(8,128)(2,1)} %frames_ref.1, f32[5,128]{1,0:T(8,128)} %amp_ref.1, s32[5,24]{1,0:T(8,128)} %start_hbm.1, f32[1,20]{1,0:T(1,128)} %bitcast.12, s32[1,128]{1,0:T(1,128)} %bitcast.13, ...), custom_call_target="tpu_custom_call" | custom-call | tf_op jit(solution)/shard_map/collapse/pallas_call | solution.py:283
  2.7 0.0 copy-start
  2.7 0.0 copy-start.2
  2.7 0.6 %collective-permute-start = (f32[576,128]{1,0:T(8,128)S(1)}, f32[576,128]{1,0:T(8,128)S(1)}, u32[]{:S(2)}, u32[]{:S(2)}) collective-permute-start(f32[576,128]{1,0:T(8,128)S(1)} %get-tuple-element.15), channel_id=1, source_target_pairs={{0,1},{1,0},{2,3},{3,2},{4,5},{5,4},{6,7},{7,6},{8,9},{9,8},{10,11... | collective-permute-start | bytes 884744 | tf_op jit(solution)/shard_map/ppermute | solution.py:565
  3.3 0.4 %tables.1 = (f32[192,128]{1,0:T(8,128)S(1)}, bf16[1024,256]{1,0:T(8,128)(2,1)S(1)}, f32[11,128,128]{2,1,0:T(8,128)S(1)}) custom-call(f32[24,128]{1,0:T(8,128)S(1)} %get-tuple-element.16.after_ref.start_ref), custom_call_target="tpu_custom_call" | custom-call | flops 2097152 | bytes 1048576 | tf_op jit(solution)/shard_map/tables/pallas_call | solution.py:147
  3.6 0.8 %collective-permute-done = f32[576,128]{1,0:T(8,128)S(1)} collective-permute-done((f32[576,128]{1,0:T(8,128)S(1)}, f32[576,128]{1,0:T(8,128)S(1)}, u32[]{:S(2)}, u32[]{:S(2)}) %collective-permute-start) | collective-permute-done | bytes 294944 | tf_op jit(solution)/shard_map/ppermute | solution.py:565
  4.5 19.0 %all_to_all.16 = f32[16,9,4,128]{3,2,1,0:T(4,128)S(1)} all-to-all(f32[16,9,4,128]{3,2,1,0:T(4,128)S(1)} %bitcast.11), channel_id=1, replica_groups={{0,2,4,6,8,10,12,14,16,18,20,22,24,26,28,30},{1,3,5,7,9,11,13,15,17,19,..., dimensions={0} | all-to-all | bytes 589824 | tf_op jit(solution)/shard_map/all_to_all | solution.py:570
  23.5 0.0 copy-done.1
  23.5 3.2 %fit.1 = f32[32,128]{1,0:T(8,128)S(1)} custom-call(f32[576,128]{1,0:T(8,128)S(1)} %bitcast.8, f32[24,128]{1,0:T(8,128)S(1)} %get-tuple-element.16.after_ref.start_ref, f32[192,128]{1,0:T(8,128)S(1)} %get-tuple-element.21.poly_ref, bf16[1024,256]{1,0:T(8,128)(2,1)S(1)} %get-tuple-element.22.split_ref, bf16[256,256]{1,0:T(8,128)(2,1)S(1)} %copy-done.1), custom_call_target="tpu_custom_call" | custom-call | tf_op jit(solution)/shard_map/fit/pallas_call | solution.py:439
  26.7 9.4 %all_to_all.17 = f32[32,1,128]{2,1,0:T(1,128)S(1)} all-to-all(f32[32,1,128]{2,1,0:T(1,128)S(1)} %bitcast.10), channel_id=1, replica_groups=mesh['rows'=8,'fib'=4] {'rows','fib'}, dimensions={0} | all-to-all | bytes 32768 | tf_op jit(solution)/shard_map/all_to_all | solution.py:579
  36.1 0.0 copy-done
  36.1 0.0 copy-done.2
  36.1 1.9 %residual.1 = (f32[4,11]{1,0:T(4,128)}, f32[4,11]{1,0:T(4,128)}, bf16[5,128,1024]{2,1,0:T(8,128)(2,1)}) custom-call(f32[32,128]{1,0:T(8,128)S(1)} %bitcast.9, f32[11,128,128]{2,1,0:T(8,128)S(1)} %get-tuple-element.23.local_ref, f32[128,640]{1,0:T(8,128)S(1)} %get-tuple-element.24.lit_ref, f32[5,128]{1,0:T(8,128)S(1)} %copy-done.2, ...), custom_call_target="tpu_custom_call" | custom-call | tf_op jit(solution)/shard_map/residual/pallas_call | solution.py:537
  (1 shorter events, 0.0 us)
Async XLA Ops:
  0.6 22.9 %copy-start.1 = (bf16[256,256]{1,0:T(8,128)(2,1)S(1)}, bf16[256,256]{1,0:T(8,128)(2,1)}, u32[]{:S(2)}) copy-start(bf16[256,256]{1,0:T(8,128)(2,1)} %constant.2.clone.map_ref) | copy-start | bytes 393220
  2.7 33.5 %copy-start = (bf16[5,128,1024]{2,1,0:T(8,128)(2,1)S(1)}, bf16[5,128,1024]{2,1,0:T(8,128)(2,1)}, u32[]{:S(2)}) copy-start(bf16[5,128,1024]{2,1,0:T(8,128)(2,1)} %frames_ref.1) | copy-start | bytes 3932164
  2.7 33.5 %copy-start.2 = (f32[5,128]{1,0:T(8,128)S(1)}, f32[5,128]{1,0:T(8,128)}, u32[]{:S(2)}) copy-start(f32[5,128]{1,0:T(8,128)} %amp_ref.1) | copy-start | bytes 7684
  2.7 1.8 %collective-permute-start = (f32[576,128]{1,0:T(8,128)S(1)}, f32[576,128]{1,0:T(8,128)S(1)}, u32[]{:S(2)}, u32[]{:S(2)}) collective-permute-start(f32[576,128]{1,0:T(8,128)S(1)} %get-tuple-element.15), channel_id=1, source_target_pairs={{0,1},{1,0},{2,3},{3,2},{4,5},{5,4},{6,7},{7,6},{8,9},{9,8},{10,11... | collective-permute-start | bytes 884744 | tf_op jit(solution)/shard_map/ppermute | solution.py:565

commit v7 on v6

--- a/solution.py
+++ b/solution.py
@@ -1,4 +1,5 @@
 import functools
+import math
 
 import jax
 import jax.numpy as jnp
@@ -17,6 +18,7 @@
 KROWS = 24
 RHS = 2 * K
 WIDTH = RHS + 1
+ROOT = math.sqrt(0.5 / math.log(2.0))
 VMEM_BYTES = 20 << 20
 
 HIGH = lax.Precision.HIGHEST
@@ -169,7 +171,7 @@
     width_hbm,
     keep_ref,
     send_ref,
-    lit_ref,
+    weight_ref,
     coef_ref,
     frames_ref,
     amp_ref,
@@ -200,7 +202,13 @@
         copy.wait()
     amp = amp_ref[...]
     lit = lit_by_lamp(start_ref[...], first, rows)
-    lit_ref[...] = lit_columns(lit)
+    columns = lit_columns(lit)
+    for tile in range(cols // LANE):
+        amp_cols = per_column(amp, tile, owned, False)
+        for lamp in range(lamps):
+            weight_ref[lamp, :, tile * LANE : (tile + 1) * LANE] = (
+                columns[:, lamp * LANE : (lamp + 1) * LANE] * amp_cols[lamp : lamp + 1]
+            )
     which = which_ref[...]
     bundles = bundle_ref[...]
     base = jnp.zeros((1, fibers), jnp.float32)
@@ -241,12 +249,10 @@
     for copy in arriving:
         copy.wait()
     for tile in range(cols // LANE):
-        amp_cols = per_column(amp, tile, owned, False)
+        at = slice(tile * LANE, (tile + 1) * LANE)
         total = jnp.zeros((rows, LANE), jnp.float32)
         for lamp in range(lamps):
-            frame = frames_ref[lamp, :, tile * LANE : (tile + 1) * LANE].astype(jnp.float32)
-            weight = lit_ref[:, lamp * LANE : (lamp + 1) * LANE] * amp_cols[lamp : lamp + 1]
-            total = total + weight * frame
+            total = total + weight_ref[lamp, :, at] * frames_ref[lamp, :, at].astype(jnp.float32)
         flipped = total.T
         for pair in range(LANE // (2 * wide)):
             low = 2 * pair * wide
@@ -277,7 +283,7 @@
     outs = (
         shape((blocks * height, rows), jnp.float32),
         shape((blocks * height, rows), jnp.float32),
-        shape((rows, lamps * LANE), jnp.float32),
+        shape((lamps, rows, cols), jnp.float32),
         shape((KROWS, LANE), jnp.float32),
     )
     return pl.pallas_call(
@@ -348,24 +354,32 @@
                     centre = centre + splat_ref[fiber, order : order + 1, :] * poly
                     spread = spread + splat_ref[fiber, K + order : K + order + 1, :] * poly
                 inverse = jnp.exp(-spread) * splat_ref[fiber, RHS : RHS + 1, :]
+                reach = inverse * ROOT
                 power = sum_ref[wide + fiber, here, :]
                 sums = [jnp.zeros((SUB, rows), jnp.float32) for _ in range(5)]
                 for pixel in range(PIX):
-                    scaled = ((pixel - (PIX - 1) / 2.0) - centre) * inverse
-                    shape = jnp.exp(-0.5 * scaled * scaled)
+                    scaled = ((pixel - (PIX - 1) / 2.0) - centre) * reach
+                    shape = jnp.exp2(-(scaled * scaled))
                     bend = shape * scaled
-                    slope = bend * inverse
                     widen = bend * scaled
                     resid = sum_ref[fiber * PIX + pixel, here, :] - power * shape
-                    sums[0] = sums[0] + slope * slope
-                    sums[1] = sums[1] + slope * widen
+                    sums[0] = sums[0] + bend * bend
+                    sums[1] = sums[1] + bend * widen
                     sums[2] = sums[2] + widen * widen
-                    sums[3] = sums[3] + resid * slope
+                    sums[3] = sums[3] + resid * bend
                     sums[4] = sums[4] + resid * widen
+                slant = inverse * (1.0 / ROOT)
+                grow = 1.0 / (ROOT * ROOT)
+                values = [
+                    sums[0] * power * slant * slant,
+                    sums[1] * power * slant * grow,
+                    sums[2] * power * (grow * grow),
+                    sums[3] * slant,
+                    sums[4] * grow,
+                ]
                 for kind in range(5):
-                    value = sums[kind] * power if kind < 3 else sums[kind]
                     at = (kind * owned + fiber) * steps + group * SUB
-                    weight_ref[at : at + SUB, :] = value
+                    weight_ref[at : at + SUB, :] = values[kind]
         count = weight_ref.shape[0] // steps
         weights = jnp.concatenate(
             [weight_ref[pl.ds(step, count, stride=steps), :] for step in range(steps)], axis=1
@@ -397,26 +411,33 @@
             for part in range(2):
                 turned = system[second * SUB : (second + 1) * SUB, part * LANE : (part + 1) * LANE].T
                 system_ref[second, part * LANE : (part + 1) * LANE, 0:SUB] = turned
-        row = lax.broadcasted_iota(jnp.int32, (KROWS, LANE), 0)
+        row = lax.broadcasted_iota(jnp.int32, (SUB, LANE), 0)
         matrix = []
         for i in range(2 * K):
             second, at = divmod(i, K)
-            value = system_ref[second, at * WIDTH : at * WIDTH + KROWS, :]
-            matrix.append(jnp.where(row == i, 1.5 * value + 1.0, value))
+            tiles = {}
+            for tile in range(i // SUB, KROWS // SUB):
+                start = at * WIDTH + tile * SUB
+                tiles[tile] = system_ref[second, start : start + SUB, :]
+            value = tiles[i // SUB]
+            tiles[i // SUB] = jnp.where(row == i % SUB, 1.5 * value + 1.0, value)
+            matrix.append(tiles)
+
+        def entry(i, column):
+            return matrix[i][column // SUB][column % SUB : column % SUB + 1]
+
         for pivot in range(2 * K):
-            cut = KROWS - matrix[pivot].shape[0]
-            inverse = 1.0 / matrix[pivot][pivot - cut : pivot - cut + 1]
-            chosen = matrix[pivot] * inverse
+            inverse = 1.0 / entry(pivot, pivot)
+            chosen = {tile: value * inverse for tile, value in matrix[pivot].items()}
             for i in range(2 * K):
-                if i != pivot:
-                    scale = matrix[i][pivot - cut : pivot - cut + 1]
-                    matrix[i] = matrix[i] - scale * chosen
+                if i == pivot:
+                    continue
+                scale = entry(pivot, i) if i > pivot else entry(i, pivot)
+                for tile in range(max(i, pivot + 1) // SUB, KROWS // SUB):
+                    matrix[i][tile] = matrix[i][tile] - scale * chosen[tile]
             matrix[pivot] = chosen
-            if (pivot + 1) % SUB == 0:
-                matrix = [item[SUB:] for item in matrix]
         for i in range(2 * K):
-            cut = KROWS - matrix[i].shape[0]
-            coef_ref[i : i + 1, :] = coef_ref[i : i + 1, :] + matrix[i][RHS - cut : RHS - cut + 1]
+            coef_ref[i : i + 1, :] = coef_ref[i : i + 1, :] + entry(i, RHS)
         return carry
 
     lax.fori_loop(0, ITERS, newton_step, 0)
@@ -459,8 +480,7 @@
     owned,
     coef_ref,
     local_ref,
-    lit_ref,
-    amp_ref,
+    weight_ref,
     frames_ref,
     trace_hbm,
     width_hbm,
@@ -469,7 +489,6 @@
     width_ref,
     image_ref,
     shape_ref,
-    bright_ref,
     small_sems,
     image_sems,
 ):
@@ -494,7 +513,6 @@
         centre = centre + poly * coef[order : order + 1]
         spread = spread + poly * coef[K + order : K + order + 1]
     inverse = jnp.exp(-spread) * coef[RHS : RHS + 1]
-    amp = amp_ref[...]
     pixel = (lax.broadcasted_iota(jnp.int32, (rows, LANE), 1) % PIX).astype(jnp.float32)
     offset = pixel - (PIX - 1) / 2.0
     for tile in range(cols // LANE):
@@ -503,9 +521,6 @@
             inverse, tile, owned, True
         )
         shape_ref[:, here] = jnp.exp(-0.5 * scaled * scaled)
-        bright = per_column(amp, tile, owned, False)
-        for lamp in range(lamps):
-            bright_ref[lamp, :, here] = bright[lamp : lamp + 1]
 
     def leave(lamp):
         return pltpu.make_async_copy(
@@ -513,12 +528,11 @@
         )
 
     def one_lamp(lamp, carry):
-        lit = lit_ref[:, pl.ds(pl.multiple_of(lamp * LANE, LANE), LANE)]
         for tile in range(cols // LANE):
             here = slice(tile * LANE, (tile + 1) * LANE)
-            weight = lit * bright_ref[lamp, :, here]
             frame = frames_ref[lamp, :, here].astype(jnp.float32)
-            image_ref[lamp, :, here] = (frame - weight * shape_ref[:, here]).astype(jnp.bfloat16)
+            model = weight_ref[lamp, :, here] * shape_ref[:, here]
+            image_ref[lamp, :, here] = (frame - model).astype(jnp.bfloat16)
         leave(lamp).start()
         return carry
 
@@ -529,7 +543,7 @@
         copy.wait()
 
 
-def residual(owned, coef, local, lit, amplitude, frames):
+def residual(owned, coef, local, weight, frames):
     lamps, rows, cols = frames.shape
     vmem = pl.BlockSpec(memory_space=pltpu.VMEM)
     hbm = pl.BlockSpec(memory_space=pltpu.HBM)
@@ -537,20 +551,19 @@
     return pl.pallas_call(
         functools.partial(residual_kernel, owned),
         out_shape=(fitted, fitted, jax.ShapeDtypeStruct(frames.shape, jnp.bfloat16)),
-        in_specs=[vmem] * 5,
+        in_specs=[vmem] * 4,
         out_specs=[hbm] * 3,
         scratch_shapes=[
             pltpu.VMEM((owned, K), jnp.float32),
             pltpu.VMEM((owned, K), jnp.float32),
             pltpu.VMEM(frames.shape, jnp.bfloat16),
             pltpu.VMEM((rows, cols), jnp.float32),
-            pltpu.VMEM((lamps, 1, cols), jnp.float32),
             pltpu.SemaphoreType.DMA((2,)),
             pltpu.SemaphoreType.DMA((lamps,)),
         ],
         compiler_params=pltpu.CompilerParams(vmem_limit_bytes=VMEM_BYTES),
         name="residual",
-    )(coef, local, lit, amplitude, frames)
+    )(coef, local, weight, frames)
 
 
 def body(frames, amplitude, line_start, bundle_width, fiber_bundle, trace_coef, width_coef):
@@ -559,7 +572,7 @@
     rows = frames.shape[1]
     owned = trace_coef.shape[0]
     height = owned * PIX + owned
-    keep, send, lit, start = collapse(
+    keep, send, weight, start = collapse(
         frames, amplitude, line_start, bundle_width, fiber_bundle, trace_coef, width_coef, height
     )
     came = lax.ppermute(send, "fib", [(index, index ^ 1) for index in range(sources)])
@@ -577,7 +590,7 @@
     ).reshape(devices // 2 * height, rows)
     reply = fit(got, start, poly, split, owned, devices, height, sources // 2)
     coef = lax.all_to_all(reply, BOTH, 0, 0, tiled=True)
-    return residual(owned, coef, local, lit, amplitude, frames)
+    return residual(owned, coef, local, weight, frames)
 
 
 def solution(mesh):

time: 38.2 us -> 37.9 us (level)
  no operation moved by 1% of the time
where the time goes in v7:
time: 37.9 us; the launch traced here: 37.7 us
  blocking collectives  28.4 us (75%)
  Pallas kernels  7.22 us (19%)
  waiting for transfers between devices  0.82 us (2%)
  between operations  0.67 us (2%)
  starting transfers between devices  0.56 us (1%)
    all_to_all x1, blocking collectives, body(): lax.all_to_all((keep + came).reshape(devices // 2, height // unit, unit,...  19 us
    all_to_all x1, blocking collectives, body(): coef = lax.all_to_all(reply, BOTH, 0, 0, tiled=True)  9.4 us
    pallas_call x1, Pallas kernels, fit(): pl.pallas_call(functools.partial(fit_kernel, height, sources, owned), out...  3.06 us
    pallas_call x1, Pallas kernels, collapse(): pl.pallas_call(collapse_kernel, out_shape=outs, in_specs=[pl.BlockSpec(me...  1.94 us
    pallas_call x1, Pallas kernels, residual(): pl.pallas_call(functools.partial(residual_kernel, owned), out_shape=(fitt...  1.84 us
    ppermute x1, waiting for transfers between devices, body(): lax.ppermute(send, 'fib', [(index, index ^ 1) for index in range(sources)])  0.82 us
  transfers between devices with their start and end apart: 1, of which 1 were waited for; matrix products, arithmetic and copies ran while one was open for 0% of the time, Pallas kernels for 1%

profile of v7, /device:TPU:0, one launch (start us, length us, event | category | flops | bytes accessed | tf_op | source)
XLA Modules:
  0.0 37.7 jit_solution(12044527620263926084)
XLA Ops:
  0.6 0.0 copy-start.1
  0.6 1.9 %collapse.1 = (f32[576,128]{1,0:T(8,128)S(1)}, f32[576,128]{1,0:T(8,128)S(1)}, f32[5,128,1024]{2,1,0:T(8,128)S(1)}, f32[24,128]{1,0:T(8,128)S(1)}) custom-call(bf16[5,128,1024]{2,1,0:T(8,128)(2,1)} %frames_ref.1, f32[5,128]{1,0:T(8,128)} %amp_hbm.1, s32[5,24]{1,0:T(8,128)} %start_hbm.1, f32[1,20]{1,0:T(1,128)} %bitcast.12, s32[1,128]{1,0:T(1,128)} %bitcast.13, ...), custom_call_target="tpu_custom_call" | custom-call | tf_op jit(solution)/shard_map/collapse/pallas_call | solution.py:289
  2.6 0.0 copy-start
  2.6 0.6 %collective-permute-start = (f32[576,128]{1,0:T(8,128)S(1)}, f32[576,128]{1,0:T(8,128)S(1)}, u32[]{:S(2)}, u32[]{:S(2)}) collective-permute-start(f32[576,128]{1,0:T(8,128)S(1)} %get-tuple-element.15), channel_id=1, source_target_pairs={{0,1},{1,0},{2,3},{3,2},{4,5},{5,4},{6,7},{7,6},{8,9},{9,8},{10,11... | collective-permute-start | bytes 884744 | tf_op jit(solution)/shard_map/ppermute | solution.py:578
  3.2 0.4 %tables.1 = (f32[192,128]{1,0:T(8,128)S(1)}, bf16[1024,256]{1,0:T(8,128)(2,1)S(1)}, f32[11,128,128]{2,1,0:T(8,128)S(1)}) custom-call(f32[24,128]{1,0:T(8,128)S(1)} %get-tuple-element.16.after_ref.start_ref), custom_call_target="tpu_custom_call" | custom-call | flops 2097152 | bytes 1048576 | tf_op jit(solution)/shard_map/tables/pallas_call | solution.py:149
  3.6 0.8 %collective-permute-done = f32[576,128]{1,0:T(8,128)S(1)} collective-permute-done((f32[576,128]{1,0:T(8,128)S(1)}, f32[576,128]{1,0:T(8,128)S(1)}, u32[]{:S(2)}, u32[]{:S(2)}) %collective-permute-start) | collective-permute-done | bytes 294944 | tf_op jit(solution)/shard_map/ppermute | solution.py:578
  4.4 19.0 %all_to_all.16 = f32[16,9,4,128]{3,2,1,0:T(4,128)S(1)} all-to-all(f32[16,9,4,128]{3,2,1,0:T(4,128)S(1)} %bitcast.11), channel_id=1, replica_groups={{0,2,4,6,8,10,12,14,16,18,20,22,24,26,28,30},{1,3,5,7,9,11,13,15,17,19,..., dimensions={0} | all-to-all | bytes 589824 | tf_op jit(solution)/shard_map/all_to_all | solution.py:583
  23.4 0.0 copy-done.1
  23.4 3.1 %fit.1 = f32[32,128]{1,0:T(8,128)S(1)} custom-call(f32[576,128]{1,0:T(8,128)S(1)} %bitcast.8, f32[24,128]{1,0:T(8,128)S(1)} %get-tuple-element.16.after_ref.start_ref, f32[192,128]{1,0:T(8,128)S(1)} %get-tuple-element.21.poly_ref, bf16[1024,256]{1,0:T(8,128)(2,1)S(1)} %get-tuple-element.22.split_ref, bf16[256,256]{1,0:T(8,128)(2,1)S(1)} %copy-done.1), custom_call_target="tpu_custom_call" | custom-call | tf_op jit(solution)/shard_map/fit/pallas_call | solution.py:460
  26.5 9.4 %all_to_all.17 = f32[32,1,128]{2,1,0:T(1,128)S(1)} all-to-all(f32[32,1,128]{2,1,0:T(1,128)S(1)} %bitcast.10), channel_id=1, replica_groups=mesh['rows'=8,'fib'=4] {'rows','fib'}, dimensions={0} | all-to-all | bytes 32768 | tf_op jit(solution)/shard_map/all_to_all | solution.py:592
  35.9 0.0 copy-done
  35.9 1.8 %residual.1 = (f32[4,11]{1,0:T(4,128)}, f32[4,11]{1,0:T(4,128)}, bf16[5,128,1024]{2,1,0:T(8,128)(2,1)}) custom-call(f32[32,128]{1,0:T(8,128)S(1)} %bitcast.9, f32[11,128,128]{2,1,0:T(8,128)S(1)} %get-tuple-element.23.local_ref, f32[5,128,1024]{2,1,0:T(8,128)S(1)} %get-tuple-element.24.weight_ref, bf16[5,128,1024]{2,1,0:T(8,128)(2,1)S(1)} %copy-done), custom_call_target="tpu_custom_call" | custom-call | tf_op jit(solution)/shard_map/residual/pallas_call | solution.py:551
  (1 shorter events, 0.0 us)
Async XLA Ops:
  0.6 22.8 %copy-start.1 = (bf16[256,256]{1,0:T(8,128)(2,1)S(1)}, bf16[256,256]{1,0:T(8,128)(2,1)}, u32[]{:S(2)}) copy-start(bf16[256,256]{1,0:T(8,128)(2,1)} %constant.2.clone.map_ref) | copy-start | bytes 393220
  2.6 33.3 %copy-start = (bf16[5,128,1024]{2,1,0:T(8,128)(2,1)S(1)}, bf16[5,128,1024]{2,1,0:T(8,128)(2,1)}, u32[]{:S(2)}) copy-start(bf16[5,128,1024]{2,1,0:T(8,128)(2,1)} %frames_ref.1) | copy-start | bytes 3932164
  2.6 1.8 %collective-permute-start = (f32[576,128]{1,0:T(8,128)S(1)}, f32[576,128]{1,0:T(8,128)S(1)}, u32[]{:S(2)}, u32[]{:S(2)}) collective-permute-start(f32[576,128]{1,0:T(8,128)S(1)} %get-tuple-element.15), channel_id=1, source_target_pairs={{0,1},{1,0},{2,3},{3,2},{4,5},{5,4},{6,7},{7,6},{8,9},{9,8},{10,11... | collective-permute-start | bytes 884744 | tf_op jit(solution)/shard_map/ppermute | solution.py:578

commit v8 on v7

--- a/solution.py
+++ b/solution.py
@@ -18,6 +18,7 @@
 KROWS = 24
 RHS = 2 * K
 WIDTH = RHS + 1
+READY = 2 * PIX + 6
 ROOT = math.sqrt(0.5 / math.log(2.0))
 VMEM_BYTES = 20 << 20
 
@@ -112,7 +113,45 @@
     return copies
 
 
-def tables_kernel(after_ref, poly_ref, split_ref, local_ref):
+def spread_coefficients(coef_ref, splat_ref):
+    owned, _, rows = splat_ref.shape
+    for fiber in range(owned):
+        splat_ref[fiber] = jnp.broadcast_to(coef_ref[:, fiber : fiber + 1], (KROWS, rows))
+
+
+def curves_of(poly_ref, splat_ref, fiber, group, steps):
+    rows = poly_ref.shape[1]
+    centre = jnp.zeros((SUB, rows), jnp.float32)
+    spread = jnp.zeros((SUB, rows), jnp.float32)
+    for order in range(K):
+        poly = poly_ref[order * steps + group * SUB : order * steps + (group + 1) * SUB, :]
+        centre = centre + splat_ref[fiber, order : order + 1, :] * poly
+        spread = spread + splat_ref[fiber, K + order : K + order + 1, :] * poly
+    return centre, jnp.exp(-spread) * splat_ref[fiber, RHS : RHS + 1, :]
+
+
+def profile_at(pixel, centre, reach):
+    scaled = ((pixel - (PIX - 1) / 2.0) - centre) * reach
+    shape = jnp.exp2(-(scaled * scaled))
+    bend = shape * scaled
+    return shape, bend, bend * scaled
+
+
+def store_weights(weight_ref, sums, power, slant, fiber, owned, group, steps):
+    grow = 1.0 / (ROOT * ROOT)
+    values = [
+        sums[0] * power * slant * slant,
+        sums[1] * power * slant * grow,
+        sums[2] * power * (grow * grow),
+        sums[3] * slant,
+        sums[4] * grow,
+    ]
+    for kind in range(5):
+        at = (kind * owned + fiber) * steps + group * SUB
+        weight_ref[at : at + SUB, :] = values[kind]
+
+
+def tables_kernel(coef_ref, poly_ref, split_ref, local_ref, ready_ref, splat_ref):
     rows = poly_ref.shape[1]
     steps = poly_ref.shape[0] // KROWS
 
@@ -140,8 +179,23 @@
     for order, poly in enumerate(legendre_list(here, steps * rows, K)):
         local_ref[order] = poly
 
-
-def tables(after, rows):
+    spread_coefficients(coef_ref, splat_ref)
+    for group in range(steps // SUB):
+        at = slice(group * SUB, (group + 1) * SUB)
+        for fiber in range(splat_ref.shape[0]):
+            centre, inverse = curves_of(poly_ref, splat_ref, fiber, group, steps)
+            sums = [jnp.zeros((SUB, rows), jnp.float32) for _ in range(5)]
+            for pixel in range(PIX):
+                shape, bend, widen = profile_at(pixel, centre, inverse * ROOT)
+                ready_ref[fiber, pixel, at, :] = bend
+                ready_ref[fiber, PIX + pixel, at, :] = widen
+                terms = [bend * bend, bend * widen, widen * widen, shape * bend, shape * widen]
+                sums = [total + term for total, term in zip(sums, terms)]
+            for index, total in enumerate(sums + [inverse * (1.0 / ROOT)]):
+                ready_ref[fiber, 2 * PIX + index, at, :] = total
+
+
+def tables(coef, owned, rows):
     steps = lax.axis_size("rows")
     shape = jax.ShapeDtypeStruct
     vmem = pl.BlockSpec(memory_space=pltpu.VMEM)
@@ -152,13 +206,15 @@
             shape((KROWS * steps, rows), jnp.float32),
             shape((steps * rows, 2 * LANE), jnp.bfloat16),
             shape((K, rows, LANE), jnp.float32),
+            shape((owned, READY, steps, rows), jnp.float32),
         ),
         in_specs=[vmem],
-        out_specs=[vmem] * 3,
+        out_specs=[vmem] * 4,
+        scratch_shapes=[pltpu.VMEM((owned, KROWS, rows), jnp.float32)],
         compiler_params=pltpu.CompilerParams(vmem_limit_bytes=VMEM_BYTES),
         cost_estimate=pl.CostEstimate(flops=8 * size, bytes_accessed=4 * size, transcendentals=0),
         name="tables",
-    )(after)
+    )(coef)
 
 
 def collapse_kernel(
@@ -310,6 +366,7 @@
     start_ref,
     poly_ref,
     split_ref,
+    ready_ref,
     map_ref,
     send_ref,
     sum_ref,
@@ -339,47 +396,36 @@
     moment_ref[...] = jnp.zeros_like(moment_ref)
     system_ref[...] = jnp.zeros_like(system_ref)
 
-    def newton_step(index, carry):
-        for fiber in range(owned):
-            splat_ref[fiber] = jnp.broadcast_to(
-                coef_ref[:, fiber : fiber + 1], (KROWS, rows)
-            )
+    def first_weights():
         for group in range(steps // SUB):
             here = slice(group * SUB, (group + 1) * SUB)
             for fiber in range(owned):
-                centre = jnp.zeros((SUB, rows), jnp.float32)
-                spread = jnp.zeros((SUB, rows), jnp.float32)
-                for order in range(K):
-                    poly = poly_ref[order * steps + group * SUB : order * steps + (group + 1) * SUB, :]
-                    centre = centre + splat_ref[fiber, order : order + 1, :] * poly
-                    spread = spread + splat_ref[fiber, K + order : K + order + 1, :] * poly
-                inverse = jnp.exp(-spread) * splat_ref[fiber, RHS : RHS + 1, :]
-                reach = inverse * ROOT
+                power = sum_ref[wide + fiber, here, :]
+                last = [ready_ref[fiber, 2 * PIX + index, here, :] for index in range(6)]
+                sums = last[0:3] + [-(power * last[3]), -(power * last[4])]
+                for pixel in range(PIX):
+                    image = sum_ref[fiber * PIX + pixel, here, :]
+                    sums[3] = sums[3] + image * ready_ref[fiber, pixel, here, :]
+                    sums[4] = sums[4] + image * ready_ref[fiber, PIX + pixel, here, :]
+                store_weights(weight_ref, sums, power, last[5], fiber, owned, group, steps)
+
+    def later_weights():
+        spread_coefficients(coef_ref, splat_ref)
+        for group in range(steps // SUB):
+            here = slice(group * SUB, (group + 1) * SUB)
+            for fiber in range(owned):
+                centre, inverse = curves_of(poly_ref, splat_ref, fiber, group, steps)
                 power = sum_ref[wide + fiber, here, :]
                 sums = [jnp.zeros((SUB, rows), jnp.float32) for _ in range(5)]
                 for pixel in range(PIX):
-                    scaled = ((pixel - (PIX - 1) / 2.0) - centre) * reach
-                    shape = jnp.exp2(-(scaled * scaled))
-                    bend = shape * scaled
-                    widen = bend * scaled
+                    shape, bend, widen = profile_at(pixel, centre, inverse * ROOT)
                     resid = sum_ref[fiber * PIX + pixel, here, :] - power * shape
-                    sums[0] = sums[0] + bend * bend
-                    sums[1] = sums[1] + bend * widen
-                    sums[2] = sums[2] + widen * widen
-                    sums[3] = sums[3] + resid * bend
-                    sums[4] = sums[4] + resid * widen
+                    terms = [bend * bend, bend * widen, widen * widen, resid * bend, resid * widen]
+                    sums = [total + term for total, term in zip(sums, terms)]
                 slant = inverse * (1.0 / ROOT)
-                grow = 1.0 / (ROOT * ROOT)
-                values = [
-                    sums[0] * power * slant * slant,
-                    sums[1] * power * slant * grow,
-                    sums[2] * power * (grow * grow),
-                    sums[3] * slant,
-                    sums[4] * grow,
-                ]
-                for kind in range(5):
-                    at = (kind * owned + fiber) * steps + group * SUB
-                    weight_ref[at : at + SUB, :] = values[kind]
+                store_weights(weight_ref, sums, power, slant, fiber, owned, group, steps)
+
+    def solve_step():
         count = weight_ref.shape[0] // steps
         weights = jnp.concatenate(
             [weight_ref[pl.ds(step, count, stride=steps), :] for step in range(steps)], axis=1
@@ -438,9 +484,16 @@
             matrix[pivot] = chosen
         for i in range(2 * K):
             coef_ref[i : i + 1, :] = coef_ref[i : i + 1, :] + entry(i, RHS)
+
+    first_weights()
+    solve_step()
+
+    def later_step(index, carry):
+        later_weights()
+        solve_step()
         return carry
 
-    lax.fori_loop(0, ITERS, newton_step, 0)
+    lax.fori_loop(1, ITERS, later_step, 0)
 
     square_ref[...] = jnp.zeros_like(square_ref)
     lane = lax.broadcasted_iota(jnp.int32, (KROWS, LANE), 1)
@@ -452,7 +505,7 @@
     send_ref[...] = jnp.broadcast_to(packed, send_ref.shape)
 
 
-def fit(got, start, poly, split, owned, devices, height, sources):
+def fit(got, start, poly, split, ready, owned, devices, height, sources):
     rows = got.shape[1]
     steps = got.shape[0] // (height * sources)
     count = -(-5 * owned // SUB) * SUB
@@ -460,7 +513,7 @@
     return pl.pallas_call(
         functools.partial(fit_kernel, height, sources, owned),
         out_shape=jax.ShapeDtypeStruct((devices, LANE), jnp.float32),
-        in_specs=[vmem] * 5,
+        in_specs=[vmem] * 6,
         out_specs=vmem,
         scratch_shapes=[
             pltpu.VMEM((owned * PIX + owned, steps, rows), jnp.float32),
@@ -473,7 +526,7 @@
         ],
         compiler_params=pltpu.CompilerParams(vmem_limit_bytes=VMEM_BYTES),
         name="fit",
-    )(got, start, poly, split, jnp.asarray(system_map()))
+    )(got, start, poly, split, ready, jnp.asarray(system_map()))
 
 
 def residual_kernel(
@@ -576,8 +629,8 @@
         frames, amplitude, line_start, bundle_width, fiber_bundle, trace_coef, width_coef, height
     )
     came = lax.ppermute(send, "fib", [(index, index ^ 1) for index in range(sources)])
-    poly, split, local = tables(start, rows)
-    came, poly, split, local = lax.optimization_barrier((came, poly, split, local))
+    poly, split, local, ready = tables(start, owned, rows)
+    came, poly, split, local, ready = lax.optimization_barrier((came, poly, split, local, ready))
     alike = [[index for index in range(devices) if index % 2 == odd] for odd in range(2)]
     unit = 4 if height % 4 == 0 else 1
     got = lax.all_to_all(
@@ -588,7 +641,7 @@
         axis_index_groups=alike,
         tiled=True,
     ).reshape(devices // 2 * height, rows)
-    reply = fit(got, start, poly, split, owned, devices, height, sources // 2)
+    reply = fit(got, start, poly, split, ready, owned, devices, height, sources // 2)
     coef = lax.all_to_all(reply, BOTH, 0, 0, tiled=True)
     return residual(owned, coef, local, weight, frames)
 

time: 37.9 us -> 37.9 us (level)
  no operation moved by 1% of the time
where the time goes in v8:
time: 37.9 us; the launch traced here: 37.7 us
  blocking collectives  28.5 us (75%)
  Pallas kernels  7.12 us (19%)
  waiting for transfers between devices  0.73 us (2%)
  between operations  0.66 us (2%)
  starting transfers between devices  0.56 us (1%)
    all_to_all x1, blocking collectives, body(): lax.all_to_all((keep + came).reshape(devices // 2, height // unit, unit,...  19.1 us
    all_to_all x1, blocking collectives, body(): coef = lax.all_to_all(reply, BOTH, 0, 0, tiled=True)  9.4 us
    pallas_call x1, Pallas kernels, fit(): pl.pallas_call(functools.partial(fit_kernel, height, sources, owned), out...  2.87 us
    pallas_call x1, Pallas kernels, collapse(): pl.pallas_call(collapse_kernel, out_shape=outs, in_specs=[pl.BlockSpec(me...  1.94 us
    pallas_call x1, Pallas kernels, residual(): pl.pallas_call(functools.partial(residual_kernel, owned), out_shape=(fitt...  1.84 us
  transfers between devices with their start and end apart: 1, of which 1 were waited for; matrix products, arithmetic and copies ran while one was open for 0% of the time, Pallas kernels for 1%

profile of v8, /device:TPU:0, one launch (start us, length us, event | category | flops | bytes accessed | tf_op | source)
XLA Modules:
  0.0 37.7 jit_solution(7451073522172264432)
XLA Ops:
  0.6 0.0 copy-start.1
  0.6 1.9 %collapse.1 = (f32[576,128]{1,0:T(8,128)S(1)}, f32[576,128]{1,0:T(8,128)S(1)}, f32[5,128,1024]{2,1,0:T(8,128)S(1)}, f32[24,128]{1,0:T(8,128)S(1)}) custom-call(bf16[5,128,1024]{2,1,0:T(8,128)(2,1)} %frames_ref.1, f32[5,128]{1,0:T(8,128)} %amp_hbm.1, s32[5,24]{1,0:T(8,128)} %start_hbm.1, f32[1,20]{1,0:T(1,128)} %bitcast.12, s32[1,128]{1,0:T(1,128)} %bitcast.13, ...), custom_call_target="tpu_custom_call" | custom-call | tf_op jit(solution)/shard_map/collapse/pallas_call | solution.py:345
  2.6 0.6 %collective-permute-start = (f32[576,128]{1,0:T(8,128)S(1)}, f32[576,128]{1,0:T(8,128)S(1)}, u32[]{:S(2)}, u32[]{:S(2)}) collective-permute-start(f32[576,128]{1,0:T(8,128)S(1)} %get-tuple-element.17), channel_id=1, source_target_pairs={{0,1},{1,0},{2,3},{3,2},{4,5},{5,4},{6,7},{7,6},{8,9},{9,8},{10,11... | collective-permute-start | bytes 884744 | tf_op jit(solution)/shard_map/ppermute | solution.py:631
  3.2 0.5 %tables.1 = (f32[192,128]{1,0:T(8,128)S(1)}, bf16[1024,256]{1,0:T(8,128)(2,1)S(1)}, f32[11,128,128]{2,1,0:T(8,128)S(1)}, f32[4,22,8,128]{3,2,1,0:T(8,128)S(1)}) custom-call(f32[24,128]{1,0:T(8,128)S(1)} %get-tuple-element.18.coef_ref.start_ref), custom_call_target="tpu_custom_call" | custom-call | flops 2097152 | bytes 1048576 | tf_op jit(solution)/shard_map/tables/pallas_call | solution.py:203
  3.6 0.7 %collective-permute-done = f32[576,128]{1,0:T(8,128)S(1)} collective-permute-done((f32[576,128]{1,0:T(8,128)S(1)}, f32[576,128]{1,0:T(8,128)S(1)}, u32[]{:S(2)}, u32[]{:S(2)}) %collective-permute-start) | collective-permute-done | bytes 294944 | tf_op jit(solution)/shard_map/ppermute | solution.py:631
  4.4 0.0 copy-start
  4.4 19.1 %all_to_all.16 = f32[16,9,4,128]{3,2,1,0:T(4,128)S(1)} all-to-all(f32[16,9,4,128]{3,2,1,0:T(4,128)S(1)} %bitcast.11), channel_id=1, replica_groups={{0,2,4,6,8,10,12,14,16,18,20,22,24,26,28,30},{1,3,5,7,9,11,13,15,17,19,..., dimensions={0} | all-to-all | bytes 589824 | tf_op jit(solution)/shard_map/all_to_all | solution.py:636
  23.5 0.0 copy-done.1
  23.5 2.9 %fit.1 = f32[32,128]{1,0:T(8,128)S(1)} custom-call(f32[576,128]{1,0:T(8,128)S(1)} %bitcast.8, f32[24,128]{1,0:T(8,128)S(1)} %get-tuple-element.18.coef_ref.start_ref, f32[192,128]{1,0:T(8,128)S(1)} %get-tuple-element.24.poly_ref, bf16[1024,256]{1,0:T(8,128)(2,1)S(1)} %get-tuple-element.25.split_ref, f32[4,22,8,128]{3,2,1,0:T(8,128)S(1)} %get-tuple-element.26.ready_ref, ...), custom_call_target="tpu_custom_call" | custom-call | tf_op jit(solution)/shard_map/fit/pallas_call | solution.py:513
  26.4 9.4 %all_to_all.17 = f32[32,1,128]{2,1,0:T(1,128)S(1)} all-to-all(f32[32,1,128]{2,1,0:T(1,128)S(1)} %bitcast.10), channel_id=1, replica_groups=mesh['rows'=8,'fib'=4] {'rows','fib'}, dimensions={0} | all-to-all | bytes 32768 | tf_op jit(solution)/shard_map/all_to_all | solution.py:645
  35.8 0.0 copy-done
  35.8 1.8 %residual.1 = (f32[4,11]{1,0:T(4,128)}, f32[4,11]{1,0:T(4,128)}, bf16[5,128,1024]{2,1,0:T(8,128)(2,1)}) custom-call(f32[32,128]{1,0:T(8,128)S(1)} %bitcast.9, f32[11,128,128]{2,1,0:T(8,128)S(1)} %get-tuple-element.27.local_ref, f32[5,128,1024]{2,1,0:T(8,128)S(1)} %get-tuple-element.28.weight_ref, bf16[5,128,1024]{2,1,0:T(8,128)(2,1)S(1)} %copy-done), custom_call_target="tpu_custom_call" | custom-call | tf_op jit(solution)/shard_map/residual/pallas_call | solution.py:604
  (1 shorter events, 0.0 us)
Async XLA Ops:
  0.6 22.9 %copy-start.1 = (bf16[256,256]{1,0:T(8,128)(2,1)S(1)}, bf16[256,256]{1,0:T(8,128)(2,1)}, u32[]{:S(2)}) copy-start(bf16[256,256]{1,0:T(8,128)(2,1)} %constant.2.clone.map_ref) | copy-start | bytes 393220
  2.6 1.8 %collective-permute-start = (f32[576,128]{1,0:T(8,128)S(1)}, f32[576,128]{1,0:T(8,128)S(1)}, u32[]{:S(2)}, u32[]{:S(2)}) collective-permute-start(f32[576,128]{1,0:T(8,128)S(1)} %get-tuple-element.17), channel_id=1, source_target_pairs={{0,1},{1,0},{2,3},{3,2},{4,5},{5,4},{6,7},{7,6},{8,9},{9,8},{10,11... | collective-permute-start | bytes 884744 | tf_op jit(solution)/shard_map/ppermute | solution.py:631
  4.4 31.5 %copy-start = (bf16[5,128,1024]{2,1,0:T(8,128)(2,1)S(1)}, bf16[5,128,1024]{2,1,0:T(8,128)(2,1)}, u32[]{:S(2)}) copy-start(bf16[5,128,1024]{2,1,0:T(8,128)(2,1)} %frames_ref.1) | copy-start | bytes 3932164

commit v9 on v8

--- a/solution.py
+++ b/solution.py
@@ -18,6 +18,7 @@
 KROWS = 24
 RHS = 2 * K
 WIDTH = RHS + 1
+EARLY = 2
 READY = 2 * PIX + 6
 ROOT = math.sqrt(0.5 / math.log(2.0))
 VMEM_BYTES = 20 << 20
@@ -568,28 +569,37 @@
     inverse = jnp.exp(-spread) * coef[RHS : RHS + 1]
     pixel = (lax.broadcasted_iota(jnp.int32, (rows, LANE), 1) % PIX).astype(jnp.float32)
     offset = pixel - (PIX - 1) / 2.0
+    def leave(lamp):
+        return pltpu.make_async_copy(
+            image_ref.at[lamp], image_hbm.at[lamp], image_sems.at[lamp]
+        )
+
+    def finish(lamp, here, shape):
+        frame = frames_ref[lamp, :, here].astype(jnp.float32)
+        model = weight_ref[lamp, :, here] * shape
+        image_ref[lamp, :, here] = (frame - model).astype(jnp.bfloat16)
+
+    early = min(EARLY, lamps)
     for tile in range(cols // LANE):
         here = slice(tile * LANE, (tile + 1) * LANE)
         scaled = (offset - per_column(centre, tile, owned, True)) * per_column(
             inverse, tile, owned, True
         )
-        shape_ref[:, here] = jnp.exp(-0.5 * scaled * scaled)
-
-    def leave(lamp):
-        return pltpu.make_async_copy(
-            image_ref.at[lamp], image_hbm.at[lamp], image_sems.at[lamp]
-        )
+        shape = jnp.exp(-0.5 * scaled * scaled)
+        shape_ref[:, here] = shape
+        for lamp in range(early):
+            finish(lamp, here, shape)
+    for lamp in range(early):
+        leave(lamp).start()
 
     def one_lamp(lamp, carry):
         for tile in range(cols // LANE):
             here = slice(tile * LANE, (tile + 1) * LANE)
-            frame = frames_ref[lamp, :, here].astype(jnp.float32)
-            model = weight_ref[lamp, :, here] * shape_ref[:, here]
-            image_ref[lamp, :, here] = (frame - model).astype(jnp.bfloat16)
+            finish(lamp, here, shape_ref[:, here])
         leave(lamp).start()
         return carry
 
-    lax.fori_loop(0, lamps, one_lamp, 0)
+    lax.fori_loop(early, lamps, one_lamp, 0)
     for lamp in range(lamps):
         leave(lamp).wait()
     for copy in leaving:

time: 37.9 us -> 37.8 us (level)
  no operation moved by 1% of the time
where the time goes in v9:
time: 37.8 us; the launch traced here: 37.6 us
  blocking collectives  28.5 us (75%)
  Pallas kernels  7.05 us (19%)
  waiting for transfers between devices  0.73 us (2%)
  between operations  0.66 us (2%)
  starting transfers between devices  0.56 us (1%)
    all_to_all x1, blocking collectives, body(): lax.all_to_all((keep + came).reshape(devices // 2, height // unit, unit,...  19.1 us
    all_to_all x1, blocking collectives, body(): coef = lax.all_to_all(reply, BOTH, 0, 0, tiled=True)  9.4 us
    pallas_call x1, Pallas kernels, fit(): pl.pallas_call(functools.partial(fit_kernel, height, sources, owned), out...  2.87 us
    pallas_call x1, Pallas kernels, collapse(): pl.pallas_call(collapse_kernel, out_shape=outs, in_specs=[pl.BlockSpec(me...  1.94 us
    pallas_call x1, Pallas kernels, residual(): pl.pallas_call(functools.partial(residual_kernel, owned), out_shape=(fitt...  1.76 us
  transfers between devices with their start and end apart: 1, of which 1 were waited for; matrix products, arithmetic and copies ran while one was open for 0% of the time, Pallas kernels for 1%

profile of v9, /device:TPU:0, one launch (start us, length us, event | category | flops | bytes accessed | tf_op | source)
XLA Modules:
  0.0 37.6 jit_solution(17721252485518309526)
XLA Ops:
  0.6 0.0 copy-start.1
  0.6 1.9 %collapse.1 = (f32[576,128]{1,0:T(8,128)S(1)}, f32[576,128]{1,0:T(8,128)S(1)}, f32[5,128,1024]{2,1,0:T(8,128)S(1)}, f32[24,128]{1,0:T(8,128)S(1)}) custom-call(bf16[5,128,1024]{2,1,0:T(8,128)(2,1)} %frames_ref.1, f32[5,128]{1,0:T(8,128)} %amp_hbm.1, s32[5,24]{1,0:T(8,128)} %start_hbm.1, f32[1,20]{1,0:T(1,128)} %bitcast.12, s32[1,128]{1,0:T(1,128)} %bitcast.13, ...), custom_call_target="tpu_custom_call" | custom-call | tf_op jit(solution)/shard_map/collapse/pallas_call | solution.py:346
  2.6 0.6 %collective-permute-start = (f32[576,128]{1,0:T(8,128)S(1)}, f32[576,128]{1,0:T(8,128)S(1)}, u32[]{:S(2)}, u32[]{:S(2)}) collective-permute-start(f32[576,128]{1,0:T(8,128)S(1)} %get-tuple-element.17), channel_id=1, source_target_pairs={{0,1},{1,0},{2,3},{3,2},{4,5},{5,4},{6,7},{7,6},{8,9},{9,8},{10,11... | collective-permute-start | bytes 884744 | tf_op jit(solution)/shard_map/ppermute | solution.py:641
  3.2 0.5 %tables.1 = (f32[192,128]{1,0:T(8,128)S(1)}, bf16[1024,256]{1,0:T(8,128)(2,1)S(1)}, f32[11,128,128]{2,1,0:T(8,128)S(1)}, f32[4,22,8,128]{3,2,1,0:T(8,128)S(1)}) custom-call(f32[24,128]{1,0:T(8,128)S(1)} %get-tuple-element.18.coef_ref.start_ref), custom_call_target="tpu_custom_call" | custom-call | flops 2097152 | bytes 1048576 | tf_op jit(solution)/shard_map/tables/pallas_call | solution.py:204
  3.6 0.7 %collective-permute-done = f32[576,128]{1,0:T(8,128)S(1)} collective-permute-done((f32[576,128]{1,0:T(8,128)S(1)}, f32[576,128]{1,0:T(8,128)S(1)}, u32[]{:S(2)}, u32[]{:S(2)}) %collective-permute-start) | collective-permute-done | bytes 294944 | tf_op jit(solution)/shard_map/ppermute | solution.py:641
  4.4 0.0 copy-start
  4.4 19.1 %all_to_all.16 = f32[16,9,4,128]{3,2,1,0:T(4,128)S(1)} all-to-all(f32[16,9,4,128]{3,2,1,0:T(4,128)S(1)} %bitcast.11), channel_id=1, replica_groups={{0,2,4,6,8,10,12,14,16,18,20,22,24,26,28,30},{1,3,5,7,9,11,13,15,17,19,..., dimensions={0} | all-to-all | bytes 589824 | tf_op jit(solution)/shard_map/all_to_all | solution.py:646
  23.5 0.0 copy-done.1
  23.5 2.9 %fit.1 = f32[32,128]{1,0:T(8,128)S(1)} custom-call(f32[576,128]{1,0:T(8,128)S(1)} %bitcast.8, f32[24,128]{1,0:T(8,128)S(1)} %get-tuple-element.18.coef_ref.start_ref, f32[192,128]{1,0:T(8,128)S(1)} %get-tuple-element.24.poly_ref, bf16[1024,256]{1,0:T(8,128)(2,1)S(1)} %get-tuple-element.25.split_ref, f32[4,22,8,128]{3,2,1,0:T(8,128)S(1)} %get-tuple-element.26.ready_ref, ...), custom_call_target="tpu_custom_call" | custom-call | tf_op jit(solution)/shard_map/fit/pallas_call | solution.py:514
  26.4 9.4 %all_to_all.17 = f32[32,1,128]{2,1,0:T(1,128)S(1)} all-to-all(f32[32,1,128]{2,1,0:T(1,128)S(1)} %bitcast.10), channel_id=1, replica_groups=mesh['rows'=8,'fib'=4] {'rows','fib'}, dimensions={0} | all-to-all | bytes 32768 | tf_op jit(solution)/shard_map/all_to_all | solution.py:655
  35.8 0.0 copy-done
  35.8 1.8 %residual.1 = (f32[4,11]{1,0:T(4,128)}, f32[4,11]{1,0:T(4,128)}, bf16[5,128,1024]{2,1,0:T(8,128)(2,1)}) custom-call(f32[32,128]{1,0:T(8,128)S(1)} %bitcast.9, f32[11,128,128]{2,1,0:T(8,128)S(1)} %get-tuple-element.27.local_ref, f32[5,128,1024]{2,1,0:T(8,128)S(1)} %get-tuple-element.28.weight_ref, bf16[5,128,1024]{2,1,0:T(8,128)(2,1)S(1)} %copy-done), custom_call_target="tpu_custom_call" | custom-call | tf_op jit(solution)/shard_map/residual/pallas_call | solution.py:614
  (1 shorter events, 0.0 us)
Async XLA Ops:
  0.6 22.9 %copy-start.1 = (bf16[256,256]{1,0:T(8,128)(2,1)S(1)}, bf16[256,256]{1,0:T(8,128)(2,1)}, u32[]{:S(2)}) copy-start(bf16[256,256]{1,0:T(8,128)(2,1)} %constant.2.clone.map_ref) | copy-start | bytes 393220
  2.6 1.8 %collective-permute-start = (f32[576,128]{1,0:T(8,128)S(1)}, f32[576,128]{1,0:T(8,128)S(1)}, u32[]{:S(2)}, u32[]{:S(2)}) collective-permute-start(f32[576,128]{1,0:T(8,128)S(1)} %get-tuple-element.17), channel_id=1, source_target_pairs={{0,1},{1,0},{2,3},{3,2},{4,5},{5,4},{6,7},{7,6},{8,9},{9,8},{10,11... | collective-permute-start | bytes 884744 | tf_op jit(solution)/shard_map/ppermute | solution.py:641
  4.4 31.5 %copy-start = (bf16[5,128,1024]{2,1,0:T(8,128)(2,1)S(1)}, bf16[5,128,1024]{2,1,0:T(8,128)(2,1)}, u32[]{:S(2)}) copy-start(bf16[5,128,1024]{2,1,0:T(8,128)(2,1)} %frames_ref.1) | copy-start | bytes 3932164

commit v10 on v9

--- a/solution.py
+++ b/solution.py
@@ -157,7 +157,7 @@
     steps = poly_ref.shape[0] // KROWS
 
     rowpos = (
-        lax.broadcasted_iota(jnp.int32, (steps, rows), 0) * rows
+        (steps - 1 - lax.broadcasted_iota(jnp.int32, (steps, rows), 0)) * rows
         + lax.broadcasted_iota(jnp.int32, (steps, rows), 1)
     ).astype(jnp.float32)
     polys = legendre_list(rowpos, steps * rows, 2 * K - 1)
@@ -291,7 +291,8 @@
     height = wide + owned
 
     def place(block, offset, even_value, odd_value):
-        at = slice(block * height + offset, block * height + offset + even_value.shape[0])
+        start = (fibers // (2 * owned) - 1 - block) * height + offset
+        at = slice(start, start + even_value.shape[0])
         keep_ref[at, :] = jnp.where(odd, odd_value, even_value)
         send_ref[at, :] = jnp.where(odd, even_value, odd_value)
 
@@ -641,7 +642,9 @@
     came = lax.ppermute(send, "fib", [(index, index ^ 1) for index in range(sources)])
     poly, split, local, ready = tables(start, owned, rows)
     came, poly, split, local, ready = lax.optimization_barrier((came, poly, split, local, ready))
-    alike = [[index for index in range(devices) if index % 2 == odd] for odd in range(2)]
+    alike = [
+        [index for index in reversed(range(devices)) if index % 2 == odd] for odd in range(2)
+    ]
     unit = 4 if height % 4 == 0 else 1
     got = lax.all_to_all(
         (keep + came).reshape(devices // 2, height // unit, unit, rows),

time: 37.8 us -> 37.4 us (0.989)
    all_to_all x1, blocking collectives: 19.1 us -> 17.2 us  [body(): lax.all_to_all((keep + came).reshape(devices // 2, height // unit, unit,...]
    all_to_all x1, blocking collectives: 9.4 us -> 11 us  [body(): coef = lax.all_to_all(reply, BOTH, 0, 0, tiled=True)]
where the time goes in v10:
time: 37.4 us; the launch traced here: 37.2 us
  blocking collectives  28.2 us (75%)
  Pallas kernels  7.05 us (19%)
  waiting for transfers between devices  0.73 us (2%)
  between operations  0.66 us (2%)
  starting transfers between devices  0.56 us (1%)
    all_to_all x1, blocking collectives, body(): lax.all_to_all((keep + came).reshape(devices // 2, height // unit, unit,...  17.2 us
    all_to_all x1, blocking collectives, body(): coef = lax.all_to_all(reply, BOTH, 0, 0, tiled=True)  11 us
    pallas_call x1, Pallas kernels, fit(): pl.pallas_call(functools.partial(fit_kernel, height, sources, owned), out...  2.87 us
    pallas_call x1, Pallas kernels, collapse(): pl.pallas_call(collapse_kernel, out_shape=outs, in_specs=[pl.BlockSpec(me...  1.94 us
    pallas_call x1, Pallas kernels, residual(): pl.pallas_call(functools.partial(residual_kernel, owned), out_shape=(fitt...  1.76 us
  transfers between devices with their start and end apart: 1, of which 1 were waited for; matrix products, arithmetic and copies ran while one was open for 0% of the time, Pallas kernels for 1%

profile of v10, /device:TPU:0, one launch (start us, length us, event | category | flops | bytes accessed | tf_op | source)
XLA Modules:
  0.0 37.2 jit_solution(5569607654553718281)
XLA Ops:
  0.6 0.0 copy-start.1
  0.6 1.9 %collapse.1 = (f32[576,128]{1,0:T(8,128)S(1)}, f32[576,128]{1,0:T(8,128)S(1)}, f32[5,128,1024]{2,1,0:T(8,128)S(1)}, f32[24,128]{1,0:T(8,128)S(1)}) custom-call(bf16[5,128,1024]{2,1,0:T(8,128)(2,1)} %frames_ref.1, f32[5,128]{1,0:T(8,128)} %amp_hbm.1, s32[5,24]{1,0:T(8,128)} %start_hbm.1, f32[1,20]{1,0:T(1,128)} %bitcast.12, s32[1,128]{1,0:T(1,128)} %bitcast.13, ...), custom_call_target="tpu_custom_call" | custom-call | tf_op jit(solution)/shard_map/collapse/pallas_call | solution.py:347
  2.6 0.6 %collective-permute-start = (f32[576,128]{1,0:T(8,128)S(1)}, f32[576,128]{1,0:T(8,128)S(1)}, u32[]{:S(2)}, u32[]{:S(2)}) collective-permute-start(f32[576,128]{1,0:T(8,128)S(1)} %get-tuple-element.17), channel_id=1, source_target_pairs={{0,1},{1,0},{2,3},{3,2},{4,5},{5,4},{6,7},{7,6},{8,9},{9,8},{10,11... | collective-permute-start | bytes 884744 | tf_op jit(solution)/shard_map/ppermute | solution.py:642
  3.2 0.5 %tables.1 = (f32[192,128]{1,0:T(8,128)S(1)}, bf16[1024,256]{1,0:T(8,128)(2,1)S(1)}, f32[11,128,128]{2,1,0:T(8,128)S(1)}, f32[4,22,8,128]{3,2,1,0:T(8,128)S(1)}) custom-call(f32[24,128]{1,0:T(8,128)S(1)} %get-tuple-element.18.coef_ref.start_ref), custom_call_target="tpu_custom_call" | custom-call | flops 2097152 | bytes 1048576 | tf_op jit(solution)/shard_map/tables/pallas_call | solution.py:204
  3.6 0.7 %collective-permute-done = f32[576,128]{1,0:T(8,128)S(1)} collective-permute-done((f32[576,128]{1,0:T(8,128)S(1)}, f32[576,128]{1,0:T(8,128)S(1)}, u32[]{:S(2)}, u32[]{:S(2)}) %collective-permute-start) | collective-permute-done | bytes 294944 | tf_op jit(solution)/shard_map/ppermute | solution.py:642
  4.4 0.0 copy-start
  4.4 17.2 %all_to_all.16 = f32[16,9,4,128]{3,2,1,0:T(4,128)S(1)} all-to-all(f32[16,9,4,128]{3,2,1,0:T(4,128)S(1)} %bitcast.11), channel_id=1, replica_groups={{30,28,26,24,22,20,18,16,14,12,10,8,6,4,2,0},{31,29,27,25,23,21,19,17,1..., dimensions={0} | all-to-all | bytes 589824 | tf_op jit(solution)/shard_map/all_to_all | solution.py:649
  21.6 0.0 copy-done.1
  21.6 2.9 %fit.1 = f32[32,128]{1,0:T(8,128)S(1)} custom-call(f32[576,128]{1,0:T(8,128)S(1)} %bitcast.8, f32[24,128]{1,0:T(8,128)S(1)} %get-tuple-element.18.coef_ref.start_ref, f32[192,128]{1,0:T(8,128)S(1)} %get-tuple-element.24.poly_ref, bf16[1024,256]{1,0:T(8,128)(2,1)S(1)} %get-tuple-element.25.split_ref, f32[4,22,8,128]{3,2,1,0:T(8,128)S(1)} %get-tuple-element.26.ready_ref, ...), custom_call_target="tpu_custom_call" | custom-call | tf_op jit(solution)/shard_map/fit/pallas_call | solution.py:515
  24.5 11.0 %all_to_all.17 = f32[32,1,128]{2,1,0:T(1,128)S(1)} all-to-all(f32[32,1,128]{2,1,0:T(1,128)S(1)} %bitcast.10), channel_id=1, replica_groups=mesh['rows'=8,'fib'=4] {'rows','fib'}, dimensions={0} | all-to-all | bytes 32768 | tf_op jit(solution)/shard_map/all_to_all | solution.py:658
  35.4 0.0 copy-done
  35.4 1.8 %residual.1 = (f32[4,11]{1,0:T(4,128)}, f32[4,11]{1,0:T(4,128)}, bf16[5,128,1024]{2,1,0:T(8,128)(2,1)}) custom-call(f32[32,128]{1,0:T(8,128)S(1)} %bitcast.9, f32[11,128,128]{2,1,0:T(8,128)S(1)} %get-tuple-element.27.local_ref, f32[5,128,1024]{2,1,0:T(8,128)S(1)} %get-tuple-element.28.weight_ref, bf16[5,128,1024]{2,1,0:T(8,128)(2,1)S(1)} %copy-done), custom_call_target="tpu_custom_call" | custom-call | tf_op jit(solution)/shard_map/residual/pallas_call | solution.py:615
  (1 shorter events, 0.0 us)
Async XLA Ops:
  0.6 21.0 %copy-start.1 = (bf16[256,256]{1,0:T(8,128)(2,1)S(1)}, bf16[256,256]{1,0:T(8,128)(2,1)}, u32[]{:S(2)}) copy-start(bf16[256,256]{1,0:T(8,128)(2,1)} %constant.2.clone.map_ref) | copy-start | bytes 393220
  2.6 1.8 %collective-permute-start = (f32[576,128]{1,0:T(8,128)S(1)}, f32[576,128]{1,0:T(8,128)S(1)}, u32[]{:S(2)}, u32[]{:S(2)}) collective-permute-start(f32[576,128]{1,0:T(8,128)S(1)} %get-tuple-element.17), channel_id=1, source_target_pairs={{0,1},{1,0},{2,3},{3,2},{4,5},{5,4},{6,7},{7,6},{8,9},{9,8},{10,11... | collective-permute-start | bytes 884744 | tf_op jit(solution)/shard_map/ppermute | solution.py:642
  4.4 31.1 %copy-start = (bf16[5,128,1024]{2,1,0:T(8,128)(2,1)S(1)}, bf16[5,128,1024]{2,1,0:T(8,128)(2,1)}, u32[]{:S(2)}) copy-start(bf16[5,128,1024]{2,1,0:T(8,128)(2,1)} %frames_ref.1) | copy-start | bytes 3932164

commit v11 on v10

--- a/solution.py
+++ b/solution.py
@@ -484,8 +484,12 @@
                 for tile in range(max(i, pivot + 1) // SUB, KROWS // SUB):
                     matrix[i][tile] = matrix[i][tile] - scale * chosen[tile]
             matrix[pivot] = chosen
-        for i in range(2 * K):
-            coef_ref[i : i + 1, :] = coef_ref[i : i + 1, :] + entry(i, RHS)
+        for tile in range(KROWS // SUB):
+            update = jnp.zeros((SUB, LANE), jnp.float32)
+            for i in range(tile * SUB, min((tile + 1) * SUB, 2 * K)):
+                update = jnp.where(row == i % SUB, entry(i, RHS), update)
+            at = slice(tile * SUB, (tile + 1) * SUB)
+            coef_ref[at, :] = coef_ref[at, :] + update
 
     first_weights()
     solve_step()

time: 37.4 us -> 37.4 us (level)
  no operation moved by 1% of the time
where the time goes in v11:
time: 37.4 us; the launch traced here: 37.2 us
  blocking collectives  28.2 us (75%)
  Pallas kernels  7.06 us (19%)
  waiting for transfers between devices  0.73 us (2%)
  between operations  0.66 us (2%)
  starting transfers between devices  0.56 us (1%)
    all_to_all x1, blocking collectives, body(): lax.all_to_all((keep + came).reshape(devices // 2, height // unit, unit,...  17.2 us
    all_to_all x1, blocking collectives, body(): coef = lax.all_to_all(reply, BOTH, 0, 0, tiled=True)  11 us
    pallas_call x1, Pallas kernels, fit(): pl.pallas_call(functools.partial(fit_kernel, height, sources, owned), out...  2.88 us
    pallas_call x1, Pallas kernels, collapse(): pl.pallas_call(collapse_kernel, out_shape=outs, in_specs=[pl.BlockSpec(me...  1.94 us
    pallas_call x1, Pallas kernels, residual(): pl.pallas_call(functools.partial(residual_kernel, owned), out_shape=(fitt...  1.76 us
  transfers between devices with their start and end apart: 1, of which 1 were waited for; matrix products, arithmetic and copies ran while one was open for 0% of the time, Pallas kernels for 1%

profile of v11, /device:TPU:0, one launch (start us, length us, event | category | flops | bytes accessed | tf_op | source)
XLA Modules:
  0.0 37.2 jit_solution(12985912276999644707)
XLA Ops:
  0.6 0.0 copy-start.1
  0.6 1.9 %collapse.1 = (f32[576,128]{1,0:T(8,128)S(1)}, f32[576,128]{1,0:T(8,128)S(1)}, f32[5,128,1024]{2,1,0:T(8,128)S(1)}, f32[24,128]{1,0:T(8,128)S(1)}) custom-call(bf16[5,128,1024]{2,1,0:T(8,128)(2,1)} %frames_ref.1, f32[5,128]{1,0:T(8,128)} %amp_hbm.1, s32[5,24]{1,0:T(8,128)} %start_hbm.1, f32[1,20]{1,0:T(1,128)} %bitcast.12, s32[1,128]{1,0:T(1,128)} %bitcast.13, ...), custom_call_target="tpu_custom_call" | custom-call | tf_op jit(solution)/shard_map/collapse/pallas_call | solution.py:347
  2.6 0.6 %collective-permute-start = (f32[576,128]{1,0:T(8,128)S(1)}, f32[576,128]{1,0:T(8,128)S(1)}, u32[]{:S(2)}, u32[]{:S(2)}) collective-permute-start(f32[576,128]{1,0:T(8,128)S(1)} %get-tuple-element.17), channel_id=1, source_target_pairs={{0,1},{1,0},{2,3},{3,2},{4,5},{5,4},{6,7},{7,6},{8,9},{9,8},{10,11... | collective-permute-start | bytes 884744 | tf_op jit(solution)/shard_map/ppermute | solution.py:646
  3.2 0.5 %tables.1 = (f32[192,128]{1,0:T(8,128)S(1)}, bf16[1024,256]{1,0:T(8,128)(2,1)S(1)}, f32[11,128,128]{2,1,0:T(8,128)S(1)}, f32[4,22,8,128]{3,2,1,0:T(8,128)S(1)}) custom-call(f32[24,128]{1,0:T(8,128)S(1)} %get-tuple-element.18.coef_ref.start_ref), custom_call_target="tpu_custom_call" | custom-call | flops 2097152 | bytes 1048576 | tf_op jit(solution)/shard_map/tables/pallas_call | solution.py:204
  3.6 0.7 %collective-permute-done = f32[576,128]{1,0:T(8,128)S(1)} collective-permute-done((f32[576,128]{1,0:T(8,128)S(1)}, f32[576,128]{1,0:T(8,128)S(1)}, u32[]{:S(2)}, u32[]{:S(2)}) %collective-permute-start) | collective-permute-done | bytes 294944 | tf_op jit(solution)/shard_map/ppermute | solution.py:646
  4.4 0.0 copy-start
  4.4 17.2 %all_to_all.16 = f32[16,9,4,128]{3,2,1,0:T(4,128)S(1)} all-to-all(f32[16,9,4,128]{3,2,1,0:T(4,128)S(1)} %bitcast.11), channel_id=1, replica_groups={{30,28,26,24,22,20,18,16,14,12,10,8,6,4,2,0},{31,29,27,25,23,21,19,17,1..., dimensions={0} | all-to-all | bytes 589824 | tf_op jit(solution)/shard_map/all_to_all | solution.py:653
  21.6 0.0 copy-done.1
  21.6 2.9 %fit.1 = f32[32,128]{1,0:T(8,128)S(1)} custom-call(f32[576,128]{1,0:T(8,128)S(1)} %bitcast.8, f32[24,128]{1,0:T(8,128)S(1)} %get-tuple-element.18.coef_ref.start_ref, f32[192,128]{1,0:T(8,128)S(1)} %get-tuple-element.24.poly_ref, bf16[1024,256]{1,0:T(8,128)(2,1)S(1)} %get-tuple-element.25.split_ref, f32[4,22,8,128]{3,2,1,0:T(8,128)S(1)} %get-tuple-element.26.ready_ref, ...), custom_call_target="tpu_custom_call" | custom-call | tf_op jit(solution)/shard_map/fit/pallas_call | solution.py:519
  24.5 11.0 %all_to_all.17 = f32[32,1,128]{2,1,0:T(1,128)S(1)} all-to-all(f32[32,1,128]{2,1,0:T(1,128)S(1)} %bitcast.10), channel_id=1, replica_groups=mesh['rows'=8,'fib'=4] {'rows','fib'}, dimensions={0} | all-to-all | bytes 32768 | tf_op jit(solution)/shard_map/all_to_all | solution.py:662
  35.4 0.0 copy-done
  35.4 1.8 %residual.1 = (f32[4,11]{1,0:T(4,128)}, f32[4,11]{1,0:T(4,128)}, bf16[5,128,1024]{2,1,0:T(8,128)(2,1)}) custom-call(f32[32,128]{1,0:T(8,128)S(1)} %bitcast.9, f32[11,128,128]{2,1,0:T(8,128)S(1)} %get-tuple-element.27.local_ref, f32[5,128,1024]{2,1,0:T(8,128)S(1)} %get-tuple-element.28.weight_ref, bf16[5,128,1024]{2,1,0:T(8,128)(2,1)S(1)} %copy-done), custom_call_target="tpu_custom_call" | custom-call | tf_op jit(solution)/shard_map/residual/pallas_call | solution.py:619
  (1 shorter events, 0.0 us)
Async XLA Ops:
  0.6 21.0 %copy-start.1 = (bf16[256,256]{1,0:T(8,128)(2,1)S(1)}, bf16[256,256]{1,0:T(8,128)(2,1)}, u32[]{:S(2)}) copy-start(bf16[256,256]{1,0:T(8,128)(2,1)} %constant.2.clone.map_ref) | copy-start | bytes 393220
  2.6 1.8 %collective-permute-start = (f32[576,128]{1,0:T(8,128)S(1)}, f32[576,128]{1,0:T(8,128)S(1)}, u32[]{:S(2)}, u32[]{:S(2)}) collective-permute-start(f32[576,128]{1,0:T(8,128)S(1)} %get-tuple-element.17), channel_id=1, source_target_pairs={{0,1},{1,0},{2,3},{3,2},{4,5},{5,4},{6,7},{7,6},{8,9},{9,8},{10,11... | collective-permute-start | bytes 884744 | tf_op jit(solution)/shard_map/ppermute | solution.py:646
  4.4 31.1 %copy-start = (bf16[5,128,1024]{2,1,0:T(8,128)(2,1)S(1)}, bf16[5,128,1024]{2,1,0:T(8,128)(2,1)}, u32[]{:S(2)}) copy-start(bf16[5,128,1024]{2,1,0:T(8,128)(2,1)} %frames_ref.1) | copy-start | bytes 3932164
